TPU v7x, 32 devices: a whole 2x2x4 slice. The times are simulated.
32 devices in a mesh: dp: 8 (over y, x, core), tensor: 4 (over z).
Axes of the slice: x: 2, y: 2, z: 4, core: 2. Of those that a mesh axis runs over, the one named last changes fastest.
Arguments:
- hidden_in: bfloat16 [8192, 2048], P(('dp', 'tensor')), may hold values from -6 to 6
- segments: int32 [8, 1024], P('dp'), may hold values from 0 to 3, never falling along the last dimension, each value on 1 to 512 neighbouring positions
- ln_gain: bfloat16 [2048], P('dp'), may hold values from 0.099609375 to 1.8984375
- ln_bias: bfloat16 [2048], P('dp'), may hold values from -3 to 3
- qkv_weight: bfloat16 [2048, 3, 2048], P('dp', None, 'tensor'), may hold values from -1 to 1
- qkv_bias: bfloat16 [3, 2048], P(None, 'tensor'), may hold values from -3 to 3
- dense_weight: bfloat16 [2048, 2048], P('tensor', 'dp'), may hold values from -0.5 to 0.5
- dense_bias: bfloat16 [2048], P('dp'), may hold values from -3 to 3
- fc1_weight: bfloat16 [2048, 8192], P('dp', 'tensor'), may hold values from -0.125 to 0.125
- fc1_bias: bfloat16 [8192], P('tensor'), may hold values from -3 to 3
- fc2_weight: bfloat16 [8192, 2048], P('tensor', 'dp'), may hold values from -0.0625 to 0.0625
- fc2_bias: bfloat16 [2048], P('dp'), may hold values from -3 to 3
- cotangent: bfloat16 [8192, 2048], P(('dp', 'tensor')), may hold values from -6 to 6
Outputs:
- out: bfloat16 [8192, 2048], P(('dp', 'tensor'))
- hidden_grad: bfloat16 [8192, 2048], P(('dp', 'tensor'))
- ln_gain_grad: float32 [2048], P(('dp', 'tensor'))
- ln_bias_grad: float32 [2048], P(('dp', 'tensor'))
- qkv_weight_grad: float32 [2048, 3, 2048], P('dp', None, 'tensor')
- qkv_bias_grad: float32 [3, 2048], P(None, 'tensor')
- dense_weight_grad: float32 [2048, 2048], P('tensor', 'dp')
- dense_bias_grad: float32 [2048], P(('dp', 'tensor'))
- fc1_weight_grad: float32 [2048, 8192], P('dp', 'tensor')
- fc1_bias_grad: float32 [8192], P('tensor')
- fc2_weight_grad: float32 [8192, 2048], P('tensor', 'dp')
- fc2_bias_grad: float32 [2048], P(('dp', 'tensor'))
Inputs may be any that keep to these rules, and one draw needn't show every extreme that they name: `segments`: segment numbers never fall along a sequence; each of the 4 documents of a sequence has 1 to 512 tokens, one exactly 512.
All inputs are finite; a program needn't handle non-finite values.
Results may differ from a plain program's by a relative error of at most 0.011.
Values may be sent and summed in bfloat16 or wider, within the bound.
A program may use at most 192 MiB of HBM per device.

v0:
```python
import jax
import jax.numpy as jnp
from jax import lax
from jax.sharding import PartitionSpec as P

HD = 64
ROT = 32


layer_eps = 1e-05


def positions_of(segments):
    length = segments.shape[-1]
    index_row = jnp.arange(length, dtype=jnp.int32)
    same_doc = segments[:, :, None] == segments[:, None, :]
    before = index_row[None, :] < index_row[:, None]
    return jnp.sum((same_doc & before[None]).astype(jnp.int32), axis=-1)


def rotary_tables(positions):
    frequency = 1.0 / 10000.0 ** (jnp.arange(0, ROT, 2, dtype=jnp.float32) / ROT)
    angles = positions.astype(jnp.float32)[..., None] * frequency
    cosine = jnp.concatenate([jnp.cos(angles), jnp.cos(angles)], -1)[:, :, None, :]
    sine_table = jnp.concatenate([jnp.sin(angles), jnp.sin(angles)], -1)[:, :, None, :]
    return (cosine, sine_table)


def rotate(fields, cosine, sine_table):
    half_rot = ROT // 2
    rotated_part = fields[..., :ROT]
    turned = jnp.concatenate([-rotated_part[..., half_rot:], rotated_part[..., :half_rot]], -1)
    return jnp.concatenate([rotated_part * cosine + turned * sine_table, fields[..., ROT:]], -1)


def rotate_back(gradient, cosine, sine_table):
    half_rot = ROT // 2
    rotated_part = gradient[..., :ROT]
    scaled = rotated_part * sine_table
    turned = jnp.concatenate([scaled[..., half_rot:], -scaled[..., :half_rot]], -1)
    return jnp.concatenate([rotated_part * cosine + turned, gradient[..., ROT:]], -1)


def block_scores(q_block, offset, key_rows, seg_row):
    block_rows = q_block.shape[0]
    length = key_rows.shape[0]
    scaling = q_block.shape[-1] ** (-0.5)
    raw_scores = (
        jnp.einsum("qhd,khd->hqk", q_block, key_rows, preferred_element_type=jnp.float32) * scaling
    )
    row_ids = offset + jnp.arange(block_rows, dtype=jnp.int32)
    col_ids = jnp.arange(length, dtype=jnp.int32)
    seg_q = lax.dynamic_slice_in_dim(seg_row, offset, block_rows)
    allowed = (col_ids[None, :] <= row_ids[:, None]) & (seg_q[:, None] == seg_row[None, :])
    return jnp.where(allowed[None], raw_scores, -1e30)


def row_forward(inputs):
    query_rows, key_rows, value_rows, seg_row = inputs
    length = query_rows.shape[0]
    block_rows = min(512, length)
    num_blocks = length // block_rows
    starts = jnp.arange(num_blocks, dtype=jnp.int32) * block_rows
    q_blocks = query_rows.reshape((num_blocks, block_rows) + query_rows.shape[1:])

    def one_block(inputs_block):
        q_block, offset = inputs_block
        scores = block_scores(q_block, offset, key_rows, seg_row)
        row_max = jnp.max(scores, -1, keepdims=True)
        exponent = jnp.exp(scores - row_max)
        row_sum = jnp.sum(exponent, -1, keepdims=True)
        attn_probs = (exponent / row_sum).astype(jnp.bfloat16)
        result = jnp.einsum(
            "hqk,khd->qhd", attn_probs, value_rows, preferred_element_type=jnp.float32
        )
        return (result, row_max + jnp.log(row_sum))

    outputs, log_sums = lax.map(one_block, (q_blocks, starts))
    return (outputs.reshape(query_rows.shape), log_sums)


def row_backward(inputs):
    query_rows, key_rows, value_rows, grad_rows, log_sums, seg_row = inputs
    length = query_rows.shape[0]
    block_rows = min(512, length)
    num_blocks = length // block_rows
    scaling = query_rows.shape[-1] ** (-0.5)
    starts = jnp.arange(num_blocks, dtype=jnp.int32) * block_rows
    q_blocks = query_rows.reshape((num_blocks, block_rows) + query_rows.shape[1:])
    g_blocks = grad_rows.reshape((num_blocks, block_rows) + grad_rows.shape[1:])

    def one_block(running, inputs_block):
        key_acc, value_acc = running
        q_block, g_block, lse_block, offset = inputs_block
        scores = block_scores(q_block, offset, key_rows, seg_row)
        attn_probs = jnp.exp(scores - lse_block)
        dprobs = jnp.einsum("qhd,khd->hqk", g_block, value_rows, preferred_element_type=jnp.float32)
        inner = jnp.sum(attn_probs * dprobs, -1, keepdims=True)
        grad_scores = (attn_probs * (dprobs - inner)).astype(jnp.bfloat16)
        grad_q = (
            jnp.einsum("hqk,khd->qhd", grad_scores, key_rows, preferred_element_type=jnp.float32)
            * scaling
        )
        key_acc = (
            key_acc
            + jnp.einsum("hqk,qhd->khd", grad_scores, q_block, preferred_element_type=jnp.float32)
            * scaling
        )
        value_acc = value_acc + jnp.einsum(
            "hqk,qhd->khd",
            attn_probs.astype(jnp.bfloat16),
            g_block,
            preferred_element_type=jnp.float32,
        )
        return ((key_acc, value_acc), grad_q)

    zero_acc = jnp.zeros(key_rows.shape, jnp.float32)
    (grad_keys, grad_values), grad_q = lax.scan(
        one_block, (zero_acc, zero_acc), (q_blocks, g_blocks, log_sums, starts)
    )
    return (grad_q.reshape(query_rows.shape), grad_keys, grad_values)


def on_device(
    hidden_in,
    segments,
    ln_gain,
    ln_bias,
    qkv_weight,
    qkv_bias,
    dense_weight,
    dense_bias,
    fc1_weight,
    fc1_bias,
    fc2_weight,
    fc2_bias,
    cotangent,
):
    params = (
        lax.all_gather(ln_gain, "dp", axis=0, tiled=True),
        lax.all_gather(ln_bias, "dp", axis=0, tiled=True),
        lax.all_gather(dense_bias, "dp", axis=0, tiled=True),
        lax.all_gather(fc2_bias, "dp", axis=0, tiled=True),
        lax.all_gather(qkv_weight, "dp", axis=0, tiled=True),
        lax.all_gather(dense_weight, "dp", axis=1, tiled=True),
        lax.all_gather(fc1_weight, "dp", axis=0, tiled=True),
        lax.all_gather(fc2_weight, "dp", axis=1, tiled=True),
    )
    gain_full, beta_full, bias_dense, bias_fc2, w_qkv, w_dense, w_fc1, w_fc2 = params
    num_rows = segments.shape[0]
    length = segments.shape[1]
    width = hidden_in.shape[1]
    local_cols = w_qkv.shape[2]
    local_heads = local_cols // HD
    tokens_group = num_rows * length
    resid_in = hidden_in.astype(jnp.float32)
    average = jnp.mean(resid_in, -1, keepdims=True)
    centred = resid_in - average
    spread = jnp.mean(centred * centred, -1, keepdims=True)
    inv_std = lax.rsqrt(spread + layer_eps)
    unit_rows = centred * inv_std
    normed_local = (
        unit_rows * gain_full.astype(jnp.float32) + beta_full.astype(jnp.float32)
    ).astype(jnp.bfloat16)
    gathered = lax.all_gather(normed_local, "tensor", axis=0, tiled=True)
    cosine, sine_table = rotary_tables(positions_of(segments))
    w_qkv_flat = w_qkv.reshape(width, 3 * local_cols)
    qkv_proj = jnp.dot(gathered, w_qkv_flat, preferred_element_type=jnp.float32) + qkv_bias.reshape(
        -1
    ).astype(jnp.float32)
    qkv_proj = qkv_proj.reshape(num_rows, length, 3, local_heads, HD)
    query_rows = rotate(qkv_proj[:, :, 0], cosine, sine_table).astype(jnp.bfloat16)
    key_rows = rotate(qkv_proj[:, :, 1], cosine, sine_table).astype(jnp.bfloat16)
    value_rows = qkv_proj[:, :, 2].astype(jnp.bfloat16)
    attended, log_sums = lax.map(row_forward, (query_rows, key_rows, value_rows, segments))
    attn_vec = attended.reshape(tokens_group, local_cols).astype(jnp.bfloat16)
    pre_act = jnp.dot(gathered, w_fc1, preferred_element_type=jnp.float32) + fc1_bias.astype(
        jnp.float32
    )
    act_vals, gelu_pull = jax.vjp(
        lambda inner_pre: jax.nn.gelu(inner_pre, approximate=True), pre_act
    )
    act_vals = act_vals.astype(jnp.bfloat16)
    branches = jnp.dot(attn_vec, w_dense, preferred_element_type=jnp.float32) + jnp.dot(
        act_vals, w_fc2, preferred_element_type=jnp.float32
    )
    summed = lax.psum_scatter(branches, "tensor", scatter_dimension=0, tiled=True)
    out = (
        resid_in + summed + bias_dense.astype(jnp.float32) + bias_fc2.astype(jnp.float32)
    ).astype(jnp.bfloat16)
    again = (
        lax.all_gather(ln_gain, "dp", axis=0, tiled=True),
        lax.all_gather(qkv_weight, "dp", axis=0, tiled=True),
        lax.all_gather(dense_weight, "dp", axis=1, tiled=True),
        lax.all_gather(fc1_weight, "dp", axis=0, tiled=True),
        lax.all_gather(fc2_weight, "dp", axis=1, tiled=True),
    )
    gain_back, w_qkv_back, w_dense_back, w_fc1_back, w_fc2_back = again
    grad_out = lax.all_gather(cotangent, "tensor", axis=0, tiled=True)
    cot_float = cotangent.astype(jnp.float32)
    out_bias_part = jnp.sum(cot_float, 0)
    grad_fc2 = jnp.dot(act_vals.T, grad_out, preferred_element_type=jnp.float32)
    grad_dense = jnp.dot(attn_vec.T, grad_out, preferred_element_type=jnp.float32)
    grad_act = jnp.dot(grad_out, w_fc2_back.T, preferred_element_type=jnp.float32)
    grad_pre = gelu_pull(grad_act)[0].astype(jnp.bfloat16)
    fc1_bias_part = jnp.sum(grad_pre.astype(jnp.float32), 0)
    grad_fc1 = jnp.dot(gathered.T, grad_pre, preferred_element_type=jnp.float32)
    grad_normed = jnp.dot(grad_pre, w_fc1_back.T, preferred_element_type=jnp.float32)
    grad_attn = jnp.dot(grad_out, w_dense_back.T, preferred_element_type=jnp.float32).astype(
        jnp.bfloat16
    )
    grad_attn = grad_attn.reshape(num_rows, length, local_heads, HD)
    grad_q, grad_keys, grad_values = lax.map(
        row_backward, (query_rows, key_rows, value_rows, grad_attn, log_sums, segments)
    )
    grad_qkv = jnp.stack(
        [
            rotate_back(grad_q, cosine, sine_table),
            rotate_back(grad_keys, cosine, sine_table),
            grad_values,
        ],
        axis=2,
    )
    grad_qkv = grad_qkv.reshape(tokens_group, 3 * local_cols).astype(jnp.bfloat16)
    qkv_bias_part = jnp.sum(grad_qkv.astype(jnp.float32), 0).reshape(3, local_cols)
    grad_wqkv = jnp.dot(gathered.T, grad_qkv, preferred_element_type=jnp.float32).reshape(
        width, 3, local_cols
    )
    grad_normed = grad_normed + jnp.dot(
        grad_qkv, w_qkv_back.reshape(width, 3 * local_cols).T, preferred_element_type=jnp.float32
    )
    sent_qkv, sent_dense, sent_fc1, sent_fc2 = (
        lax.psum_scatter(grad_wqkv, "dp", scatter_dimension=0, tiled=True),
        lax.psum_scatter(grad_dense, "dp", scatter_dimension=1, tiled=True),
        lax.psum_scatter(grad_fc1, "dp", scatter_dimension=0, tiled=True),
        lax.psum_scatter(grad_fc2, "dp", scatter_dimension=1, tiled=True),
    )
    grad_local = lax.psum_scatter(grad_normed, "tensor", scatter_dimension=0, tiled=True)
    gain_part = jnp.sum(grad_local * unit_rows, 0)
    beta_part = jnp.sum(grad_local, 0)
    scaled_grad = grad_local * gain_back.astype(jnp.float32)
    first_mean = jnp.mean(scaled_grad, -1, keepdims=True)
    second_mean = jnp.mean(scaled_grad * unit_rows, -1, keepdims=True)
    hidden_grad = (
        cot_float + inv_std * (scaled_grad - first_mean - unit_rows * second_mean)
    ).astype(jnp.bfloat16)
    gain_grad, beta_grad, out_bias_grad = (
        lax.psum_scatter(gain_part, ("dp", "tensor"), scatter_dimension=0, tiled=True),
        lax.psum_scatter(beta_part, ("dp", "tensor"), scatter_dimension=0, tiled=True),
        lax.psum_scatter(out_bias_part, ("dp", "tensor"), scatter_dimension=0, tiled=True),
    )
    qkv_bias_grad, fc1_bias_grad = lax.psum((qkv_bias_part, fc1_bias_part), "dp")
    return (
        out,
        hidden_grad,
        gain_grad,
        beta_grad,
        sent_qkv,
        qkv_bias_grad,
        sent_dense,
        out_bias_grad,
        sent_fc1,
        fc1_bias_grad,
        sent_fc2,
        out_bias_grad,
    )


def solution(mesh):
    placed = (
        P(("dp", "tensor"), None),
        P("dp", None),
        P("dp"),
        P("dp"),
        P("dp", None, "tensor"),
        P(None, "tensor"),
        P("tensor", "dp"),
        P("dp"),
        P("dp", "tensor"),
        P("tensor"),
        P("tensor", "dp"),
        P("dp"),
        P(("dp", "tensor"), None),
    )
    return jax.shard_map(
        on_device,
        mesh=mesh,
        in_specs=placed,
        out_specs=(
            P(("dp", "tensor"), None),
            P(("dp", "tensor"), None),
            P(("dp", "tensor")),
            P(("dp", "tensor")),
            P("dp", None, "tensor"),
            P(None, "tensor"),
            P("tensor", "dp"),
            P(("dp", "tensor")),
            P("dp", "tensor"),
            P("tensor"),
            P("tensor", "dp"),
            P(("dp", "tensor")),
        ),
        check_vma=False,
    )
```

profile of v0, /device:TPU:0, one launch (start us, length us, event | category | flops | bytes accessed | tf_op | source)
XLA Modules:
  0.0 1222.7 jit_solution(10483540351876912921)
XLA Ops:
  40.8 82.3 %all-gather.21.cloned.1.call-done = bf16[1024,2048]{1,0:T(8,128)(2,1)} async-done(((bf16[256,2048]{1,0:T(8,128)(2,1)}), bf16[1024,2048]{1,0:T(8,128)(2,1)}) %all-gather.21.cloned.1.call-update) | async-done | bytes 4194320 | tf_op jit(solution)/shard_map/all_gather | solution.py:199
  131.7 72.8 %all-gather.11.cloned.1.call-done = bf16[1024,2048]{1,0:T(8,128)(2,1)} async-done(((bf16[256,2048]{1,0:T(8,128)(2,1)}), bf16[1024,2048]{1,0:T(8,128)(2,1)}) %all-gather.11.cloned.1.call-update) | async-done | bytes 4194320 | tf_op jit(solution)/shard_map/all_gather | solution.py:165
  204.5 47.4 %all-gather.13.cloned.1.call-done = bf16[2048,3,512]{0,2,1:T(8,128)(2,1)} async-done(((bf16[256,3,512]{0,2,1:T(8,128)(2,1)}), bf16[2048,3,512]{0,2,1:T(8,128)(2,1)}) %all-gather.13.cloned.1.call-update) | async-done | bytes 6291472 | tf_op jit(solution)/shard_map/all_gather | solution.py:144
  251.9 11.8 convolution_add_fusion
  280.8 39.5 %while.47 = (s32[]{:T(128)}, bf16[2,512,8,64]{1,3,2,0:T(8,128)(2,1)}, f32[2,8,512,1]{2,1,3,0:T(8,128)}, s32[2]{0:T(128)S(1)}, s32[1024]{0:T(1024)S(1)}, /*index=...) while((s32[]{:T(128)}, ...), condition=%wide.region_6.7_spmd, body=%wide.region_3.6_spmd.sunk | while | flops 1125642752 | bytes 64634080 | solution.py:78
  320.4 146.3 %while.48 = (s32[]{:T(128)}, f32[1024,8,64]{0,2,1:T(8,128)}, f32[1024,8,64]{0,2,1:T(8,128)}, f32[2,512,8,64]{1,0,3,2:T(2,128)}, bf16[2,512,8,64]{1,3,2,0:T(8,128...) while((s32[]{:T(128)}, f32[1024,8,64]{0,2,1:T(8,128)}, ...), condition=%wide.region_10.11_spmd.clone, body=%wide.region_8.10_spmd.clone.sunk | while | flops 2726556160 | bytes 166952784 | solution.py:118
  329.7 11.7 multiply_reduce_fusion.3
  359.1 19.7 %dynamic_update_slice.31 = f32[2,512,8,64]{1,0,3,2:T(2,128)} dynamic-update-slice(f32[2,512,8,64]{1,0,3,2:T(2,128)} %get-tuple-element.508, f32[1,512,8,64]{1,0,3,2:T(1,128)} %copy.78, s32[]{:T(128)} %get-tuple-element.505, s32[]{:T(128)} %constant.89.clone.1..sunk.1, s32[]{:T(128)} %constant.89.clone.1..sunk.1, s32[]{:T(128)} %constant.89.clone.1..sunk.1) | dynamic-update-slice | bytes 2097156 | tf_op jit(solution)/shard_map/while/body/eval_jaxpr/while/body/jit(dynamic_update_index_in_dim)/dynamic_update_slice | solution.py:78
  402.6 11.5 multiply_reduce_fusion.3
  431.6 19.6 %dynamic_update_slice.31 = f32[2,512,8,64]{1,0,3,2:T(2,128)} dynamic-update-slice(f32[2,512,8,64]{1,0,3,2:T(2,128)} %get-tuple-element.508, f32[1,512,8,64]{1,0,3,2:T(1,128)} %copy.78, s32[]{:T(128)} %get-tuple-element.505, s32[]{:T(128)} %constant.89.clone.1..sunk.1, s32[]{:T(128)} %constant.89.clone.1..sunk.1, s32[]{:T(128)} %constant.89.clone.1..sunk.1) | dynamic-update-slice | bytes 2097156 | tf_op jit(solution)/shard_map/while/body/eval_jaxpr/while/body/jit(dynamic_update_index_in_dim)/dynamic_update_slice | solution.py:78
  476.3 14.6 %fusion.70 = f32[1024,2048]{1,0:T(8,128)} fusion(bf16[1024,2048]{1,0:T(8,128)(2,1)} %all-gather.11.cloned.1.call-done, bf16[2048,2048]{1,0:T(8,128)(2,1)} %all-gather.17.cloned.1.call-done), kind=kOutput, calls=%fused_computation.132 | convolution fusion | flops 8589934592 | bytes 20971520 | tf_op jit(solution)/shard_map/dot_general | solution.py:177
  490.9 19.0 %convert_reduce_fusion = (f32[2048]{0:T(1024)S(1)}, bf16[1024,2048]{1,0:T(8,128)(2,1)S(1)}) fusion(f32[1024,2048]{1,0:T(8,128)} %fusion.70, f32[2048]{0:T(1024)S(1)} %copy-done.26, bf16[1024,2048]{1,0:T(8,128)(2,1)} %all-gather.21.cloned.1.call-done, bf16[2048,2048]{1,0:T(8,128)(2,1)} %all-gather.19.cloned.1.call-done), kind=kOutput, calls=%fused_computation.53 | convolution fusion | flops 8638167040 | bytes 25182208 | tf_op jit(solution)/shard_map/dot_general | solution.py:204
  518.8 10.9 convolution_add_fusion.2
  532.4 17.2 %fusion.66 = f32[1024,2048]{1,0:T(8,128)S(1)} fusion(bf16[2048,2048]{1,0:T(8,128)(2,1)} %all-gather.19.cloned.1.call-done, f32[1024,2048]{1,0:T(8,128)} %fusion.70, f32[2048]{0:T(1024)S(1)} %copy-done.26), kind=kOutput, calls=%fused_computation.129 | convolution fusion | flops 8610906112 | bytes 25174016 | tf_op jit(solution)/shard_map/dot_general | solution.py:184
  562.3 11.4 fusion.38
  573.8 15.5 %fusion.73 = f32[2048,2048]{1,0:T(8,128)} fusion(bf16[1024,2048]{1,0:T(8,128)(2,1)} %all-gather.11.cloned.1.call-done, bf16[1024,2048]{1,0:T(8,128)(2,1)} %copy-done.33), kind=kOutput, calls=%fused_computation.135 | convolution fusion | flops 8589934592 | bytes 25165824 | tf_op jit(solution)/shard_map/dot_general | solution.py:207
  589.3 17.5 %fusion.65 = f32[2048,2048]{1,0:T(8,128)} fusion(bf16[1024,2048]{1,0:T(8,128)(2,1)} %all-gather.21.cloned.1.call-done, f32[1024,2048]{1,0:T(8,128)} %fusion.70, f32[2048]{0:T(1024)S(1)} %copy-done.26), kind=kOutput, calls=%fused_computation.128 | convolution fusion | flops 8610906112 | bytes 29368320 | tf_op jit(solution)/shard_map/dot_general | solution.py:202
  625.1 24.5 %all-reduce.4 = (f32[3,512]{1,0:T(4,128)}, f32[2048]{0:T(1024)}) all-reduce(f32[3,512]{1,0:T(4,128)S(1)} %reshape.577, f32[2048]{0:T(1024)S(1)} %get-tuple-element.297), channel_id=1, replica_groups=mesh['dp'=8,'tensor'=4] {'dp'}, use_global_device_ids=true, to_apply=%region_20.21 | all-reduce | flops 3584 | bytes 28672 | tf_op jit(solution)/shard_map/psum | solution.py:252
  649.6 25.6 %reduce-scatter.9.cloned.1.call-done = f32[256,2048]{1,0:T(8,128)} async-done(((f32[1024,2048]{1,0:T(8,128)}), f32[256,2048]{1,0:T(8,128)}) %reduce-scatter.9.cloned.1.call-update) | async-done | bytes 2097168 | tf_op jit(solution)/shard_map/reduce_scatter | solution.py:238
  678.0 144.9 %reduce-scatter.7.cloned.1.call-done = f32[256,2048]{1,0:T(8,128)} async-done(((f32[1024,2048]{1,0:T(8,128)}), f32[256,2048]{1,0:T(8,128)}) %reduce-scatter.7.cloned.1.call-update) | async-done | bytes 2097168 | tf_op jit(solution)/shard_map/reduce_scatter | solution.py:187
  827.7 41.0 %all-reduce.3 = (f32[2048]{0:T(1024)S(1)}, f32[2048]{0:T(1024)S(1)}, f32[2048]{0:T(1024)S(1)}) all-reduce(f32[2048]{0:T(1024)S(1)} %get-tuple-element.250, f32[2048]{0:T(1024)S(1)} %get-tuple-element.253, f32[2048]{0:T(1024)S(1)} %get-tuple-element.315), channel_id=4, replica_groups=mesh['dp'=8,'tensor'=4] {'dp','tensor'}, use_global_device_ids=true, to_apply=%region_15.16.clone | all-reduce | flops 6144 | bytes 49152
  878.8 96.0 %reduce-scatter.11.cloned.1.call-done = f32[256,3,512]{2,0,1:T(8,128)} async-done(((f32[2048,3,512]{2,0,1:T(8,128)}), f32[256,3,512]{2,0,1:T(8,128)}) %reduce-scatter.11.cloned.1.call-update) | async-done | bytes 1572880 | tf_op jit(solution)/shard_map/reduce_scatter | solution.py:233
  974.8 120.4 %reduce-scatter.15.cloned.1.call-done = f32[256,2048]{1,0:T(8,128)} async-done(((f32[2048,2048]{1,0:T(8,128)}), f32[256,2048]{1,0:T(8,128)}) %reduce-scatter.15.cloned.1.call-update) | async-done | bytes 2097168 | tf_op jit(solution)/shard_map/reduce_scatter | solution.py:235
  1095.1 120.0 %reduce-scatter.17.cloned.1.call-done = f32[2048,256]{1,0:T(8,128)} async-done(((f32[2048,2048]{1,0:T(8,128)}), f32[2048,256]{1,0:T(8,128)}) %reduce-scatter.17.cloned.1.call-update) | async-done | bytes 2097168 | tf_op jit(solution)/shard_map/reduce_scatter | solution.py:236
  (214 shorter events, 243.8 us)
Async XLA Ops:
  7.2 25.5 %copy-start.4 = (bf16[256,2048]{1,0:T(8,128)(2,1)S(1)}, bf16[256,2048]{1,0:T(8,128)(2,1)}, u32[]{:S(2)}) copy-start(bf16[256,2048]{1,0:T(8,128)(2,1)} %param.17) | copy-start | bytes 3145732
  7.2 27.0 %copy-start.17 = (bf16[256,3,512]{2,0,1:T(8,128)(2,1)S(1)}, bf16[256,3,512]{2,0,1:T(8,128)(2,1)}, u32[]{:S(2)}) copy-start(bf16[256,3,512]{2,0,1:T(8,128)(2,1)} %param.21) | copy-start | bytes 2359300
  7.2 33.6 %all-gather.15.cloned.1.call-start = ((), (), s32[]{:S(2)}) async-start(), calls=%async_computation.8 | async-start | bytes 2359296 | tf_op jit(solution)/shard_map/all_gather | solution.py:145
  7.9 115.2 %all-gather.21.cloned.1.call-start = ((), (), s32[]{:S(2)}) async-start(), calls=%async_computation.12 | async-start | bytes 5242880 | tf_op jit(solution)/shard_map/all_gather | solution.py:199
  8.7 195.8 %all-gather.11.cloned.1.call-start = ((), (), s32[]{:S(2)}) async-start(), calls=%async_computation.6 | async-start | bytes 5242880 | tf_op jit(solution)/shard_map/all_gather | solution.py:165
  32.7 90.4 %copy-start.24 = (f32[256]{0:T(256)}, f32[256]{0:T(256)S(1)}, u32[]{:S(2)}) copy-start(f32[256]{0:T(256)S(1)} %add_rsqrt_fusion) | copy-start | bytes 3076
  34.2 217.8 %all-gather.13.cloned.1.call-start = ((), (), s32[]{:S(2)}) async-start(), calls=%async_computation.7 | async-start | bytes 7077888 | tf_op jit(solution)/shard_map/all_gather | solution.py:144
  35.4 441.0 %all-gather.17.cloned.1.call-start = ((), (), s32[]{:S(2)}) async-start(), calls=%async_computation.9 | async-start | bytes 9437184 | tf_op jit(solution)/shard_map/all_gather | solution.py:146
  36.0 454.9 %all-gather.19.cloned.1.call-start = ((), (), s32[]{:S(2)}) async-start(), calls=%async_computation.10 | async-start | bytes 9437184 | tf_op jit(solution)/shard_map/all_gather | solution.py:147
  36.6 638.7 %reduce-scatter.9.cloned.1.call-start = ((), (), s32[]{:S(2)}) async-start(), calls=%async_computation.13 | async-start | bytes 10485760 | tf_op jit(solution)/shard_map/reduce_scatter | solution.py:238
  38.2 237.6 %copy-start.10 = (f32[1024,32]{0,1:T(8,128)}, f32[1024,32]{0,1:T(8,128)S(1)}, u32[]{:S(2)}) copy-start(f32[1024,32]{0,1:T(8,128)S(1)} %get-tuple-element.332) | copy-start | bytes 393220
  38.2 237.6 %copy-start.12 = (f32[1024,32]{0,1:T(8,128)}, f32[1024,32]{0,1:T(8,128)S(1)}, u32[]{:S(2)}) copy-start(f32[1024,32]{0,1:T(8,128)S(1)} %get-tuple-element.333) | copy-start | bytes 393220
  357.1 21.7 %copy-start = (f32[1024,8,64]{0,2,1:T(8,128)S(1)}, f32[1024,8,64]{0,2,1:T(8,128)}, u32[]{:S(2)}) copy-start(f32[1024,8,64]{0,2,1:T(8,128)} %get-tuple-element.506) | copy-start | bytes 6291460 | tf_op jit(solution)/shard_map/while/body/eval_jaxpr/while
  529.8 293.1 %reduce-scatter.7.cloned.1.call-start = ((), (), s32[]{:S(2)}) async-start(), calls=%async_computation.11 | async-start | bytes 10485760 | tf_op jit(solution)/shard_map/reduce_scatter | solution.py:187
  555.3 323.5 %reduce-scatter.13.cloned.1.call-start = ((), (), s32[]{:S(2)}) async-start(), calls=%async_computation.15 | async-start | bytes 4718592 | tf_op jit(solution)/shard_map/reduce_scatter | solution.py:234
  562.2 412.5 %reduce-scatter.11.cloned.1.call-start = ((), (), s32[]{:S(2)}) async-start(), calls=%async_computation.14 | async-start | bytes 14155776 | tf_op jit(solution)/shard_map/reduce_scatter | solution.py:233
  573.7 521.4 %reduce-scatter.15.cloned.1.call-start = ((), (), s32[]{:S(2)}) async-start(), calls=%async_computation.16 | async-start | bytes 18874368 | tf_op jit(solution)/shard_map/reduce_scatter | solution.py:235
  589.2 625.9 %reduce-scatter.17.cloned.1.call-start = ((), (), s32[]{:S(2)}) async-start(), calls=%async_computation.17 | async-start | bytes 18874368 | tf_op jit(solution)/shard_map/reduce_scatter | solution.py:236
  606.8 68.5 %copy-start.5 = (bf16[256,2048]{1,0:T(8,128)(2,1)S(1)}, bf16[256,2048]{1,0:T(8,128)(2,1)}, u32[]{:S(2)}) copy-start(bf16[256,2048]{1,0:T(8,128)(2,1)} %param.17) | copy-start | bytes 3145732
  606.8 68.5 %copy-start.20 = (f32[8,1,256]{2,1,0:T(1,128)S(1)}, f32[8,1,256]{2,1,0:T(1,128)}, u32[]{:S(2)}) copy-start(f32[8,1,256]{2,1,0:T(1,128)} %copy-done.19) | copy-start | bytes 24580
  606.8 68.5 %copy-start.23 = (f32[256]{0:T(256)S(1)}, f32[256]{0:T(256)}, u32[]{:S(2)}) copy-start(f32[256]{0:T(256)} %copy-done.22) | copy-start | bytes 3076
  606.8 68.4 %copy-start.25 = (f32[256]{0:T(256)S(1)}, f32[256]{0:T(256)}, u32[]{:S(2)}) copy-start(f32[256]{0:T(256)} %copy-done.24) | copy-start | bytes 3076
  675.3 147.6 %copy-start.7 = (f32[256,2048]{1,0:T(8,128)S(1)}, f32[256,2048]{1,0:T(8,128)}, u32[]{:S(2)}) copy-start(f32[256,2048]{1,0:T(8,128)} %reduce-scatter.9.cloned.1.call-done) | copy-start | bytes 6291460
  868.8 346.9 %copy-start.32 = (f32[64]{0:T(128)}, f32[64]{0:T(128)S(1)}, u32[]{:S(2)}) copy-start(f32[64]{0:T(128)S(1)} %dynamic-slice.3) | copy-start | bytes 772
  (28 other events, 229.1 us)
Sparse Core Ops, SparseCore 0:
  9.9 30.8 all-gather.14
  42.3 80.7 all-gather.20
  125.2 79.2 all-gather.10
  206.8 45.0 all-gather.12
  253.6 54.2 all-gather.16
  309.7 55.8 all-gather.18
  529.9 145.3 reduce-scatter.8
  677.6 145.2 reduce-scatter.6
  826.8 51.8 reduce-scatter.12
  882.7 92.0 reduce-scatter.10
  978.9 116.1 reduce-scatter.14
  1099.1 115.9 reduce-scatter.16
where the time goes:
time: 1240 us; the launch traced here: 1220 us
  waiting for transfers between devices  723 us (58%)
  matrix products  238 us (19%)
  blocking collectives  102 us (8%)
  local copies, waits for them, and re-layouts  79 us (6%)
  other arithmetic  56.2 us (5%)
  between operations  15 us (1%)
    reduce_scatter x1, waiting for transfers between devices, on_device(): lax.psum_scatter(branches, 'tensor', scatter_dimension=0, tiled=True)  145 us
    reduce_scatter x1, waiting for transfers between devices, on_device(): lax.psum_scatter(grad_fc1, 'dp', scatter_dimension=0, tiled=True)  120 us
    reduce_scatter x1, waiting for transfers between devices, on_device(): lax.psum_scatter(grad_fc2, 'dp', scatter_dimension=1, tiled=True)  120 us
    reduce_scatter x1, waiting for transfers between devices, on_device(): lax.psum_scatter(grad_wqkv, 'dp', scatter_dimension=0, tiled=True)  96 us
    all_gather x1, waiting for transfers between devices, on_device(): grad_out = lax.all_gather(cotangent, 'tensor', axis=0, tiled=True)  82.3 us
    all_gather x1, waiting for transfers between devices, on_device(): gathered = lax.all_gather(normed_local, 'tensor', axis=0, tiled=True)  72.8 us
    all_gather x1, waiting for transfers between devices, on_device(): lax.all_gather(qkv_weight, 'dp', axis=0, tiled=True)  47.4 us
    dynamic_update_slice x4, local copies, waits for them, and re-layouts, row_forward(): outputs, log_sums = lax.map(one_block, (q_blocks, starts))  43.4 us
  transfers between devices with their start and end apart: 12, of which 10 were waited for; matrix products, arithmetic and copies ran while one was open for 27% of the time, Pallas kernels for 0%

commit v1 on v0

v1 whole, which is shorter than its diff:
```python
import functools

import jax
import jax.numpy as jnp
from jax import lax
from jax.experimental import pallas as pl
from jax.experimental.pallas import tpu as pltpu
from jax.sharding import PartitionSpec as P

HD = 64
ROT = 32
BLOCK = 256
MAX_DOC = 512
VMEM_LIMIT = 66_000_000
MESH = pl.DeviceIdType.MESH
ANY = pl.BlockSpec(memory_space=pl.ANY)
VMEM = pl.BlockSpec(memory_space=pltpu.VMEM)

layer_eps = 1e-05
f32 = jnp.float32
bf16 = jnp.bfloat16


def dot_nn(a, b):
    return lax.dot_general(a, b, (((1,), (0,)), ((), ())), preferred_element_type=f32)


def dot_nt(a, b):
    return lax.dot_general(a, b, (((1,), (1,)), ((), ())), preferred_element_type=f32)


def dot_tn(a, b):
    return lax.dot_general(a, b, (((0,), (0,)), ((), ())), preferred_element_type=f32)


def flip(index, bit):
    step = 1 << bit
    return index + step * (1 - 2 * (lax.div(index, step) % 2))


def relative(index, offset):
    bit = 0
    while offset >> bit:
        if (offset >> bit) & 1:
            index = flip(index, bit)
        bit += 1
    return index


def stages_of(order):
    held, stages = [0], []
    for bit in order:
        got = [r ^ (1 << bit) for r in held]
        stages.append((bit, list(held), got))
        held = held + got
    return stages


class Sems:
    def __init__(self):
        self.count = 0

    def take(self):
        self.count += 1
        return self.count - 1


class CubeGather:
    def __init__(self, sems, orders):
        self.plans = [stages_of(order) for order in orders]
        self.ids = {
            (h, j, i): sems.take()
            for h, stages in enumerate(self.plans)
            for j, (_, held, _) in enumerate(stages)
            for i in range(len(held))
        }

    def bind(self, me, other, own, window, send_sem, recv_sem):
        self.me, self.other, self.own, self.window = me, other, own, window
        self.send_sem, self.recv_sem = send_sem, recv_sem
        return self

    def copy(self, h, j, i):
        bit, held, _ = self.plans[h][j]
        slot = relative(self.me, held[i])
        target = self.window(slot, h)
        source = self.own(h) if held[i] == 0 else target
        k = self.ids[h, j, i]
        return pltpu.make_async_remote_copy(
            src_ref=source,
            dst_ref=target,
            send_sem=self.send_sem.at[k],
            recv_sem=self.recv_sem.at[k],
            device_id=(flip(self.me, bit), self.other),
            device_id_type=MESH,
        )

    def start(self):
        depth = len(self.plans[0])
        for j in range(depth):
            for h in range(len(self.plans)):
                self.copy(h, j, 0).start()

    def advance(self, j):
        for i in range(len(self.plans[0][j][1])):
            for h, stages in enumerate(self.plans):
                self.copy(h, j, i).wait_recv()
                slot = stages[j][2][i]
                for later in range(j + 1, len(stages)):
                    self.copy(h, later, stages[later][1].index(slot)).start()

    def finish(self):
        for h, j, i in self.ids:
            self.copy(h, j, i).wait_send()


class LineGather:
    def __init__(self, sems, size, subs):
        self.size, self.subs = size, subs
        self.ids = {
            (way, s, u): sems.take()
            for way in (0, 1)
            for s in range(size - 1)
            for u in range(subs)
        }

    def bind(self, me, other, own, window, send_sem, recv_sem):
        self.me, self.other, self.own, self.window = me, other, own, window
        self.send_sem, self.recv_sem = send_sem, recv_sem
        return self

    def copy(self, way, s, u):
        block = self.me - s if way == 0 else self.me + s
        target = self.window(block, u)
        k = self.ids[way, s, u]
        return pltpu.make_async_remote_copy(
            src_ref=self.own(u) if s == 0 else target,
            dst_ref=target,
            send_sem=self.send_sem.at[k],
            recv_sem=self.recv_sem.at[k],
            device_id=(self.other, self.me + 1 if way == 0 else self.me - 1),
            device_id_type=MESH,
        )

    def sends(self, way, s):
        if way == 0:
            return (self.me >= s) & (self.me < self.size - 1)
        return (self.me + s < self.size) & (self.me > 0)

    def gets(self, way, s):
        if way == 0:
            return self.me - 1 - s >= 0
        return self.me + 1 + s < self.size

    def start(self, u):
        for way in (0, 1):

            @pl.when(self.sends(way, 0))
            def _():
                self.copy(way, 0, u).start()

    def advance(self, s, u):
        for way in (0, 1):

            @pl.when(self.gets(way, s))
            def _():
                self.copy(way, s, u).wait_recv()

            if s + 1 < self.size - 1:

                @pl.when(self.sends(way, s + 1))
                def _():
                    self.copy(way, s + 1, u).start()

    def finish(self):
        for way, s, u in self.ids:

            @pl.when(self.sends(way, s))
            def _():
                self.copy(way, s, u).wait_send()


def greet(dp, me, tensor, line):
    barrier = pltpu.get_barrier_semaphore()
    bits = dp.bit_length() - 1
    for bit in range(bits):
        pl.semaphore_signal(barrier, inc=1, device_id=(flip(me, bit), line), device_id_type=MESH)

    @pl.when(line > 0)
    def _():
        pl.semaphore_signal(barrier, inc=1, device_id=(me, line - 1), device_id_type=MESH)

    @pl.when(line < tensor - 1)
    def _():
        pl.semaphore_signal(barrier, inc=1, device_id=(me, line + 1), device_id_type=MESH)

    left, right = jnp.minimum(line, 1), jnp.minimum(tensor - 1 - line, 1)
    pl.semaphore_wait(barrier, bits + left + right)


def orders_of(dp):
    bits = list(range(1, dp.bit_length() - 1))
    return [bits + [0], bits[::-1] + [0]]


def gather_call(dp, tensor, hidden, cotangent, w_qkv, w_dense, w_fc1, w_fc2, vectors):
    rows, width = hidden.shape
    local = w_qkv.shape[2]
    hidden_units = w_fc1.shape[1]
    part = width // dp
    sems = Sems()
    orders = orders_of(dp)
    plan_vec = CubeGather(sems, orders[:1])
    plan_qkv, plan_dense, plan_fc1, plan_fc2 = (CubeGather(sems, orders) for _ in range(4))
    plan_n, plan_c = LineGather(sems, tensor, 2), LineGather(sems, tensor, 2)

    def kernel(
        x_ref, c_ref, wq_ref, wd_ref, w1_ref, w2_ref, vec_ref,
        gq_ref, gd_ref, g1_ref, g2_ref, gn_ref, gc_ref, gvec_ref,
        x_buf, n_buf, vec_buf, send_sem, recv_sem, local_sem,
    ):
        me, line = lax.axis_index("dp"), lax.axis_index("tensor")
        half = part // 2

        def cols(a):
            return pl.ds(pl.multiple_of(a * part, part), part)

        def half_rows(a, h):
            return pl.ds(pl.multiple_of(a * part + h * half, half), half)

        def tok(b, u):
            return pl.ds(pl.multiple_of(b * rows + u * (rows // 2), rows // 2), rows // 2)

        def sub(u):
            return pl.ds(u * (rows // 2), rows // 2)

        def piece(n, h):
            return pl.ds(h * (n // 2), n // 2)

        pair = (send_sem, recv_sem)
        vec = plan_vec.bind(me, line, lambda h: vec_ref, lambda a, h: vec_buf.at[:, cols(a)], *pair)
        qkv = plan_qkv.bind(
            me, line,
            lambda h: wq_ref.at[:, pl.ds(h * half, half), :],
            lambda a, h: gq_ref.at[:, half_rows(a, h), :], *pair)
        fc1 = plan_fc1.bind(
            me, line,
            lambda h: w1_ref.at[pl.ds(h * half, half), :],
            lambda a, h: g1_ref.at[half_rows(a, h), :], *pair)
        dense = plan_dense.bind(
            me, line,
            lambda h: wd_ref.at[piece(local, h), :],
            lambda a, h: gd_ref.at[piece(local, h), cols(a)], *pair)
        fc2 = plan_fc2.bind(
            me, line,
            lambda h: w2_ref.at[piece(hidden_units, h), :],
            lambda a, h: g2_ref.at[piece(hidden_units, h), cols(a)], *pair)
        norm = plan_n.bind(
            line, me, lambda u: n_buf.at[sub(u)], lambda b, u: gn_ref.at[tok(b, u)], *pair)
        cot = plan_c.bind(
            line, me, lambda u: c_ref.at[sub(u)], lambda b, u: gc_ref.at[tok(b, u)], *pair)

        keep = [
            (x_ref, x_buf),
            (vec_ref, vec_buf.at[:, cols(me)]),
            (wq_ref, gq_ref.at[:, pl.ds(pl.multiple_of(me * part, part), part), :]),
            (w1_ref, g1_ref.at[pl.ds(pl.multiple_of(me * part, part), part), :]),
            (wd_ref, gd_ref.at[:, cols(me)]),
            (w2_ref, g2_ref.at[:, cols(me)]),
            (c_ref, gc_ref.at[pl.ds(pl.multiple_of(line * rows, rows), rows), :]),
        ]
        keeps = [
            pltpu.make_async_copy(a, b, local_sem.at[k]) for k, (a, b) in enumerate(keep)
        ]
        keeps[0].start()
        greet(dp, me, tensor, line)
        vec.start()
        qkv.start()
        for copy in keeps[1:]:
            copy.start()
        stages = dp.bit_length() - 1
        for j in range(stages):
            vec.advance(j)
        keeps[0].wait()
        keeps[1].wait()

        @pl.loop(0, rows, step=32)
        def _(r):
            x = x_buf[pl.ds(r, 32), :].astype(f32)
            centred = x - jnp.mean(x, -1, keepdims=True)
            spread = jnp.mean(centred * centred, -1, keepdims=True)
            unit = centred * lax.rsqrt(spread + layer_eps)
            n_buf[pl.ds(r, 32), :] = (unit * vec_buf[0:1, :] + vec_buf[1:2, :]).astype(bf16)

        norm.start(0)
        norm.start(1)
        own_n = pltpu.make_async_copy(
            n_buf, gn_ref.at[pl.ds(pl.multiple_of(line * rows, rows), rows), :], local_sem.at[len(keep)])
        own_n.start()
        gvec_ref[...] = vec_buf[...]
        qkv.advance(0)
        fc1.start()
        norm.advance(0, 0)
        for j in range(1, stages - 1):
            qkv.advance(j)
        norm.advance(0, 1)
        fc1.advance(0)
        dense.start()
        fc2.start()
        qkv.advance(stages - 1)
        norm.advance(1, 0)
        norm.advance(1, 1)
        cot.start(0)
        cot.start(1)
        for j in range(1, stages - 1):
            fc1.advance(j)
        dense.advance(0)
        norm.advance(2, 0)
        norm.advance(2, 1)
        fc1.advance(stages - 1)
        fc2.advance(0)
        cot.advance(0, 0)
        for j in range(1, stages - 1):
            dense.advance(j)
        cot.advance(0, 1)
        for j in range(1, stages - 1):
            fc2.advance(j)
        dense.advance(stages - 1)
        fc2.advance(stages - 1)
        for s in (1, 2):
            for u in (0, 1):
                cot.advance(s, u)
        for copy in keeps[2:]:
            copy.wait()
        own_n.wait()
        for plan in (vec, qkv, fc1, dense, fc2, norm, cot):
            plan.finish()

    tokens = rows * tensor
    return pl.pallas_call(
        kernel,
        out_shape=(
            jax.ShapeDtypeStruct((3, width, local), bf16),
            jax.ShapeDtypeStruct((local, width), bf16),
            jax.ShapeDtypeStruct((width, hidden_units), bf16),
            jax.ShapeDtypeStruct((hidden_units, width), bf16),
            jax.ShapeDtypeStruct((tokens, width), bf16),
            jax.ShapeDtypeStruct((tokens, width), bf16),
            jax.ShapeDtypeStruct((8, width), f32),
        ),
        in_specs=[ANY] * 7,
        out_specs=(ANY,) * 6 + (VMEM,),
        scratch_shapes=[
            pltpu.VMEM((rows, width), bf16),
            pltpu.VMEM((rows, width), bf16),
            pltpu.VMEM((8, width), f32),
            pltpu.SemaphoreType.DMA((sems.count,)),
            pltpu.SemaphoreType.DMA((sems.count,)),
            pltpu.SemaphoreType.DMA((8,)),
        ],
        compiler_params=pltpu.CompilerParams(
            collective_id=0, has_side_effects=True, vmem_limit_bytes=VMEM_LIMIT
        ),
        name="gather",
    )(hidden, cotangent, w_qkv, w_dense, w_fc1, w_fc2, vectors)


def normalize(x, gain, bias):
    centred = x - jnp.mean(x, -1, keepdims=True)
    spread = jnp.mean(centred * centred, -1, keepdims=True)
    unit = centred * lax.rsqrt(spread + layer_eps)
    return (unit * gain + bias).astype(bf16)


def gather_plain(hidden, cotangent, w_qkv, w_dense, w_fc1, w_fc2, vectors):
    vec = lax.all_gather(vectors, "dp", axis=1, tiled=True)
    normed = normalize(hidden.astype(f32), vec[0:1], vec[1:2])
    return (
        lax.all_gather(w_qkv, "dp", axis=1, tiled=True),
        lax.all_gather(w_dense, "dp", axis=1, tiled=True),
        lax.all_gather(w_fc1, "dp", axis=0, tiled=True),
        lax.all_gather(w_fc2, "dp", axis=1, tiled=True),
        lax.all_gather(normed, "tensor", axis=0, tiled=True),
        lax.all_gather(cotangent, "tensor", axis=0, tiled=True),
        vec,
    )


def spans_of(length):
    back = -(-(MAX_DOC - 1) // BLOCK)
    spans, at = [], 0
    for i in range(length // BLOCK):
        low = max(0, i - back) * BLOCK
        spans.append((low, (i + 1) * BLOCK, at))
        at += (i + 1) * BLOCK - low
    return spans, at


def turn(x, cosine, sine_lo, sine_hi):
    return x * cosine + pltpu.roll(x, 128 - ROT // 2, 1) * sine_lo + pltpu.roll(x, ROT // 2, 1) * sine_hi


def head_lanes(shape, e):
    lane = lax.broadcasted_iota(jnp.int32, shape, 1)
    return (lane >= e * HD) & (lane < (e + 1) * HD)


def only(x, e):
    return jnp.where(head_lanes(x.shape, e), x, jnp.zeros_like(x))


def attend_kernel(
    q_ref, k_ref, v_ref, bias_ref, cos_ref, slo_ref, shi_ref, segc_ref, segr_ref,
    qs_ref, ks_ref, vs_ref, o_ref, p_ref, mask_ref,
):
    length = q_ref.shape[0]
    spans, _ = spans_of(length)

    @pl.when(pl.program_id(1) == 0)
    def _():
        for i, (low, high, at) in enumerate(spans):
            keys = lax.broadcasted_iota(jnp.int32, (high - low, BLOCK), 0) + low
            queries = lax.broadcasted_iota(jnp.int32, (high - low, BLOCK), 1) + i * BLOCK
            same = segc_ref[low:high, :] == segr_ref[:, i * BLOCK : (i + 1) * BLOCK]
            mask_ref[at : at + high - low, :] = jnp.where((keys <= queries) & same, 0.0, -1e30)

    cosine, slo, shi = cos_ref[...], slo_ref[...], shi_ref[...]
    query = turn(q_ref[...] + bias_ref[0:1, :], cosine, slo, shi).astype(bf16) * bf16(HD**-0.5)
    key = turn(k_ref[...] + bias_ref[1:2, :], cosine, slo, shi).astype(bf16)
    value = (v_ref[...] + bias_ref[2:3, :]).astype(bf16)
    qs_ref[...] = query
    ks_ref[...] = key
    vs_ref[...] = value
    heads = 128 // HD
    for i, (low, high, at) in enumerate(spans):
        q_i = query[i * BLOCK : (i + 1) * BLOCK]
        total = jnp.zeros((BLOCK, 128), f32)
        for e in range(heads):
            scores = dot_nt(only(key[low:high], e), q_i) + mask_ref[at : at + high - low, :]
            exponent = jnp.exp(scores - jnp.max(scores, 0, keepdims=True))
            inverse = 1.0 / jnp.sum(exponent, 0, keepdims=True)
            probs = (exponent * inverse).astype(bf16)
            p_ref[e, at : at + high - low, :] = probs
            total = total + dot_tn(probs, only(value[low:high], e))
        o_ref[i * BLOCK : (i + 1) * BLOCK, :] = total.astype(bf16)


def attend(q, k, v, qkv_bias, tables, segments, rows):
    tokens, local = q.shape
    length = tokens // rows
    pairs = local // 128
    _, stored = spans_of(length)
    block = pl.BlockSpec((length, 128), lambda r, h: (r, h))
    table = pl.BlockSpec((length, 128), lambda r, h: (r, 0))
    shape = jax.ShapeDtypeStruct((tokens, local), bf16)
    return pl.pallas_call(
        attend_kernel,
        grid=(rows, pairs),
        out_shape=(shape,) * 4 + (jax.ShapeDtypeStruct((rows, local // HD, stored, BLOCK), bf16),),
        in_specs=[block] * 3
        + [pl.BlockSpec((8, 128), lambda r, h: (0, h))]
        + [table] * 3
        + [
            pl.BlockSpec((length, 1), lambda r, h: (r, 0)),
            pl.BlockSpec((pl.Squeezed(), 1, length), lambda r, h: (r, 0, 0)),
        ],
        out_specs=(block,) * 4
        + (pl.BlockSpec((pl.Squeezed(), 128 // HD, stored, BLOCK), lambda r, h: (r, h, 0, 0)),),
        scratch_shapes=[pltpu.VMEM((stored, BLOCK), f32)],
        compiler_params=pltpu.CompilerParams(vmem_limit_bytes=VMEM_LIMIT),
        cost_estimate=pl.CostEstimate(
            flops=16 * tokens * 768 * local, bytes_accessed=24 << 20, transcendentals=0
        ),
        name="attend",
    )(q, k, v, qkv_bias, *tables, segments.reshape(tokens, 1), segments.reshape(rows, 1, length))


def attend_back_kernel(
    q_ref, k_ref, v_ref, g_ref, o_ref, p_ref, cos_ref, slo_ref, shi_ref,
    dq_ref, dk_ref, dv_ref, bias_ref, kacc_ref, vacc_ref,
):
    length = q_ref.shape[0]
    spans, _ = spans_of(length)
    heads = 128 // HD
    grad = g_ref[...]
    inner = grad.astype(f32) * o_ref[...].astype(f32)
    lane = lax.broadcasted_iota(jnp.int32, (8, 128), 1)
    row = lax.broadcasted_iota(jnp.int32, (8, 128), 0)
    pick = jnp.where(lax.div(lane, HD) == row, 1.0, 0.0)
    delta = lax.dot_general(
        pick, inner, (((1,), (1,)), ((), ())),
        precision=lax.Precision.HIGHEST, preferred_element_type=f32)
    query, key, value = q_ref[...], k_ref[...], v_ref[...]
    kacc_ref[...] = jnp.zeros_like(kacc_ref)
    vacc_ref[...] = jnp.zeros_like(vacc_ref)
    cosine, slo, shi = cos_ref[...], slo_ref[...], shi_ref[...]
    first = jnp.zeros((1, 128), f32)
    for i, (low, high, at) in enumerate(spans):
        mine = slice(i * BLOCK, (i + 1) * BLOCK)
        g_i, q_i = grad[mine], query[mine]
        dq = jnp.zeros((BLOCK, 128), f32)
        ps, dss = [], []
        for e in range(heads):
            probs = p_ref[e, at : at + high - low, :]
            dprobs = dot_nt(only(value[low:high], e), g_i)
            ds = (probs.astype(f32) * (dprobs - delta[e : e + 1, mine])).astype(bf16)
            dq = dq + dot_tn(ds, only(key[low:high], e))
            ps.append(probs)
            dss.append(ds)
        g_cat = jnp.concatenate([only(g_i, e) for e in range(heads)], 0)
        q_cat = jnp.concatenate([only(q_i, e) for e in range(heads)], 0)
        vacc_ref[low:high, :] += dot_nn(jnp.concatenate(ps, 1), g_cat)
        kacc_ref[low:high, :] += dot_nn(jnp.concatenate(dss, 1), q_cat)
        dq = dq * f32(HD**-0.5)
        dq = turn(dq, cosine[mine], -slo[mine], -shi[mine]).astype(bf16)
        dq_ref[mine, :] = dq
        first = first + jnp.sum(dq.astype(f32), 0, keepdims=True)
    dk = turn(kacc_ref[...], cosine, -slo, -shi).astype(bf16)
    dv = vacc_ref[...].astype(bf16)
    dk_ref[...] = dk
    dv_ref[...] = dv
    sums = [first, jnp.sum(dk.astype(f32), 0, keepdims=True), jnp.sum(dv.astype(f32), 0, keepdims=True)]
    sums = jnp.concatenate(sums + [jnp.zeros((5, 128), f32)], 0)

    @pl.when(pl.program_id(1) == 0)
    def _():
        bias_ref[...] = sums

    @pl.when(pl.program_id(1) > 0)
    def _():
        bias_ref[...] += sums


def attend_back(q, k, v, g, o, probs, tables, rows):
    tokens, local = q.shape
    length = tokens // rows
    pairs = local // 128
    stored = probs.shape[2]
    block = pl.BlockSpec((length, 128), lambda h, r: (r, h))
    table = pl.BlockSpec((length, 128), lambda h, r: (r, 0))
    shape = jax.ShapeDtypeStruct((tokens, local), bf16)
    return pl.pallas_call(
        attend_back_kernel,
        grid=(pairs, rows),
        out_shape=(shape,) * 3 + (jax.ShapeDtypeStruct((8, local), f32),),
        in_specs=[block] * 5
        + [pl.BlockSpec((pl.Squeezed(), 128 // HD, stored, BLOCK), lambda h, r: (r, h, 0, 0))]
        + [table] * 3,
        out_specs=(block,) * 3 + (pl.BlockSpec((8, 128), lambda h, r: (0, h)),),
        scratch_shapes=[pltpu.VMEM((length, 128), f32)] * 2,
        compiler_params=pltpu.CompilerParams(vmem_limit_bytes=VMEM_LIMIT),
        cost_estimate=pl.CostEstimate(
            flops=32 * tokens * 768 * local, bytes_accessed=24 << 20, transcendentals=0
        ),
        name="attend_back",
    )(q, k, v, g, o, probs, *tables)


def rotary_tables(segments):
    rows, length = segments.shape
    index = jnp.arange(length, dtype=jnp.int32)[None]
    start = jnp.zeros_like(segments)
    for number in range(1, 4):
        start = jnp.where(segments == number, jnp.sum(segments < number, -1, keepdims=True), start)
    position = (index - start).astype(f32).reshape(rows * length, 1)
    lane = jnp.arange(128, dtype=jnp.int32) % HD
    exponent = (2 * (lane % (ROT // 2))).astype(f32) / ROT
    angle = position * (1.0 / 10000.0**exponent)[None]
    cosine, sine = jnp.cos(angle), jnp.sin(angle)
    low, high = lane < ROT // 2, (lane >= ROT // 2) & (lane < ROT)
    return (
        jnp.where(lane < ROT, cosine, 1.0),
        jnp.where(low, -sine, 0.0),
        jnp.where(high, sine, 0.0),
    )


def matmul(a, b):
    return jnp.dot(a, b, preferred_element_type=f32)


def on_device(
    dp, tensor, fast,
    hidden_in, segments, ln_gain, ln_bias, qkv_weight, qkv_bias, dense_weight, dense_bias,
    fc1_weight, fc1_bias, fc2_weight, fc2_bias, cotangent,
):
    seqs = segments.shape[0]
    local = qkv_weight.shape[2]
    vectors = jnp.stack([ln_gain.astype(f32), ln_bias.astype(f32), dense_bias.astype(f32) + fc2_bias.astype(f32)])
    vectors = jnp.pad(vectors, ((0, 5), (0, 0)))
    mine = (
        hidden_in, cotangent, qkv_weight.transpose(1, 0, 2),
        dense_weight, fc1_weight, fc2_weight, vectors,
    )
    gathered = gather_call(dp, tensor, *mine) if fast else gather_plain(*mine)
    w_qkv, w_dense, w_fc1, w_fc2, normed, grad_out, vec = gathered
    gain, out_bias = vec[0:1], vec[2:3]
    resid_in = hidden_in.astype(f32)
    cot_float = cotangent.astype(f32)
    centred = resid_in - jnp.mean(resid_in, -1, keepdims=True)
    spread = jnp.mean(centred * centred, -1, keepdims=True)
    inv_std = lax.rsqrt(spread + layer_eps)
    unit_rows = centred * inv_std

    tables = rotary_tables(segments)
    bias = jnp.pad(qkv_bias.astype(f32), ((0, 5), (0, 0)))
    query, key, value, attn_vec, probs = attend(
        *(matmul(normed, w_qkv[i]) for i in range(3)), bias, tables, segments, seqs
    )
    pre_act = matmul(normed, w_fc1) + fc1_bias.astype(f32)
    act_vals, gelu_pull = jax.vjp(lambda pre: jax.nn.gelu(pre, approximate=True), pre_act)
    act_vals = act_vals.astype(bf16)
    branches = matmul(attn_vec, w_dense) + matmul(act_vals, w_fc2)
    summed = lax.psum_scatter(branches.astype(bf16), "tensor", scatter_dimension=0, tiled=True)
    out = (resid_in + summed.astype(f32) + out_bias).astype(bf16)

    out_bias_part = jnp.sum(cot_float, 0)
    grad_fc2 = matmul(act_vals.T, grad_out)
    grad_dense = matmul(attn_vec.T, grad_out)
    grad_pre = gelu_pull(matmul(grad_out, w_fc2.T))[0].astype(bf16)
    fc1_bias_part = jnp.sum(grad_pre.astype(f32), 0)
    grad_fc1 = matmul(normed.T, grad_pre)
    grad_attn = matmul(grad_out, w_dense.T).astype(bf16)
    *grads, qkv_bias_part = attend_back(query, key, value, grad_attn, attn_vec, probs, tables, seqs)
    grad_wqkv = jnp.stack([matmul(normed.T, g) for g in grads])
    grad_normed = matmul(grad_pre, w_fc1.T) + sum(matmul(g, w.T) for g, w in zip(grads, w_qkv))
    sent_qkv, sent_dense, sent_fc1, sent_fc2 = (
        lax.psum_scatter(grad_wqkv.astype(bf16), "dp", scatter_dimension=1, tiled=True),
        lax.psum_scatter(grad_dense.astype(bf16), "dp", scatter_dimension=1, tiled=True),
        lax.psum_scatter(grad_fc1.astype(bf16), "dp", scatter_dimension=0, tiled=True),
        lax.psum_scatter(grad_fc2.astype(bf16), "dp", scatter_dimension=1, tiled=True),
    )
    grad_local = lax.psum_scatter(
        grad_normed.astype(bf16), "tensor", scatter_dimension=0, tiled=True
    ).astype(f32)
    gain_part = jnp.sum(grad_local * unit_rows, 0)
    beta_part = jnp.sum(grad_local, 0)
    scaled_grad = grad_local * gain
    first_mean = jnp.mean(scaled_grad, -1, keepdims=True)
    second_mean = jnp.mean(scaled_grad * unit_rows, -1, keepdims=True)
    hidden_grad = (
        cot_float + inv_std * (scaled_grad - first_mean - unit_rows * second_mean)
    ).astype(bf16)
    gain_grad, beta_grad, out_bias_grad = (
        lax.psum_scatter(gain_part, ("dp", "tensor"), scatter_dimension=0, tiled=True),
        lax.psum_scatter(beta_part, ("dp", "tensor"), scatter_dimension=0, tiled=True),
        lax.psum_scatter(out_bias_part, ("dp", "tensor"), scatter_dimension=0, tiled=True),
    )
    qkv_bias_grad, fc1_bias_grad = lax.psum((qkv_bias_part[:3], fc1_bias_part), "dp")
    return (
        out,
        hidden_grad,
        gain_grad,
        beta_grad,
        sent_qkv.transpose(1, 0, 2).astype(f32),
        qkv_bias_grad,
        sent_dense.astype(f32),
        out_bias_grad,
        sent_fc1.astype(f32),
        fc1_bias_grad,
        sent_fc2.astype(f32),
        out_bias_grad,
    )


def solution(mesh):
    dp, tensor = mesh.shape["dp"], mesh.shape["tensor"]
    fast = dp == 8 and tensor == 4
    placed = (
        P(("dp", "tensor"), None),
        P("dp", None),
        P("dp"),
        P("dp"),
        P("dp", None, "tensor"),
        P(None, "tensor"),
        P("tensor", "dp"),
        P("dp"),
        P("dp", "tensor"),
        P("tensor"),
        P("tensor", "dp"),
        P("dp"),
        P(("dp", "tensor"), None),
    )
    return jax.shard_map(
        functools.partial(on_device, dp, tensor, fast),
        mesh=mesh,
        in_specs=placed,
        out_specs=(
            P(("dp", "tensor"), None),
            P(("dp", "tensor"), None),
            P(("dp", "tensor")),
            P(("dp", "tensor")),
            P("dp", None, "tensor"),
            P(None, "tensor"),
            P("tensor", "dp"),
            P(("dp", "tensor")),
            P("dp", "tensor"),
            P("tensor"),
            P("tensor", "dp"),
            P(("dp", "tensor")),
        ),
        check_vma=False,
    )
```

time: 1240 us -> 707 us (0.57)
  waiting for transfers between devices: 723 us -> 224 us
  Pallas kernels: 0 us -> 202 us
  matrix products: 238 us -> 158 us
  local copies, waits for them, and re-layouts: 79 us -> 4.45 us
  blocking collectives: 102 us -> 65.5 us
  other arithmetic: 56.2 us -> 29.1 us
    reduce_scatter x6, waiting for transfers between devices: 516 us -> 224 us  [the longest x1 72.3 us: on_device(): lax.psum_scatter(grad_fc1.astype(bf16), 'dp', scatter_dimension=0, tiled=...]
    all_gather x6 -> x0, waiting for transfers between devices: 205 us -> none  [the longest x1 82.3 us: on_device(): grad_out = lax.all_gather(cotangent, 'tensor', axis=0, tiled=True)]
    pallas_call x0 -> x3, Pallas kernels: none -> 202 us  [the longest x1 164 us: gather_call(): pl.pallas_call(kernel, out_shape=(jax.ShapeDtypeStruct((3, width, local),...]
    dot_general x26 -> x18, matrix products: 238 us -> 158 us  [matmul(): return jnp.dot(a, b, preferred_element_type=f32)]
    dynamic_update_slice x4 -> x0, local copies, waits for them, and re-layouts: 43.4 us -> none  [row_forward(): outputs, log_sums = lax.map(one_block, (q_blocks, starts))]
    all_gather x4 -> x0, blocking collectives: 36.9 us -> none  [the longest x1 10.4 us: on_device(): lax.all_gather(ln_gain, 'dp', axis=0, tiled=True)]
  transfers between devices with their start and end apart: 12 -> 6, of which waited for: 10 -> 4; matrix products, arithmetic and copies ran while one was open for 27% -> 23% of each run, Pallas kernels for 0% -> 3%
where the time goes in v1:
time: 707 us; the launch traced here: 698 us
  waiting for transfers between devices  224 us (32%)
  Pallas kernels  202 us (29%)
  matrix products  158 us (22%)
  blocking collectives  65.5 us (9%)
  other arithmetic  29.1 us (4%)
  between operations  14.6 us (2%)
    pallas_call x1, Pallas kernels, gather_call(): pl.pallas_call(kernel, out_shape=(jax.ShapeDtypeStruct((3, width, local),...  164 us
    dot_general x18, matrix products, matmul(): return jnp.dot(a, b, preferred_element_type=f32)  158 us
    reduce_scatter x1, waiting for transfers between devices, on_device(): lax.psum_scatter(grad_fc1.astype(bf16), 'dp', scatter_dimension=0, tiled=...  72.3 us
    reduce_scatter x1, waiting for transfers between devices, on_device(): lax.psum_scatter(grad_fc2.astype(bf16), 'dp', scatter_dimension=1, tiled=...  71.8 us
    reduce_scatter x1, waiting for transfers between devices, on_device(): lax.psum_scatter(branches.astype(bf16), 'tensor', scatter_dimension=0, ti...  60.9 us
    unnamed x1, blocking collectives  41.5 us
    psum x1, blocking collectives, on_device(): lax.psum((qkv_bias_part[:3], fc1_bias_part), 'dp')  24 us
    reduce_scatter x1, waiting for transfers between devices, on_device(): lax.psum_scatter(grad_wqkv.astype(bf16), 'dp', scatter_dimension=1, tiled...  19.1 us
  transfers between devices with their start and end apart: 6, of which 4 were waited for; matrix products, arithmetic and copies ran while one was open for 23% of the time, Pallas kernels for 3%

profile of v1, /device:TPU:0, one launch (start us, length us, event | category | flops | bytes accessed | tf_op | source)
XLA Modules:
  0.0 698.1 jit_solution(15046863038365166221)
XLA Ops:
  9.8 164.3 %gather.1 = (bf16[3,2048,512]{2,1,0:T(8,128)(2,1)}, bf16[512,2048]{1,0:T(8,128)(2,1)}, bf16[2048,2048]{1,0:T(8,128)(2,1)}, bf16[2048,2048]{1,0:T(8,128)(2,1)}, b...) custom-call(bf16[256,2048]{1,0:T(8,128)(2,1)} %x_ref.1, bf16[256,2048]{1,0:T(8,128)(2,1)} %c_ref.1, ...), custom_call_target="tpu_custom_call" | custom-call | tf_op jit(solution)/shard_map/gather/pallas_call | solution.py:340
  174.1 6.7 fusion.25.v_ref
  195.6 18.2 %attend.1 = (bf16[1024,512]{1,0:T(8,128)(2,1)}, bf16[1024,512]{1,0:T(8,128)(2,1)}, bf16[1024,512]{1,0:T(8,128)(2,1)}, bf16[1024,512]{1,0:T(8,128)(2,1)}, bf16[1,8,2304,256]{3,2,1,0:T(8,128)(2,1)}) custom-call(f32[1024,512]{1,0:T(8,128)} %fusion.33.q_ref, f32[1024,512]{1,0:T(8,128)} %fusion.29.k_ref, f32[1024,512]{1,0:T(8,128)} %fusion.25.v_ref, ...), custom_call_target="tpu_custom_call" | custom-call | flops 6442450944 | bytes 25165824 | tf_op jit(solution)/shard_map/attend/pallas_call | solution.py:456
  213.8 6.3 convolution_convert_fusion.2
  220.2 5.7 convolution_convert_fusion.6.g_ref
  225.9 13.5 %fusion.59 = f32[1024,2048]{1,0:T(8,128)} fusion(bf16[1024,2048]{1,0:T(8,128)(2,1)S(1)} %copy-done.10, bf16[2048,2048]{1,0:T(8,128)(2,1)} %get-tuple-element.32), kind=kOutput, calls=%fused_computation.105 | convolution fusion | flops 8589934592 | bytes 20971520 | tf_op jit(solution)/shard_map/dot_general | solution.py:579
  239.4 19.1 %attend_back.1 = (bf16[1024,512]{1,0:T(8,128)(2,1)}, bf16[1024,512]{1,0:T(8,128)(2,1)}, bf16[1024,512]{1,0:T(8,128)(2,1)}, f32[8,512]{1,0:T(8,128)}) custom-call(bf16[1024,512]{1,0:T(8,128)(2,1)} %get-tuple-element.36.q_ref, bf16[1024,512]{1,0:T(8,128)(2,1)} %get-tuple-element.37.k_ref, bf16[1024,512]{1,0:T(8,128)(2,1)} %get-tuple-element.38.v_ref, ...), custom_call_target="tpu_custom_call" | custom-call | flops 12884901888 | bytes 25165824 | tf_op jit(solution)/shard_map/attend_back/pallas_call | solution.py:542
  258.5 4.4 fusion.27
  263.0 7.3 %fusion.31 = f32[1024,2048]{1,0:T(8,128)} fusion(bf16[1024,512]{1,0:T(8,128)(2,1)S(1)} %copy-done.16, bf16[3,2048,512]{2,1,0:T(8,128)(2,1)} %get-tuple-element.29), kind=kOutput, calls=%fused_computation.52 | convolution fusion | flops 2147483648 | bytes 11534336 | tf_op jit(solution)/shard_map/dot_general | solution.py:579
  270.3 20.2 %convert_reduce_fusion = (f32[2048]{0:T(1024)S(1)}, bf16[1024,2048]{1,0:T(8,128)(2,1)}) fusion(f32[1024,2048]{1,0:T(8,128)} %fusion.59, f32[2048]{0:T(1024)S(1)} %convert_element_type.104, bf16[1024,2048]{1,0:T(8,128)(2,1)S(1)} %copy-done.8, bf16[2048,2048]{1,0:T(8,128)(2,1)} %get-tuple-element.33), kind=kOutput, calls=%fused_computation.9 | convolution fusion | flops 8638167040 | bytes 25182208 | tf_op jit(solution)/shard_map/dot_general | solution.py:579
  290.5 14.6 %fusion.60 = f32[1024,2048]{1,0:T(8,128)} fusion(bf16[1024,2048]{1,0:T(8,128)(2,1)} %get-tuple-element.57, bf16[2048,2048]{1,0:T(8,128)(2,1)} %get-tuple-element.32), kind=kOutput, calls=%fused_computation.106 | convolution fusion | flops 8589934592 | bytes 20971520 | tf_op jit(solution)/shard_map/dot_general | solution.py:579
  305.1 11.6 %add_convert_fusion = bf16[1024,2048]{1,0:T(8,128)(2,1)} fusion(f32[1024,2048]{1,0:T(8,128)} %fusion.60, f32[1024,2048]{1,0:T(8,128)} %fusion.31, f32[1024,2048]{1,0:T(8,128)S(1)} %fusion.27, bf16[1024,512]{1,0:T(8,128)(2,1)S(1)} %copy-done.2, bf16[3,2048,512]{2,1,0:T(8,128)(2,1)} %get-tuple-element.29), kind=kOutput, calls=%fused_computation.10 | convolution fusion | flops 2155872256 | bytes 32505856 | tf_op jit(solution)/shard_map/dot_general | solution.py:579
  316.8 16.3 %fusion.56 = f32[1024,2048]{1,0:T(8,128)S(1)} fusion(bf16[2048,2048]{1,0:T(8,128)(2,1)} %get-tuple-element.33, f32[1024,2048]{1,0:T(8,128)} %fusion.59, f32[2048]{0:T(1024)S(1)} %convert_element_type.104), kind=kOutput, calls=%fused_computation.103 | convolution fusion | flops 8610906112 | bytes 25174016 | tf_op jit(solution)/shard_map/dot_general | solution.py:579
  333.1 4.3 add_convert_fusion.1
  337.5 5.0 fusion.10
  350.7 14.1 %convolution_convert_fusion.1 = bf16[2048,2048]{1,0:T(8,128)(2,1)} fusion(bf16[1024,2048]{1,0:T(8,128)(2,1)} %get-tuple-element.28, bf16[1024,2048]{1,0:T(8,128)(2,1)} %get-tuple-element.57), kind=kOutput, calls=%fused_computation.14 | convolution fusion | flops 8594128896 | bytes 16777216 | tf_op jit(solution)/shard_map/dot_general | solution.py:579
  365.0 15.9 %convolution_convert_fusion = bf16[2048,2048]{1,0:T(8,128)(2,1)} fusion(bf16[1024,2048]{1,0:T(8,128)(2,1)} %get-tuple-element.35, f32[1024,2048]{1,0:T(8,128)} %fusion.59, f32[2048]{0:T(1024)S(1)} %convert_element_type.104), kind=kOutput, calls=%fused_computation.13 | convolution fusion | flops 8615100416 | bytes 20979712 | tf_op jit(solution)/shard_map/dot_general | solution.py:579
  381.6 24.0 %all-reduce.6 = (f32[3,512]{1,0:T(4,128)}, f32[2048]{0:T(1024)}) all-reduce(f32[3,512]{1,0:T(4,128)S(1)} %slice.23, f32[2048]{0:T(1024)S(1)} %get-tuple-element.56), channel_id=1, replica_groups=mesh['dp'=8,'tensor'=4] {'dp'}, use_global_device_ids=true, to_apply=%region_14.15 | all-reduce | flops 3584 | bytes 28672 | tf_op jit(solution)/shard_map/psum | solution.py:649
  411.4 60.9 %reduce-scatter.7.cloned.1.call-done = bf16[256,2048]{1,0:T(8,128)(2,1)} async-done(((bf16[1024,2048]{1,0:T(8,128)(2,1)}), bf16[256,2048]{1,0:T(8,128)(2,1)}) %reduce-scatter.7.cloned.1.call-update) | async-done | bytes 1048592 | tf_op jit(solution)/shard_map/reduce_scatter | solution.py:614
  472.3 4.3 convert_reduce_fusion.3
  476.6 41.5 %all-reduce.5 = (f32[2048]{0:T(1024)S(1)}, f32[2048]{0:T(1024)S(1)}, f32[2048]{0:T(1024)S(1)}) all-reduce(f32[2048]{0:T(1024)S(1)} %get-tuple-element.44, f32[2048]{0:T(1024)S(1)} %get-tuple-element.47, f32[2048]{0:T(1024)S(1)} %get-tuple-element.58), channel_id=4, replica_groups=mesh['dp'=8,'tensor'=4] {'dp','tensor'}, use_global_device_ids=true, to_apply=%region_10.11.clone | all-reduce | flops 6144 | bytes 49152
  519.3 19.1 %reduce-scatter.11.cloned.1.call-done = bf16[3,256,512]{2,1,0:T(8,128)(2,1)} async-done(((bf16[3,2048,512]{2,1,0:T(8,128)(2,1)}), bf16[3,256,512]{2,1,0:T(8,128)(2,1)}) %reduce-scatter.11.cloned.1.call-update) | async-done | bytes 786448 | tf_op jit(solution)/shard_map/reduce_scatter | solution.py:628
  540.9 72.3 %reduce-scatter.15.cloned.1.call-done = bf16[256,2048]{1,0:T(8,128)(2,1)} async-done(((bf16[2048,2048]{1,0:T(8,128)(2,1)}), bf16[256,2048]{1,0:T(8,128)(2,1)}) %reduce-scatter.15.cloned.1.call-update) | async-done | bytes 1048592 | tf_op jit(solution)/shard_map/reduce_scatter | solution.py:630
  616.0 71.8 %reduce-scatter.17.cloned.1.call-done = bf16[2048,256]{1,0:T(8,128)(2,1)} async-done(((bf16[2048,2048]{1,0:T(8,128)(2,1)}), bf16[2048,256]{1,0:T(8,128)(2,1)}) %reduce-scatter.17.cloned.1.call-update) | async-done | bytes 1048592 | tf_op jit(solution)/shard_map/reduce_scatter | solution.py:631
  (85 shorter events, 42.0 us)
Async XLA Ops:
  7.2 400.1 %reduce-scatter.13.cloned.1.call-start = ((), (), s32[]{:S(2)}) async-start(), calls=%async_computation.9 | async-start | bytes 2359296 | tf_op jit(solution)/shard_map/reduce_scatter | solution.py:629
  174.1 6.7 copy-start.3
  174.1 6.7 copy-start.9
  184.5 3.7 copy-start.4
  184.5 5.4 copy-start.5
  213.8 6.4 copy-start.12
  220.2 188.9 %reduce-scatter.9.cloned.1.call-start = ((), (), s32[]{:S(2)}) async-start(), calls=%async_computation.7 | async-start | bytes 5242880 | tf_op jit(solution)/shard_map/reduce_scatter | solution.py:633
  220.2 5.7 copy-start.10
  225.9 13.6 %copy-start.6 = (bf16[2048]{0:T(1024)(128)(2,1)S(1)}, bf16[2048]{0:T(1024)(128)(2,1)}, u32[]{:S(2)}) copy-start(bf16[2048]{0:T(1024)(128)(2,1)} %param.22) | copy-start | bytes 12292
  258.5 4.4 copy-start.16
  262.9 7.4 %copy-start.8 = (bf16[1024,2048]{1,0:T(8,128)(2,1)S(1)}, bf16[1024,2048]{1,0:T(8,128)(2,1)}, u32[]{:S(2)}) copy-start(bf16[1024,2048]{1,0:T(8,128)(2,1)} %get-tuple-element.35) | copy-start | bytes 12582916
  290.5 14.6 %copy-start.2 = (bf16[1024,512]{1,0:T(8,128)(2,1)S(1)}, bf16[1024,512]{1,0:T(8,128)(2,1)}, u32[]{:S(2)}) copy-start(bf16[1024,512]{1,0:T(8,128)(2,1)} %get-tuple-element.42) | copy-start | bytes 3145732
  316.7 155.6 %reduce-scatter.7.cloned.1.call-start = ((), (), s32[]{:S(2)}) async-start(), calls=%async_computation.6 | async-start | bytes 5242880 | tf_op jit(solution)/shard_map/reduce_scatter | solution.py:614
  316.8 16.3 %copy-start.13 = (bf16[512,2048]{1,0:T(8,128)(2,1)S(1)}, bf16[512,2048]{1,0:T(8,128)(2,1)}, u32[]{:S(2)}) copy-start(bf16[512,2048]{1,0:T(8,128)(2,1)} %get-tuple-element.31) | copy-start | bytes 6291460
  316.8 16.3 %copy-start.17 = (bf16[1024,512]{1,0:T(8,128)(2,1)S(1)}, bf16[1024,512]{1,0:T(8,128)(2,1)}, u32[]{:S(2)}) copy-start(bf16[1024,512]{1,0:T(8,128)(2,1)} %get-tuple-element.30.o_ref) | copy-start | bytes 3145732
  337.4 201.0 %reduce-scatter.11.cloned.1.call-start = ((), (), s32[]{:S(2)}) async-start(), calls=%async_computation.8 | async-start | bytes 7077888 | tf_op jit(solution)/shard_map/reduce_scatter | solution.py:628
  337.5 5.0 copy-start.11
  337.5 5.0 copy-start.15
  350.6 262.7 %reduce-scatter.15.cloned.1.call-start = ((), (), s32[]{:S(2)}) async-start(), calls=%async_computation.10 | async-start | bytes 9437184 | tf_op jit(solution)/shard_map/reduce_scatter | solution.py:630
  364.8 323.1 %reduce-scatter.17.cloned.1.call-start = ((), (), s32[]{:S(2)}) async-start(), calls=%async_computation.11 | async-start | bytes 9437184 | tf_op jit(solution)/shard_map/reduce_scatter | solution.py:631
  380.9 0.7 copy-start.7
  380.9 24.7 %copy-start = (bf16[256,2048]{1,0:T(8,128)(2,1)S(1)}, bf16[256,2048]{1,0:T(8,128)(2,1)}, u32[]{:S(2)}) copy-start(bf16[256,2048]{1,0:T(8,128)(2,1)} %x_ref.1) | copy-start | bytes 3145732
  381.0 91.4 %copy-start.1 = (bf16[256,2048]{1,0:T(8,128)(2,1)S(1)}, bf16[256,2048]{1,0:T(8,128)(2,1)}, u32[]{:S(2)}) copy-start(bf16[256,2048]{1,0:T(8,128)(2,1)} %c_ref.1) | copy-start | bytes 3145732
  518.2 172.4 %copy-start.14 = (f32[64]{0:T(128)}, f32[64]{0:T(128)S(1)}, u32[]{:S(2)}) copy-start(f32[64]{0:T(128)S(1)} %dynamic-slice.2) | copy-start | bytes 772
Sparse Core Ops, SparseCore 0:
  220.3 40.2 reduce-scatter.12
  316.8 75.7 reduce-scatter.8
  395.0 77.2 reduce-scatter.6
  475.5 62.8 reduce-scatter.10
  541.7 71.4 reduce-scatter.14
  616.6 71.2 reduce-scatter.16

commit v2 on v1

--- a/solution.py
+++ b/solution.py
@@ -180,19 +180,30 @@
                 self.copy(way, s, u).wait_send()
 
 
-def greet(dp, me, tensor, line):
+def greet(dp, me, tensor, line, wide=False):
     barrier = pltpu.get_barrier_semaphore()
+
+    def hello(a, b):
+        pl.semaphore_signal(barrier, inc=1, device_id=(a, b), device_id_type=MESH)
+
+    if wide:
+        for r in range(1, dp):
+            hello(relative(me, r), line)
+        for k in range(1, tensor):
+            hello(me, lax.rem(line + k, tensor))
+        pl.semaphore_wait(barrier, dp + tensor - 2)
+        return
     bits = dp.bit_length() - 1
     for bit in range(bits):
-        pl.semaphore_signal(barrier, inc=1, device_id=(flip(me, bit), line), device_id_type=MESH)
+        hello(flip(me, bit), line)
 
     @pl.when(line > 0)
     def _():
-        pl.semaphore_signal(barrier, inc=1, device_id=(me, line - 1), device_id_type=MESH)
+        hello(me, line - 1)
 
     @pl.when(line < tensor - 1)
     def _():
-        pl.semaphore_signal(barrier, inc=1, device_id=(me, line + 1), device_id_type=MESH)
+        hello(me, line + 1)
 
     left, right = jnp.minimum(line, 1), jnp.minimum(tensor - 1 - line, 1)
     pl.semaphore_wait(barrier, bits + left + right)
@@ -384,6 +395,587 @@
         lax.all_gather(cotangent, "tensor", axis=0, tiled=True),
         vec,
     )
+
+
+class ChipReduce:
+    COUNT = 6
+
+    def __init__(self, sems):
+        self.ids = [sems.take() for _ in range(self.COUNT)]
+
+    def bind(self, me, other, parts, landing, send_sem, recv_sem):
+        self.me, self.other, self.parts, self.landing = me, other, parts, landing
+        self.send_sem, self.recv_sem = send_sem, recv_sem
+        self.half = parts.shape[-1] // 2
+        return self
+
+    def view(self, r, h):
+        return self.parts.at[r, :, pl.ds(h * self.half, self.half)]
+
+    def copy(self, slot):
+        r, h, bit = [(2, 0, 2), (3, 0, 2), (1, 0, 1), (1, 1, 1), (3, 1, 1), (2, 1, 2)][slot]
+        k = self.ids[slot]
+        return pltpu.make_async_remote_copy(
+            src_ref=self.view(r, h),
+            dst_ref=self.landing.at[slot],
+            send_sem=self.send_sem.at[k],
+            recv_sem=self.recv_sem.at[k],
+            device_id=(flip(self.me, bit), self.other),
+            device_id_type=MESH,
+        )
+
+    def start(self, r):
+        for slot in {3: (1, 4), 2: (0,), 1: (3,), 0: ()}[r]:
+            self.copy(slot).start()
+
+    def middle(self):
+        for slot, r, h, last in ((1, 1, 0, 2), (4, 2, 1, 5)):
+            self.copy(slot).wait_recv()
+            view = self.view(r, h)
+            view[...] = (view[...].astype(f32) + self.landing[slot].astype(f32)).astype(bf16)
+            self.copy(last).start()
+
+    def final(self):
+        for h in (0, 1):
+            for slot in ((0, 2), (3, 5))[h]:
+                self.copy(slot).wait_recv()
+            a, b = ((0, 2), (3, 5))[h]
+            view = self.view(0, h)
+            total = view[...].astype(f32) + self.landing[a].astype(f32) + self.landing[b].astype(f32)
+            view[...] = total.astype(bf16)
+
+    def finish(self):
+        for slot in range(self.COUNT):
+            self.copy(slot).wait_send()
+
+
+class LineReduce:
+    def __init__(self, sems, size):
+        self.size = size
+        self.ids = {(way, i): sems.take() for way in (0, 1) for i in range(size - 1)}
+
+    def bind(self, me, other, own, landing, send_sem, recv_sem):
+        self.me, self.other, self.own, self.landing = me, other, own, landing
+        self.send_sem, self.recv_sem = send_sem, recv_sem
+        return self
+
+    def target(self, way, i):
+        return self.size - 1 - i if way == 0 else i
+
+    def copy(self, way, i, edge):
+        k = self.ids[way, i]
+        here = self.landing.at[way, i]
+        return pltpu.make_async_remote_copy(
+            src_ref=self.own(self.target(way, i)) if edge else here,
+            dst_ref=here,
+            send_sem=self.send_sem.at[k],
+            recv_sem=self.recv_sem.at[k],
+            device_id=(self.other, self.me + 1 if way == 0 else self.me - 1),
+            device_id_type=MESH,
+        )
+
+    def edge(self, way):
+        return self.me == (0 if way == 0 else self.size - 1)
+
+    def passes(self, way, i):
+        d = self.target(way, i)
+        return (self.me > 0) & (self.me < d) if way == 0 else (self.me < self.size - 1) & (self.me > d)
+
+    def start(self, way, i):
+        @pl.when(self.edge(way))
+        def _():
+            self.copy(way, i, True).start()
+
+    def advance(self, step, add):
+        for way in (0, 1):
+            steps_from_edge = self.me if way == 0 else self.size - 1 - self.me
+            for i in range(step):
+
+                @pl.when(self.passes(way, i) & (steps_from_edge == step - i))
+                def _():
+                    self.copy(way, i, False).wait_recv()
+                    add(self.landing.at[way, i], self.own(self.target(way, i)))
+                    self.copy(way, i, False).start()
+
+    def arrive(self):
+        for way in (0, 1):
+            for i in range(self.size - 1):
+
+                @pl.when(self.me == self.target(way, i))
+                def _():
+                    self.copy(way, i, False).wait_recv()
+
+    def finish(self):
+        for way, i in self.ids:
+
+            @pl.when(self.edge(way))
+            def _():
+                self.copy(way, i, True).wait_send()
+
+            @pl.when(self.passes(way, i))
+            def _():
+                self.copy(way, i, False).wait_send()
+
+    def total(self, own, rows):
+        last = self.size - 1
+        value = own.astype(f32)
+        lefts = jnp.clip(last - self.me, 0, last - 1)
+        rights = jnp.clip(self.me, 0, last - 1)
+        from_left = self.landing[0, lefts, rows, :].astype(f32)
+        from_right = self.landing[1, rights, rows, :].astype(f32)
+        value = value + jnp.where(self.me > 0, from_left, 0.0)
+        return value + jnp.where(self.me < last, from_right, 0.0)
+
+
+def add_into(landing, own):
+    rows = landing.shape[0]
+
+    @pl.loop(0, rows, step=64)
+    def _(r):
+        at = pl.ds(r, 64)
+        landing[at, :] = (landing[at, :].astype(f32) + own[at, :].astype(f32)).astype(bf16)
+
+
+def first_call(dp, tensor, arrays):
+    hidden, vec, branches, grad_out, act, slope, attn, w_fc2 = arrays
+    rows, width = hidden.shape
+    tokens, units = act.shape
+    local = attn.shape[1]
+    part = width // dp
+    chips = dp // 2
+    sems = Sems()
+    reduce_fc2, reduce_dense = ChipReduce(sems), ChipReduce(sems)
+    line_out = LineReduce(sems, tensor)
+    swaps = [sems.take() for _ in range(chips + 2)]
+
+    def kernel(
+        x_ref, vec_ref, b_ref, c_ref, a_ref, d_ref, t_ref, w2_ref,
+        out_ref, gp_ref, sum_ref, s2_out, sd_out,
+        x_buf, c_buf, cx_buf, a_buf, ax_buf, t_buf, tx_buf, w2_buf, d_buf, own_buf,
+        s2, sd, r2, rd, rz, send_sem, recv_sem, local_sem,
+    ):
+        me, line = lax.axis_index("dp"), lax.axis_index("tensor")
+        twin = flip(me, 0)
+
+        def cols(a):
+            return pl.ds(pl.multiple_of(a * part, part), part)
+
+        def block(d):
+            return pl.ds(pl.multiple_of(d * rows, rows), rows)
+
+        pair = (send_sem, recv_sem)
+        fc2 = reduce_fc2.bind(me, line, s2, r2, *pair)
+        dense = reduce_dense.bind(me, line, sd, rd, *pair)
+        outs = line_out.bind(line, me, lambda d: b_ref.at[pl.ds(d * rows, rows), :], rz, *pair)
+
+        def swap(k, source, target):
+            return pltpu.make_async_remote_copy(
+                src_ref=source, dst_ref=target,
+                send_sem=send_sem.at[swaps[k]], recv_sem=recv_sem.at[swaps[k]],
+                device_id=(twin, line), device_id_type=MESH)
+
+        crossing = [
+            swap(r, c_ref.at[:, cols(relative(twin, r << 1))], cx_buf.at[r]) for r in range(chips)
+        ] + [swap(chips, a_ref, ax_buf), swap(chips + 1, t_ref, tx_buf)]
+        loads = [
+            pltpu.make_async_copy(a, b, local_sem.at[k])
+            for k, (a, b) in enumerate([
+                (c_ref, c_buf), (a_ref, a_buf), (t_ref, t_buf), (w2_ref, w2_buf), (d_ref, d_buf),
+                (x_ref, x_buf), (b_ref.at[block(line), :], own_buf),
+            ])
+        ]
+        loads[0].start()
+        loads[1].start()
+        greet(dp, me, tensor, line)
+        for copy in (crossing[3], crossing[chips]):
+            copy.start()
+        for i in range(tensor - 1):
+            outs.start(0, i)
+            outs.start(1, i)
+        for copy in crossing[:3] + crossing[chips + 1 :]:
+            copy.start()
+        for copy in loads[2:]:
+            copy.start()
+        loads[0].wait()
+        loads[1].wait()
+        crossing[chips].wait_recv()
+
+        @pl.loop(0, chips)
+        def _(i):
+            r = chips - 1 - i
+            slot = me + 2 * ((r % 2) * (1 - 2 * (lax.div(me, 2) % 2))) + 4 * (
+                lax.div(r, 2) * (1 - 2 * (lax.div(me, 4) % 2)))
+            for k in range(chips):
+
+                @pl.when(r == k)
+                def _():
+                    crossing[k].wait_recv()
+
+            @pl.loop(0, units, step=1024)
+            def _(n):
+                at = pl.ds(pl.multiple_of(n, 1024), 1024)
+                value = dot_tn(c_buf[:, cols(slot)], a_buf[:, at])
+                value = value + dot_tn(cx_buf[r], ax_buf[:, at])
+                s2[r, :, at] = value.astype(bf16)
+
+            for k in range(1, chips):
+
+                @pl.when(r == k)
+                def _():
+                    fc2.start(k)
+
+        loads[2].wait()
+        crossing[chips + 1].wait_recv()
+
+        @pl.loop(0, chips)
+        def _(i):
+            r = chips - 1 - i
+            slot = me + 2 * ((r % 2) * (1 - 2 * (lax.div(me, 2) % 2))) + 4 * (
+                lax.div(r, 2) * (1 - 2 * (lax.div(me, 4) % 2)))
+            value = dot_tn(c_buf[:, cols(slot)], t_buf[...]) + dot_tn(cx_buf[r], tx_buf[...])
+            sd[r] = value.astype(bf16)
+            for k in range(1, chips):
+
+                @pl.when(r == k)
+                def _():
+                    dense.start(k)
+
+        loads[3].wait()
+        loads[4].wait()
+
+        def slope_tile(n):
+            at = pl.ds(pl.multiple_of(n, 512), 512)
+            value = dot_nt(c_buf[...], w2_buf[at, :]) * d_buf[:, at].astype(f32)
+            value = value.astype(bf16)
+            d_buf[:, at] = value
+            sum_ref[0:1, at] = jnp.sum(value.astype(f32), 0, keepdims=True)
+
+        @pl.loop(0, units, step=512)
+        def _(n):
+            slope_tile(n)
+
+        store = pltpu.make_async_copy(d_buf, gp_ref, local_sem.at[len(loads)])
+        store.start()
+
+        def add_out(landing, own):
+            copy = pltpu.make_async_copy(own, a_buf.at[pl.ds(0, rows), :], local_sem.at[len(loads) + 1])
+            copy.start()
+            copy.wait()
+            add_into(landing, a_buf.at[pl.ds(0, rows), :])
+
+        outs.advance(1, add_out)
+        fc2.middle()
+        outs.advance(2, add_out)
+        dense.middle()
+        fc2.final()
+        dense.final()
+        store2 = pltpu.make_async_copy(s2.at[0], s2_out, local_sem.at[len(loads) + 2])
+        stored = pltpu.make_async_copy(sd.at[0], sd_out, local_sem.at[len(loads) + 3])
+        store2.start()
+        stored.start()
+        for copy in loads[5:]:
+            copy.wait()
+        outs.arrive()
+
+        @pl.loop(0, rows, step=32)
+        def _(r):
+            at = pl.ds(r, 32)
+            total = x_buf[at, :].astype(f32) + outs.total(own_buf[at, :], at) + vec_ref[2:3, :]
+            x_buf[at, :] = total.astype(bf16)
+
+        last = pltpu.make_async_copy(x_buf, out_ref, local_sem.at[len(loads) + 4])
+        last.start()
+        for copy in crossing:
+            copy.wait_send()
+        for plan in (fc2, dense, outs):
+            plan.finish()
+        for copy in (store, store2, stored, last):
+            copy.wait()
+
+    return pl.pallas_call(
+        kernel,
+        out_shape=(
+            jax.ShapeDtypeStruct((rows, width), bf16),
+            jax.ShapeDtypeStruct((tokens, units), bf16),
+            jax.ShapeDtypeStruct((8, units), f32),
+            jax.ShapeDtypeStruct((part, units), bf16),
+            jax.ShapeDtypeStruct((part, local), bf16),
+        ),
+        in_specs=[ANY, VMEM] + [ANY] * 6,
+        out_specs=(ANY, ANY, VMEM, ANY, ANY),
+        scratch_shapes=[
+            pltpu.VMEM((rows, width), bf16),
+            pltpu.VMEM((tokens, width), bf16),
+            pltpu.VMEM((chips, tokens, part), bf16),
+            pltpu.VMEM((tokens, units), bf16),
+            pltpu.VMEM((tokens, units), bf16),
+            pltpu.VMEM((tokens, local), bf16),
+            pltpu.VMEM((tokens, local), bf16),
+            pltpu.VMEM((units, width), bf16),
+            pltpu.VMEM((tokens, units), bf16),
+            pltpu.VMEM((rows, width), bf16),
+            pltpu.VMEM((chips, part, units), bf16),
+            pltpu.VMEM((chips, part, local), bf16),
+            pltpu.VMEM((6, part, units // 2), bf16),
+            pltpu.VMEM((6, part, local // 2), bf16),
+            pltpu.VMEM((2, tensor - 1, rows, width), bf16),
+            pltpu.SemaphoreType.DMA((sems.count,)),
+            pltpu.SemaphoreType.DMA((sems.count,)),
+            pltpu.SemaphoreType.DMA((12,)),
+        ],
+        compiler_params=pltpu.CompilerParams(
+            collective_id=1, has_side_effects=True, vmem_limit_bytes=VMEM_LIMIT
+        ),
+        name="first_back",
+    )(*arrays)
+
+
+def second_call(dp, tensor, arrays):
+    hidden, cotangent, vec, sums, normed, grad_pre, dq, dk, dv, w_qkv, w_fc1 = arrays
+    rows, width = hidden.shape
+    tokens, units = grad_pre.shape
+    local = dq.shape[1]
+    wide = 3 * local
+    part = width // dp
+    chips = dp // 2
+    sems = Sems()
+    reduce_fc1, reduce_qkv = ChipReduce(sems), ChipReduce(sems)
+    line_in = LineReduce(sems, tensor)
+    swaps = [sems.take() for _ in range(chips + 4)]
+    tells = [sems.take() for _ in range(2 * (dp - 1) + tensor - 1)]
+
+    def kernel(
+        x_ref, c_ref, vec_ref, sum_ref, n_ref, gp_in, dq_in, dk_in, dv_in, wq_ref, w1_ref,
+        hid_ref, s1_out, sq_out, vout_ref, bout_ref,
+        x_buf, c_buf, n_buf, nx_buf, gp, gpx, gq, gqx, wq, w1, gn,
+        s1, sq, r1, rq, rz, parts, tell_v, tell_b, tell_z, send_sem, recv_sem, local_sem,
+    ):
+        me, line = lax.axis_index("dp"), lax.axis_index("tensor")
+        twin = flip(me, 0)
+
+        def cols(a):
+            return pl.ds(pl.multiple_of(a * part, part), part)
+
+        pair = (send_sem, recv_sem)
+        fc1 = reduce_fc1.bind(me, line, s1, r1, *pair)
+        qkv = reduce_qkv.bind(me, line, sq, rq, *pair)
+        ins = line_in.bind(line, me, lambda d: gn.at[pl.ds(d * rows, rows), :], rz, *pair)
+
+        def remote(k, source, target, device):
+            return pltpu.make_async_remote_copy(
+                src_ref=source, dst_ref=target,
+                send_sem=send_sem.at[k], recv_sem=recv_sem.at[k],
+                device_id=device, device_id_type=MESH)
+
+        grads_in = (dq_in, dk_in, dv_in)
+
+        def third(i):
+            return pl.ds(i * local, local)
+
+        crossing = [
+            remote(swaps[r], n_ref.at[:, cols(relative(twin, r << 1))], nx_buf.at[r], (twin, line))
+            for r in range(chips)
+        ] + [remote(swaps[chips], gp_in, gpx, (twin, line))] + [
+            remote(swaps[chips + 1 + i], grads_in[i], gqx.at[:, third(i)], (twin, line))
+            for i in range(3)
+        ]
+        bias_tells = [
+            remote(tells[r - 1], sum_ref, tell_b.at[r], (relative(me, r), line)) for r in range(1, dp)
+        ]
+        vec_tells = [
+            remote(tells[dp - 2 + r], parts.at[:, cols(relative(me, r))], tell_v.at[r],
+                   (relative(me, r), line))
+            for r in range(1, dp)
+        ]
+        line_tells = [
+            remote(tells[2 * dp - 3 + k], tell_z.at[0], tell_z.at[k],
+                   (me, lax.rem(line + k, tensor)))
+            for k in range(1, tensor)
+        ]
+        tile = 512
+        pieces = (
+            [(gp_in, gp)]
+            + [(grads_in[i], gq.at[:, third(i)]) for i in range(3)]
+            + [(w1_ref.at[pl.ds(n, tile), :], w1.at[pl.ds(n, tile), :]) for n in range(0, width, tile)]
+            + [
+                (wq_ref.at[i, pl.ds(n, tile), :], wq.at[pl.ds(n, tile), third(i)])
+                for n in range(0, width, tile) for i in range(3)
+            ]
+            + [(n_ref, n_buf), (x_ref, x_buf), (c_ref, c_buf)]
+        )
+        loads = [pltpu.make_async_copy(a, b, local_sem.at[k]) for k, (a, b) in enumerate(pieces)]
+        tiles = width // tile
+        for copy in loads[:4]:
+            copy.start()
+        for n in range(tiles):
+            loads[4 + n].start()
+            for i in range(3):
+                loads[4 + tiles + 3 * n + i].start()
+        greet(dp, me, tensor, line, wide=True)
+        for copy in loads[4 + 4 * tiles :]:
+            copy.start()
+        for copy in crossing:
+            copy.start()
+        for copy in bias_tells:
+            copy.start()
+        for copy in loads[:4]:
+            copy.wait()
+        for n in range(tiles):
+            loads[4 + n].wait()
+            for i in range(3):
+                loads[4 + tiles + 3 * n + i].wait()
+
+        upper = lax.div(line, tensor // 2)
+
+        @pl.loop(0, tensor)
+        def _(i):
+            d = (1 - upper) * (tensor - 1 - i) + upper * i
+            at = pl.ds(pl.multiple_of(d * rows, rows), rows)
+
+            @pl.loop(0, width, step=1024)
+            def _(n):
+                to = pl.ds(pl.multiple_of(n, 1024), 1024)
+                value = dot_nt(gp[at, :], w1[to, :]) + dot_nt(gq[at, :], wq[to, :])
+                gn[at, to] = value.astype(bf16)
+
+            for k in range(tensor - 1):
+
+                @pl.when(i == k)
+                def _():
+                    ins.start(0, k)
+                    ins.start(1, k)
+
+        loads[4 + 4 * tiles].wait()
+
+        def weight_grad(target, plan, own, crossed, size, step):
+            @pl.loop(0, chips)
+            def _(i):
+                r = chips - 1 - i
+                slot = me + 2 * ((r % 2) * (1 - 2 * (lax.div(me, 2) % 2))) + 4 * (
+                    lax.div(r, 2) * (1 - 2 * (lax.div(me, 4) % 2)))
+
+                @pl.loop(0, size, step=step)
+                def _(n):
+                    at = pl.ds(pl.multiple_of(n, step), step)
+                    value = dot_tn(n_buf[:, cols(slot)], own[:, at])
+                    value = value + dot_tn(nx_buf[r], crossed[:, at])
+                    target[r, :, at] = value.astype(bf16)
+
+                for k in range(1, chips):
+
+                    @pl.when(r == k)
+                    def _():
+                        plan.start(k)
+
+        for copy in crossing:
+            copy.wait_recv()
+        weight_grad(s1, fc1, gp, gpx, units, 1024)
+        ins.advance(1, add_into)
+        weight_grad(sq, qkv, gq, gqx, wide, 768)
+        ins.advance(2, add_into)
+        fc1.middle()
+        for copy in bias_tells:
+            copy.wait_recv()
+        total = sum_ref[...]
+        for r in range(1, dp):
+            total = total + tell_b[r]
+        bout_ref[...] = total
+        for copy in loads[5 + 4 * tiles :]:
+            copy.wait()
+        qkv.middle()
+        ins.arrive()
+        parts[...] = jnp.zeros_like(parts)
+
+        @pl.loop(0, rows, step=32)
+        def _(r):
+            at = pl.ds(r, 32)
+            x = x_buf[at, :].astype(f32)
+            centred = x - jnp.mean(x, -1, keepdims=True)
+            inv_std = lax.rsqrt(jnp.mean(centred * centred, -1, keepdims=True) + layer_eps)
+            unit = centred * inv_std
+            own = pl.ds(pl.multiple_of(line * rows + r, 32), 32)
+            grad = ins.total(gn[own, :], at)
+            cot = c_buf[at, :].astype(f32)
+            scaled = grad * vec_ref[0:1, :]
+            first = jnp.mean(scaled, -1, keepdims=True)
+            second = jnp.mean(scaled * unit, -1, keepdims=True)
+            c_buf[at, :] = (cot + inv_std * (scaled - first - unit * second)).astype(bf16)
+            parts[0:1, :] += jnp.sum(grad * unit, 0, keepdims=True)
+            parts[1:2, :] += jnp.sum(grad, 0, keepdims=True)
+            parts[2:3, :] += jnp.sum(cot, 0, keepdims=True)
+
+        last = pltpu.make_async_copy(c_buf, hid_ref, local_sem.at[len(loads)])
+        last.start()
+        for copy in vec_tells:
+            copy.start()
+        fc1.final()
+        store1 = pltpu.make_async_copy(s1.at[0], s1_out, local_sem.at[len(loads) + 1])
+        store1.start()
+        for copy in vec_tells:
+            copy.wait_recv()
+        total_v = parts[:, cols(me)]
+        for r in range(1, dp):
+            total_v = total_v + tell_v[r]
+        tell_z[0] = total_v
+        for copy in line_tells:
+            copy.start()
+        qkv.final()
+        storeq = pltpu.make_async_copy(sq.at[0], sq_out, local_sem.at[len(loads) + 2])
+        storeq.start()
+        for copy in line_tells:
+            copy.wait_recv()
+        total_z = tell_z[0]
+        for k in range(1, tensor):
+            total_z = total_z + tell_z[k]
+        vout_ref[...] = total_z
+        for copy in crossing + bias_tells + vec_tells + line_tells:
+            copy.wait_send()
+        for plan in (fc1, qkv, ins):
+            plan.finish()
+        for copy in (last, store1, storeq):
+            copy.wait()
+
+    return pl.pallas_call(
+        kernel,
+        out_shape=(
+            jax.ShapeDtypeStruct((rows, width), bf16),
+            jax.ShapeDtypeStruct((part, units), bf16),
+            jax.ShapeDtypeStruct((part, wide), bf16),
+            jax.ShapeDtypeStruct((8, part), f32),
+            jax.ShapeDtypeStruct((8, local), f32),
+        ),
+        in_specs=[ANY] * 2 + [VMEM] * 2 + [ANY] * 7,
+        out_specs=(ANY, ANY, ANY, VMEM, VMEM),
+        scratch_shapes=[
+            pltpu.VMEM((rows, width), bf16),
+            pltpu.VMEM((rows, width), bf16),
+            pltpu.VMEM((tokens, width), bf16),
+            pltpu.VMEM((chips, tokens, part), bf16),
+            pltpu.VMEM((tokens, units), bf16),
+            pltpu.VMEM((tokens, units), bf16),
+            pltpu.VMEM((tokens, wide), bf16),
+            pltpu.VMEM((tokens, wide), bf16),
+            pltpu.VMEM((width, wide), bf16),
+            pltpu.VMEM((width, units), bf16),
+            pltpu.VMEM((tokens, width), bf16),
+            pltpu.VMEM((chips, part, units), bf16),
+            pltpu.VMEM((chips, part, wide), bf16),
+            pltpu.VMEM((6, part, units // 2), bf16),
+            pltpu.VMEM((6, part, wide // 2), bf16),
+            pltpu.VMEM((2, tensor - 1, rows, width), bf16),
+            pltpu.VMEM((8, width), f32),
+            pltpu.VMEM((dp, 8, part), f32),
+            pltpu.VMEM((dp, 8, local), f32),
+            pltpu.VMEM((tensor, 8, part), f32),
+            pltpu.SemaphoreType.DMA((sems.count,)),
+            pltpu.SemaphoreType.DMA((sems.count,)),
+            pltpu.SemaphoreType.DMA((30,)),
+        ],
+        compiler_params=pltpu.CompilerParams(
+            collective_id=2, has_side_effects=True, vmem_limit_bytes=VMEM_LIMIT
+        ),
+        name="second_back",
+    )(*arrays)
 
 
 def spans_of(length):
@@ -595,13 +1187,6 @@
     gathered = gather_call(dp, tensor, *mine) if fast else gather_plain(*mine)
     w_qkv, w_dense, w_fc1, w_fc2, normed, grad_out, vec = gathered
     gain, out_bias = vec[0:1], vec[2:3]
-    resid_in = hidden_in.astype(f32)
-    cot_float = cotangent.astype(f32)
-    centred = resid_in - jnp.mean(resid_in, -1, keepdims=True)
-    spread = jnp.mean(centred * centred, -1, keepdims=True)
-    inv_std = lax.rsqrt(spread + layer_eps)
-    unit_rows = centred * inv_std
-
     tables = rotary_tables(segments)
     bias = jnp.pad(qkv_bias.astype(f32), ((0, 5), (0, 0)))
     query, key, value, attn_vec, probs = attend(
@@ -610,18 +1195,50 @@
     pre_act = matmul(normed, w_fc1) + fc1_bias.astype(f32)
     act_vals, gelu_pull = jax.vjp(lambda pre: jax.nn.gelu(pre, approximate=True), pre_act)
     act_vals = act_vals.astype(bf16)
+    slope = gelu_pull(jnp.ones_like(pre_act))[0].astype(bf16)
     branches = matmul(attn_vec, w_dense) + matmul(act_vals, w_fc2)
+    grad_attn = matmul(grad_out, w_dense.T).astype(bf16)
+    *grads, qkv_sums = attend_back(query, key, value, grad_attn, attn_vec, probs, tables, seqs)
+    if fast:
+        out, grad_pre, fc1_sums, sent_fc2, sent_dense = first_call(
+            dp, tensor,
+            (hidden_in, vec, branches.astype(bf16), grad_out, act_vals, slope, attn_vec, w_fc2))
+        sums = jnp.concatenate([fc1_sums[0].reshape(4, local), qkv_sums[:3], jnp.zeros((1, local), f32)], 0)
+        hidden_grad, sent_fc1, sent_qkv, vec_sums, all_sums = second_call(
+            dp, tensor,
+            (hidden_in, cotangent, vec, sums, normed, grad_pre, *grads, w_qkv, w_fc1))
+        quarter = vec_sums.shape[1] // tensor
+        at = lax.axis_index("tensor") * quarter
+        small = lax.dynamic_slice(vec_sums, (0, at), (3, quarter))
+        return (
+            out,
+            hidden_grad,
+            small[0],
+            small[1],
+            sent_qkv.astype(f32).reshape(-1, 3, local),
+            all_sums[4:7],
+            sent_dense.T.astype(f32),
+            small[2],
+            sent_fc1.astype(f32),
+            all_sums[:4].reshape(-1),
+            sent_fc2.T.astype(f32),
+            small[2],
+        )
+
+    resid_in = hidden_in.astype(f32)
+    cot_float = cotangent.astype(f32)
+    centred = resid_in - jnp.mean(resid_in, -1, keepdims=True)
+    spread = jnp.mean(centred * centred, -1, keepdims=True)
+    inv_std = lax.rsqrt(spread + layer_eps)
+    unit_rows = centred * inv_std
     summed = lax.psum_scatter(branches.astype(bf16), "tensor", scatter_dimension=0, tiled=True)
     out = (resid_in + summed.astype(f32) + out_bias).astype(bf16)
-
     out_bias_part = jnp.sum(cot_float, 0)
     grad_fc2 = matmul(act_vals.T, grad_out)
     grad_dense = matmul(attn_vec.T, grad_out)
-    grad_pre = gelu_pull(matmul(grad_out, w_fc2.T))[0].astype(bf16)
+    grad_pre = (matmul(grad_out, w_fc2.T) * slope.astype(f32)).astype(bf16)
     fc1_bias_part = jnp.sum(grad_pre.astype(f32), 0)
     grad_fc1 = matmul(normed.T, grad_pre)
-    grad_attn = matmul(grad_out, w_dense.T).astype(bf16)
-    *grads, qkv_bias_part = attend_back(query, key, value, grad_attn, attn_vec, probs, tables, seqs)
     grad_wqkv = jnp.stack([matmul(normed.T, g) for g in grads])
     grad_normed = matmul(grad_pre, w_fc1.T) + sum(matmul(g, w.T) for g, w in zip(grads, w_qkv))
     sent_qkv, sent_dense, sent_fc1, sent_fc2 = (
@@ -646,7 +1263,7 @@
         lax.psum_scatter(beta_part, ("dp", "tensor"), scatter_dimension=0, tiled=True),
         lax.psum_scatter(out_bias_part, ("dp", "tensor"), scatter_dimension=0, tiled=True),
     )
-    qkv_bias_grad, fc1_bias_grad = lax.psum((qkv_bias_part[:3], fc1_bias_part), "dp")
+    qkv_bias_grad, fc1_bias_grad = lax.psum((qkv_sums[:3], fc1_bias_part), "dp")
     return (
         out,
         hidden_grad,

time: 707 us -> 477 us (0.67)
  waiting for transfers between devices: 224 us -> 0 us
  Pallas kernels: 202 us -> 385 us
  matrix products: 158 us -> 56.2 us
  blocking collectives: 65.5 us -> 0 us
  other arithmetic: 29.1 us -> 12.8 us
  between operations: 14.6 us -> 1.27 us
  local copies, waits for them, and re-layouts: 4.45 us -> 13.6 us
    reduce_scatter x6 -> x0, waiting for transfers between devices: 224 us -> none  [the longest x1 72.3 us: on_device(): lax.psum_scatter(grad_fc1.astype(bf16), 'dp', scatter_dimension=0, tiled=...]
    pallas_call x0 -> x2, Pallas kernels: none -> 184 us  [the longest x1 94.6 us: second_call(): pl.pallas_call(kernel, out_shape=(jax.ShapeDtypeStruct((rows, width), bf1...]
    dot_general x18 -> x7, matrix products: 158 us -> 56.2 us  [matmul(): return jnp.dot(a, b, preferred_element_type=f32)]
    unnamed x1 -> x0, blocking collectives: 41.5 us -> none
    psum x1 -> x0, blocking collectives: 24 us -> none  [on_device(): lax.psum((qkv_bias_part[:3], fc1_bias_part), 'dp')]
    reduce_sum x4 -> x0, other arithmetic: 7.19 us -> none  [the longest x1 4.28 us: on_device(): out_bias_part = jnp.sum(cot_float, 0)]
  transfers between devices with their start and end apart: 6 -> 0, of which waited for: 4 -> 0; matrix products, arithmetic and copies ran while one was open for 23% -> 0% of each run, Pallas kernels for 3% -> 0%
where the time goes in v2:
time: 477 us; the launch traced here: 469 us
  Pallas kernels  385 us (81%)
  matrix products  56.2 us (12%)
  local copies, waits for them, and re-layouts  13.6 us (3%)
  other arithmetic  12.8 us (3%)
    pallas_call x1, Pallas kernels, gather_call(): pl.pallas_call(kernel, out_shape=(jax.ShapeDtypeStruct((3, width, local),...  164 us
    pallas_call x1, Pallas kernels, second_call(): pl.pallas_call(kernel, out_shape=(jax.ShapeDtypeStruct((rows, width), bf1...  94.6 us
    pallas_call x1, Pallas kernels, first_call(): pl.pallas_call(kernel, out_shape=(jax.ShapeDtypeStruct((rows, width), bf1...  89.6 us
    dot_general x7, matrix products, matmul(): return jnp.dot(a, b, preferred_element_type=f32)  56.2 us
    pallas_call x1, Pallas kernels, attend_back(): pl.pallas_call(attend_back_kernel, grid=(pairs, rows), out_shape=(shape,)...  18.7 us
    pallas_call x1, Pallas kernels, attend(): pl.pallas_call(attend_kernel, grid=(rows, pairs), out_shape=(shape,) * 4...  17.9 us

profile of v2, /device:TPU:0, one launch (start us, length us, event | category | flops | bytes accessed | tf_op | source)
XLA Modules:
  0.0 468.9 jit_solution(486814362337129082)
XLA Ops:
  3.2 164.3 %gather.1 = (bf16[3,2048,512]{2,1,0:T(8,128)(2,1)}, bf16[512,2048]{1,0:T(8,128)(2,1)}, bf16[2048,2048]{1,0:T(8,128)(2,1)}, bf16[2048,2048]{1,0:T(8,128)(2,1)}, b...) custom-call(bf16[256,2048]{1,0:T(8,128)(2,1)} %x_ref.5, bf16[256,2048]{1,0:T(8,128)(2,1)} %c_ref.3, ...), custom_call_target="tpu_custom_call" | custom-call | tf_op jit(solution)/shard_map/gather/pallas_call | solution.py:351
  167.6 6.7 %fusion.7.v_ref = f32[1024,512]{1,0:T(8,128)} fusion(bf16[1024,2048]{1,0:T(8,128)(2,1)} %get-tuple-element.39.n_ref, bf16[3,2048,512]{2,1,0:T(8,128)(2,1)} %get-tuple-element.40.wq_ref), kind=kOutput, calls=%fused_computation.11 | convolution fusion | flops 2147483648 | bytes 8388608 | tf_op jit(solution)/shard_map/dot_general | solution.py:1171
  174.2 3.6 fusion.9.k_ref
  177.9 3.7 fusion.11.q_ref
  182.2 2.0 fusion.24
  184.2 3.2 fusion.16
  187.4 1.1 copy.28.segc_ref
  189.1 17.9 %attend.1 = (bf16[1024,512]{1,0:T(8,128)(2,1)}, bf16[1024,512]{1,0:T(8,128)(2,1)}, bf16[1024,512]{1,0:T(8,128)(2,1)}, bf16[1024,512]{1,0:T(8,128)(2,1)}, bf16[1,8,2304,256]{3,2,1,0:T(8,128)(2,1)}) custom-call(f32[1024,512]{1,0:T(8,128)} %fusion.11.q_ref, f32[1024,512]{1,0:T(8,128)} %fusion.9.k_ref, f32[1024,512]{1,0:T(8,128)} %fusion.7.v_ref, ...), custom_call_target="tpu_custom_call" | custom-call | flops 6442450944 | bytes 25165824 | tf_op jit(solution)/shard_map/attend/pallas_call | solution.py:1048
  207.0 6.2 %convolution_convert_fusion.g_ref = bf16[1024,512]{1,0:T(8,128)(2,1)} fusion(bf16[1024,2048]{1,0:T(8,128)(2,1)} %get-tuple-element.45.c_ref, bf16[512,2048]{1,0:T(8,128)(2,1)} %get-tuple-element.42), kind=kOutput, calls=%fused_computation.21 | convolution fusion | flops 2148007936 | bytes 7340032 | tf_op jit(solution)/shard_map/dot_general | solution.py:1171
  213.2 18.7 %attend_back.1 = (bf16[1024,512]{1,0:T(8,128)(2,1)}, bf16[1024,512]{1,0:T(8,128)(2,1)}, bf16[1024,512]{1,0:T(8,128)(2,1)}, f32[8,512]{1,0:T(8,128)}) custom-call(bf16[1024,512]{1,0:T(8,128)(2,1)} %get-tuple-element.48.q_ref, bf16[1024,512]{1,0:T(8,128)(2,1)} %get-tuple-element.49.k_ref, bf16[1024,512]{1,0:T(8,128)(2,1)} %get-tuple-element.50.v_ref, ...), custom_call_target="tpu_custom_call" | custom-call | flops 12884901888 | bytes 25165824 | tf_op jit(solution)/shard_map/attend_back/pallas_call | solution.py:1134
  232.6 18.5 %fusion.6 = (bf16[1024,2048]{1,0:T(8,128)(2,1)}, bf16[1024,2048]{1,0:T(8,128)(2,1)S(1)}) fusion(f32[2048]{0:T(1024)S(1)} %convert_element_type.70, bf16[1024,2048]{1,0:T(8,128)(2,1)} %get-tuple-element.39.n_ref, bf16[2048,2048]{1,0:T(8,128)(2,1)} %get-tuple-element.43.w1_ref), kind=kOutput, calls=%fused_computation.8 | convolution fusion | flops 8633974784 | bytes 20979712 | tf_op jit(solution)/shard_map/dot_general | solution.py:1171
  251.1 13.1 %fusion.31 = f32[1024,2048]{1,0:T(8,128)S(1)} fusion(bf16[1024,2048]{1,0:T(8,128)(2,1)S(1)} %get-tuple-element.92.a_ref, bf16[2048,2048]{1,0:T(8,128)(2,1)} %get-tuple-element.44.w2_ref), kind=kOutput, calls=%fused_computation.65 | convolution fusion | flops 8589934592 | bytes 20971520 | tf_op jit(solution)/shard_map/dot_general | solution.py:1171
  264.2 4.4 add_convert_fusion.b_ref
  268.6 89.6 %first_back.1 = (bf16[256,2048]{1,0:T(8,128)(2,1)}, bf16[1024,2048]{1,0:T(8,128)(2,1)}, f32[8,2048]{1,0:T(8,128)}, bf16[256,2048]{1,0:T(8,128)(2,1)}, bf16[256,512]{1,0:T(8,128)(2,1)}) custom-call(bf16[256,2048]{1,0:T(8,128)(2,1)} %x_ref.5, f32[8,2048]{1,0:T(8,128)} %get-tuple-element.38.vec_ref, bf16[1024,2048]{1,0:T(8,128)(2,1)} %add_convert_fusion.b_ref, ...), custom_call_target="tpu_custom_call" | custom-call | tf_op jit(solution)/shard_map/first_back/pallas_call | solution.py:695
  358.2 0.9 slice_reduce_fusion
  359.9 94.6 %second_back.1 = (bf16[256,2048]{1,0:T(8,128)(2,1)}, bf16[256,2048]{1,0:T(8,128)(2,1)}, bf16[256,1536]{1,0:T(8,128)(2,1)}, f32[8,256]{1,0:T(8,128)}, f32[8,512]{1,0:T(8,128)}) custom-call(bf16[256,2048]{1,0:T(8,128)(2,1)} %x_ref.5, bf16[256,2048]{1,0:T(8,128)(2,1)} %c_ref.3, f32[8,2048]{1,0:T(8,128)} %get-tuple-element.38.vec_ref, ...), custom_call_target="tpu_custom_call" | custom-call | tf_op jit(solution)/shard_map/second_back/pallas_call | solution.py:938
  454.4 1.5 copy.29
  455.9 1.6 copy.30
  457.6 2.8 convert_element_type.77
  461.0 0.7 constant_dynamic-slice_fusion
  463.1 1.8 copy.32
  465.0 1.0 copy.31
  466.5 1.0 copy.38
  467.4 1.0 copy.39
  (49 shorter events, 8.0 us)
Async XLA Ops:
  167.5 6.7 %copy-start = (bf16[3,2048,512]{2,1,0:T(8,128)(2,1)S(1)}, bf16[3,2048,512]{2,1,0:T(8,128)(2,1)}, u32[]{:S(2)}) copy-start(bf16[3,2048,512]{2,1,0:T(8,128)(2,1)} %get-tuple-element.40.wq_ref) | copy-start | bytes 18874372
  167.5 6.7 %copy-start.1 = (bf16[1024,2048]{1,0:T(8,128)(2,1)S(1)}, bf16[1024,2048]{1,0:T(8,128)(2,1)}, u32[]{:S(2)}) copy-start(bf16[1024,2048]{1,0:T(8,128)(2,1)} %get-tuple-element.39.n_ref) | copy-start | bytes 12582916
  177.9 3.7 copy-start.8
  177.9 10.6 %copy-start.10 = (bf16[3,512]{1,0:T(4,128)(2,1)S(1)}, bf16[3,512]{1,0:T(4,128)(2,1)}, u32[]{:S(2)}) copy-start(bf16[3,512]{1,0:T(4,128)(2,1)} %param.18) | copy-start | bytes 9220
  213.2 19.4 %copy-start.11 = (bf16[2048]{0:T(1024)(128)(2,1)S(1)}, bf16[2048]{0:T(1024)(128)(2,1)}, u32[]{:S(2)}) copy-start(bf16[2048]{0:T(1024)(128)(2,1)} %param.22) | copy-start | bytes 12292
  251.1 13.1 %copy-start.2 = (bf16[1024,2048]{1,0:T(8,128)(2,1)}, bf16[1024,2048]{1,0:T(8,128)(2,1)S(1)}, u32[]{:S(2)}) copy-start(bf16[1024,2048]{1,0:T(8,128)(2,1)S(1)} %get-tuple-element.92.a_ref) | copy-start | bytes 12582916
  251.1 13.1 %copy-start.6 = (bf16[1024,512]{1,0:T(8,128)(2,1)S(1)}, bf16[1024,512]{1,0:T(8,128)(2,1)}, u32[]{:S(2)}) copy-start(bf16[1024,512]{1,0:T(8,128)(2,1)} %get-tuple-element.41.t_ref.o_ref) | copy-start | bytes 3145732
  251.1 13.1 %copy-start.13 = (bf16[512,2048]{1,0:T(8,128)(2,1)S(1)}, bf16[512,2048]{1,0:T(8,128)(2,1)}, u32[]{:S(2)}) copy-start(bf16[512,2048]{1,0:T(8,128)(2,1)} %get-tuple-element.42) | copy-start | bytes 6291460
  454.4 5.9 %copy-start.9 = (f32[8,512]{1,0:T(8,128)S(1)}, f32[8,512]{1,0:T(8,128)}, u32[]{:S(2)}) copy-start(f32[8,512]{1,0:T(8,128)} %get-tuple-element.60) | copy-start | bytes 49156
  454.4 8.4 %copy-start.3 = (bf16[256,2048]{1,0:T(8,128)(2,1)S(1)}, bf16[256,2048]{1,0:T(8,128)(2,1)}, u32[]{:S(2)}) copy-start(bf16[256,2048]{1,0:T(8,128)(2,1)} %get-tuple-element.63) | copy-start | bytes 3145732
  460.3 4.5 copy-start.7
  462.2 3.7 copy-start.12
  463.1 3.4 copy-start.4
  464.9 2.6 copy-start.5

commit v3 on v2

--- a/solution.py
+++ b/solution.py
@@ -214,168 +214,6 @@
     return [bits + [0], bits[::-1] + [0]]
 
 
-def gather_call(dp, tensor, hidden, cotangent, w_qkv, w_dense, w_fc1, w_fc2, vectors):
-    rows, width = hidden.shape
-    local = w_qkv.shape[2]
-    hidden_units = w_fc1.shape[1]
-    part = width // dp
-    sems = Sems()
-    orders = orders_of(dp)
-    plan_vec = CubeGather(sems, orders[:1])
-    plan_qkv, plan_dense, plan_fc1, plan_fc2 = (CubeGather(sems, orders) for _ in range(4))
-    plan_n, plan_c = LineGather(sems, tensor, 2), LineGather(sems, tensor, 2)
-
-    def kernel(
-        x_ref, c_ref, wq_ref, wd_ref, w1_ref, w2_ref, vec_ref,
-        gq_ref, gd_ref, g1_ref, g2_ref, gn_ref, gc_ref, gvec_ref,
-        x_buf, n_buf, vec_buf, send_sem, recv_sem, local_sem,
-    ):
-        me, line = lax.axis_index("dp"), lax.axis_index("tensor")
-        half = part // 2
-
-        def cols(a):
-            return pl.ds(pl.multiple_of(a * part, part), part)
-
-        def half_rows(a, h):
-            return pl.ds(pl.multiple_of(a * part + h * half, half), half)
-
-        def tok(b, u):
-            return pl.ds(pl.multiple_of(b * rows + u * (rows // 2), rows // 2), rows // 2)
-
-        def sub(u):
-            return pl.ds(u * (rows // 2), rows // 2)
-
-        def piece(n, h):
-            return pl.ds(h * (n // 2), n // 2)
-
-        pair = (send_sem, recv_sem)
-        vec = plan_vec.bind(me, line, lambda h: vec_ref, lambda a, h: vec_buf.at[:, cols(a)], *pair)
-        qkv = plan_qkv.bind(
-            me, line,
-            lambda h: wq_ref.at[:, pl.ds(h * half, half), :],
-            lambda a, h: gq_ref.at[:, half_rows(a, h), :], *pair)
-        fc1 = plan_fc1.bind(
-            me, line,
-            lambda h: w1_ref.at[pl.ds(h * half, half), :],
-            lambda a, h: g1_ref.at[half_rows(a, h), :], *pair)
-        dense = plan_dense.bind(
-            me, line,
-            lambda h: wd_ref.at[piece(local, h), :],
-            lambda a, h: gd_ref.at[piece(local, h), cols(a)], *pair)
-        fc2 = plan_fc2.bind(
-            me, line,
-            lambda h: w2_ref.at[piece(hidden_units, h), :],
-            lambda a, h: g2_ref.at[piece(hidden_units, h), cols(a)], *pair)
-        norm = plan_n.bind(
-            line, me, lambda u: n_buf.at[sub(u)], lambda b, u: gn_ref.at[tok(b, u)], *pair)
-        cot = plan_c.bind(
-            line, me, lambda u: c_ref.at[sub(u)], lambda b, u: gc_ref.at[tok(b, u)], *pair)
-
-        keep = [
-            (x_ref, x_buf),
-            (vec_ref, vec_buf.at[:, cols(me)]),
-            (wq_ref, gq_ref.at[:, pl.ds(pl.multiple_of(me * part, part), part), :]),
-            (w1_ref, g1_ref.at[pl.ds(pl.multiple_of(me * part, part), part), :]),
-            (wd_ref, gd_ref.at[:, cols(me)]),
-            (w2_ref, g2_ref.at[:, cols(me)]),
-            (c_ref, gc_ref.at[pl.ds(pl.multiple_of(line * rows, rows), rows), :]),
-        ]
-        keeps = [
-            pltpu.make_async_copy(a, b, local_sem.at[k]) for k, (a, b) in enumerate(keep)
-        ]
-        keeps[0].start()
-        greet(dp, me, tensor, line)
-        vec.start()
-        qkv.start()
-        for copy in keeps[1:]:
-            copy.start()
-        stages = dp.bit_length() - 1
-        for j in range(stages):
-            vec.advance(j)
-        keeps[0].wait()
-        keeps[1].wait()
-
-        @pl.loop(0, rows, step=32)
-        def _(r):
-            x = x_buf[pl.ds(r, 32), :].astype(f32)
-            centred = x - jnp.mean(x, -1, keepdims=True)
-            spread = jnp.mean(centred * centred, -1, keepdims=True)
-            unit = centred * lax.rsqrt(spread + layer_eps)
-            n_buf[pl.ds(r, 32), :] = (unit * vec_buf[0:1, :] + vec_buf[1:2, :]).astype(bf16)
-
-        norm.start(0)
-        norm.start(1)
-        own_n = pltpu.make_async_copy(
-            n_buf, gn_ref.at[pl.ds(pl.multiple_of(line * rows, rows), rows), :], local_sem.at[len(keep)])
-        own_n.start()
-        gvec_ref[...] = vec_buf[...]
-        qkv.advance(0)
-        fc1.start()
-        norm.advance(0, 0)
-        for j in range(1, stages - 1):
-            qkv.advance(j)
-        norm.advance(0, 1)
-        fc1.advance(0)
-        dense.start()
-        fc2.start()
-        qkv.advance(stages - 1)
-        norm.advance(1, 0)
-        norm.advance(1, 1)
-        cot.start(0)
-        cot.start(1)
-        for j in range(1, stages - 1):
-            fc1.advance(j)
-        dense.advance(0)
-        norm.advance(2, 0)
-        norm.advance(2, 1)
-        fc1.advance(stages - 1)
-        fc2.advance(0)
-        cot.advance(0, 0)
-        for j in range(1, stages - 1):
-            dense.advance(j)
-        cot.advance(0, 1)
-        for j in range(1, stages - 1):
-            fc2.advance(j)
-        dense.advance(stages - 1)
-        fc2.advance(stages - 1)
-        for s in (1, 2):
-            for u in (0, 1):
-                cot.advance(s, u)
-        for copy in keeps[2:]:
-            copy.wait()
-        own_n.wait()
-        for plan in (vec, qkv, fc1, dense, fc2, norm, cot):
-            plan.finish()
-
-    tokens = rows * tensor
-    return pl.pallas_call(
-        kernel,
-        out_shape=(
-            jax.ShapeDtypeStruct((3, width, local), bf16),
-            jax.ShapeDtypeStruct((local, width), bf16),
-            jax.ShapeDtypeStruct((width, hidden_units), bf16),
-            jax.ShapeDtypeStruct((hidden_units, width), bf16),
-            jax.ShapeDtypeStruct((tokens, width), bf16),
-            jax.ShapeDtypeStruct((tokens, width), bf16),
-            jax.ShapeDtypeStruct((8, width), f32),
-        ),
-        in_specs=[ANY] * 7,
-        out_specs=(ANY,) * 6 + (VMEM,),
-        scratch_shapes=[
-            pltpu.VMEM((rows, width), bf16),
-            pltpu.VMEM((rows, width), bf16),
-            pltpu.VMEM((8, width), f32),
-            pltpu.SemaphoreType.DMA((sems.count,)),
-            pltpu.SemaphoreType.DMA((sems.count,)),
-            pltpu.SemaphoreType.DMA((8,)),
-        ],
-        compiler_params=pltpu.CompilerParams(
-            collective_id=0, has_side_effects=True, vmem_limit_bytes=VMEM_LIMIT
-        ),
-        name="gather",
-    )(hidden, cotangent, w_qkv, w_dense, w_fc1, w_fc2, vectors)
-
-
 def normalize(x, gain, bias):
     centred = x - jnp.mean(x, -1, keepdims=True)
     spread = jnp.mean(centred * centred, -1, keepdims=True)
@@ -462,9 +300,12 @@
     def target(self, way, i):
         return self.size - 1 - i if way == 0 else i
 
+    def place(self, way, i):
+        return i if way == 0 else 2 * self.size - 4 - i
+
     def copy(self, way, i, edge):
         k = self.ids[way, i]
-        here = self.landing.at[way, i]
+        here = self.landing.at[self.place(way, i)]
         return pltpu.make_async_remote_copy(
             src_ref=self.own(self.target(way, i)) if edge else here,
             dst_ref=here,
@@ -494,7 +335,7 @@
                 @pl.when(self.passes(way, i) & (steps_from_edge == step - i))
                 def _():
                     self.copy(way, i, False).wait_recv()
-                    add(self.landing.at[way, i], self.own(self.target(way, i)))
+                    add(self.landing.at[self.place(way, i)], self.own(self.target(way, i)))
                     self.copy(way, i, False).start()
 
     def arrive(self):
@@ -521,8 +362,8 @@
         value = own.astype(f32)
         lefts = jnp.clip(last - self.me, 0, last - 1)
         rights = jnp.clip(self.me, 0, last - 1)
-        from_left = self.landing[0, lefts, rows, :].astype(f32)
-        from_right = self.landing[1, rights, rows, :].astype(f32)
+        from_left = self.landing[lefts, rows, :].astype(f32)
+        from_right = self.landing[2 * self.size - 4 - rights, rows, :].astype(f32)
         value = value + jnp.where(self.me > 0, from_left, 0.0)
         return value + jnp.where(self.me < last, from_right, 0.0)
 
@@ -536,175 +377,119 @@
         landing[at, :] = (landing[at, :].astype(f32) + own[at, :].astype(f32)).astype(bf16)
 
 
+def chip_slot(me, r):
+    return (
+        me
+        + 2 * ((r % 2) * (1 - 2 * (lax.div(me, 2) % 2)))
+        + 4 * (lax.div(r, 2) * (1 - 2 * (lax.div(me, 4) % 2)))
+    )
+
+
 def first_call(dp, tensor, arrays):
-    hidden, vec, branches, grad_out, act, slope, attn, w_fc2 = arrays
-    rows, width = hidden.shape
-    tokens, units = act.shape
+    grad_out, crossed_out, act, crossed_act, slope, attn, crossed_attn, w_fc2 = arrays
+    tokens, width = grad_out.shape
+    units = act.shape[1]
     local = attn.shape[1]
     part = width // dp
     chips = dp // 2
     sems = Sems()
     reduce_fc2, reduce_dense = ChipReduce(sems), ChipReduce(sems)
-    line_out = LineReduce(sems, tensor)
-    swaps = [sems.take() for _ in range(chips + 2)]
+    swap_at = sems.take()
 
     def kernel(
-        x_ref, vec_ref, b_ref, c_ref, a_ref, d_ref, t_ref, w2_ref,
-        out_ref, gp_ref, sum_ref, s2_out, sd_out,
-        x_buf, c_buf, cx_buf, a_buf, ax_buf, t_buf, tx_buf, w2_buf, d_buf, own_buf,
-        s2, sd, r2, rd, rz, send_sem, recv_sem, local_sem,
+        c_ref, cx_ref, a_ref, ax_ref, d_ref, t_ref, tx_ref, w2_ref,
+        gp_ref, gpx_ref, sum_ref, s2_out, sd_out,
+        c_buf, cx_buf, a_buf, ax_buf, t_buf, tx_buf, w2_buf, d_buf,
+        s2, sd, r2, rd, send_sem, recv_sem, local_sem,
     ):
         me, line = lax.axis_index("dp"), lax.axis_index("tensor")
-        twin = flip(me, 0)
 
         def cols(a):
             return pl.ds(pl.multiple_of(a * part, part), part)
-
-        def block(d):
-            return pl.ds(pl.multiple_of(d * rows, rows), rows)
 
         pair = (send_sem, recv_sem)
         fc2 = reduce_fc2.bind(me, line, s2, r2, *pair)
         dense = reduce_dense.bind(me, line, sd, rd, *pair)
-        outs = line_out.bind(line, me, lambda d: b_ref.at[pl.ds(d * rows, rows), :], rz, *pair)
-
-        def swap(k, source, target):
-            return pltpu.make_async_remote_copy(
-                src_ref=source, dst_ref=target,
-                send_sem=send_sem.at[swaps[k]], recv_sem=recv_sem.at[swaps[k]],
-                device_id=(twin, line), device_id_type=MESH)
-
-        crossing = [
-            swap(r, c_ref.at[:, cols(relative(twin, r << 1))], cx_buf.at[r]) for r in range(chips)
-        ] + [swap(chips, a_ref, ax_buf), swap(chips + 1, t_ref, tx_buf)]
         loads = [
             pltpu.make_async_copy(a, b, local_sem.at[k])
             for k, (a, b) in enumerate([
-                (c_ref, c_buf), (a_ref, a_buf), (t_ref, t_buf), (w2_ref, w2_buf), (d_ref, d_buf),
-                (x_ref, x_buf), (b_ref.at[block(line), :], own_buf),
+                (c_ref, c_buf), (cx_ref, cx_buf), (a_ref, a_buf), (ax_ref, ax_buf),
+                (t_ref, t_buf), (tx_ref, tx_buf), (w2_ref, w2_buf), (d_ref, d_buf),
             ])
         ]
-        loads[0].start()
-        loads[1].start()
+        for copy in loads:
+            copy.start()
         greet(dp, me, tensor, line)
-        for copy in (crossing[3], crossing[chips]):
-            copy.start()
-        for i in range(tensor - 1):
-            outs.start(0, i)
-            outs.start(1, i)
-        for copy in crossing[:3] + crossing[chips + 1 :]:
-            copy.start()
-        for copy in loads[2:]:
-            copy.start()
-        loads[0].wait()
-        loads[1].wait()
-        crossing[chips].wait_recv()
-
-        @pl.loop(0, chips)
-        def _(i):
-            r = chips - 1 - i
-            slot = me + 2 * ((r % 2) * (1 - 2 * (lax.div(me, 2) % 2))) + 4 * (
-                lax.div(r, 2) * (1 - 2 * (lax.div(me, 4) % 2)))
-            for k in range(chips):
-
-                @pl.when(r == k)
-                def _():
-                    crossing[k].wait_recv()
-
-            @pl.loop(0, units, step=1024)
-            def _(n):
-                at = pl.ds(pl.multiple_of(n, 1024), 1024)
-                value = dot_tn(c_buf[:, cols(slot)], a_buf[:, at])
-                value = value + dot_tn(cx_buf[r], ax_buf[:, at])
-                s2[r, :, at] = value.astype(bf16)
-
-            for k in range(1, chips):
-
-                @pl.when(r == k)
-                def _():
-                    fc2.start(k)
-
-        loads[2].wait()
-        crossing[chips + 1].wait_recv()
-
-        @pl.loop(0, chips)
-        def _(i):
-            r = chips - 1 - i
-            slot = me + 2 * ((r % 2) * (1 - 2 * (lax.div(me, 2) % 2))) + 4 * (
-                lax.div(r, 2) * (1 - 2 * (lax.div(me, 4) % 2)))
-            value = dot_tn(c_buf[:, cols(slot)], t_buf[...]) + dot_tn(cx_buf[r], tx_buf[...])
-            sd[r] = value.astype(bf16)
-            for k in range(1, chips):
-
-                @pl.when(r == k)
-                def _():
-                    dense.start(k)
-
-        loads[3].wait()
-        loads[4].wait()
-
-        def slope_tile(n):
+        for copy in loads[:4]:
+            copy.wait()
+
+        def weight_grad(target, plan, own, crossed, size, step):
+            @pl.loop(0, chips)
+            def _(i):
+                r = chips - 1 - i
+                slot = chip_slot(me, r)
+
+                @pl.loop(0, size, step=step)
+                def _(n):
+                    at = pl.ds(pl.multiple_of(n, step), step)
+                    value = dot_tn(c_buf[:, cols(slot)], own[:, at])
+                    value = value + dot_tn(cx_buf[r], crossed[:, at])
+                    target[r, :, at] = value.astype(bf16)
+
+                for k in range(1, chips):
+
+                    @pl.when(r == k)
+                    def _():
+                        plan.start(k)
+
+        weight_grad(s2, fc2, a_buf, ax_buf, units, 1024)
+        for copy in loads[4:6]:
+            copy.wait()
+        weight_grad(sd, dense, t_buf, tx_buf, local, local)
+        for copy in loads[6:]:
+            copy.wait()
+
+        @pl.loop(0, units, step=512)
+        def _(n):
             at = pl.ds(pl.multiple_of(n, 512), 512)
             value = dot_nt(c_buf[...], w2_buf[at, :]) * d_buf[:, at].astype(f32)
             value = value.astype(bf16)
             d_buf[:, at] = value
             sum_ref[0:1, at] = jnp.sum(value.astype(f32), 0, keepdims=True)
 
-        @pl.loop(0, units, step=512)
-        def _(n):
-            slope_tile(n)
-
         store = pltpu.make_async_copy(d_buf, gp_ref, local_sem.at[len(loads)])
         store.start()
-
-        def add_out(landing, own):
-            copy = pltpu.make_async_copy(own, a_buf.at[pl.ds(0, rows), :], local_sem.at[len(loads) + 1])
-            copy.start()
-            copy.wait()
-            add_into(landing, a_buf.at[pl.ds(0, rows), :])
-
-        outs.advance(1, add_out)
+        cross = pltpu.make_async_remote_copy(
+            src_ref=d_buf, dst_ref=gpx_ref,
+            send_sem=send_sem.at[swap_at], recv_sem=recv_sem.at[swap_at],
+            device_id=(flip(me, 0), line), device_id_type=MESH)
+        cross.start()
         fc2.middle()
-        outs.advance(2, add_out)
         dense.middle()
         fc2.final()
         dense.final()
-        store2 = pltpu.make_async_copy(s2.at[0], s2_out, local_sem.at[len(loads) + 2])
-        stored = pltpu.make_async_copy(sd.at[0], sd_out, local_sem.at[len(loads) + 3])
+        store2 = pltpu.make_async_copy(s2.at[0], s2_out, local_sem.at[len(loads) + 1])
+        stored = pltpu.make_async_copy(sd.at[0], sd_out, local_sem.at[len(loads) + 2])
         store2.start()
         stored.start()
-        for copy in loads[5:]:
-            copy.wait()
-        outs.arrive()
-
-        @pl.loop(0, rows, step=32)
-        def _(r):
-            at = pl.ds(r, 32)
-            total = x_buf[at, :].astype(f32) + outs.total(own_buf[at, :], at) + vec_ref[2:3, :]
-            x_buf[at, :] = total.astype(bf16)
-
-        last = pltpu.make_async_copy(x_buf, out_ref, local_sem.at[len(loads) + 4])
-        last.start()
-        for copy in crossing:
-            copy.wait_send()
-        for plan in (fc2, dense, outs):
+        cross.wait()
+        for plan in (fc2, dense):
             plan.finish()
-        for copy in (store, store2, stored, last):
+        for copy in (store, store2, stored):
             copy.wait()
 
     return pl.pallas_call(
         kernel,
         out_shape=(
-            jax.ShapeDtypeStruct((rows, width), bf16),
+            jax.ShapeDtypeStruct((tokens, units), bf16),
             jax.ShapeDtypeStruct((tokens, units), bf16),
             jax.ShapeDtypeStruct((8, units), f32),
             jax.ShapeDtypeStruct((part, units), bf16),
             jax.ShapeDtypeStruct((part, local), bf16),
         ),
-        in_specs=[ANY, VMEM] + [ANY] * 6,
+        in_specs=[ANY] * 8,
         out_specs=(ANY, ANY, VMEM, ANY, ANY),
         scratch_shapes=[
-            pltpu.VMEM((rows, width), bf16),
             pltpu.VMEM((tokens, width), bf16),
             pltpu.VMEM((chips, tokens, part), bf16),
             pltpu.VMEM((tokens, units), bf16),
@@ -713,12 +498,10 @@
             pltpu.VMEM((tokens, local), bf16),
             pltpu.VMEM((units, width), bf16),
             pltpu.VMEM((tokens, units), bf16),
-            pltpu.VMEM((rows, width), bf16),
             pltpu.VMEM((chips, part, units), bf16),
             pltpu.VMEM((chips, part, local), bf16),
             pltpu.VMEM((6, part, units // 2), bf16),
             pltpu.VMEM((6, part, local // 2), bf16),
-            pltpu.VMEM((2, tensor - 1, rows, width), bf16),
             pltpu.SemaphoreType.DMA((sems.count,)),
             pltpu.SemaphoreType.DMA((sems.count,)),
             pltpu.SemaphoreType.DMA((12,)),
@@ -731,21 +514,20 @@
 
 
 def second_call(dp, tensor, arrays):
-    hidden, cotangent, vec, sums, normed, grad_pre, dq, dk, dv, w_qkv, w_fc1 = arrays
+    hidden, cotangent, vec, sums, normed, grad_pre, grad_qkv = arrays[:7]
     rows, width = hidden.shape
     tokens, units = grad_pre.shape
-    local = dq.shape[1]
-    wide = 3 * local
+    wide = grad_qkv.shape[1]
+    local = wide // 3
     part = width // dp
     chips = dp // 2
     sems = Sems()
     reduce_fc1, reduce_qkv = ChipReduce(sems), ChipReduce(sems)
     line_in = LineReduce(sems, tensor)
-    swaps = [sems.take() for _ in range(chips + 4)]
     tells = [sems.take() for _ in range(2 * (dp - 1) + tensor - 1)]
 
     def kernel(
-        x_ref, c_ref, vec_ref, sum_ref, n_ref, gp_in, dq_in, dk_in, dv_in, wq_ref, w1_ref,
+        x_ref, c_ref, vec_ref, sum_ref, n_ref, gp_in, gq_in, nx_in, gpx_in, gqx_in, wq_ref, w1_ref,
         hid_ref, s1_out, sq_out, vout_ref, bout_ref,
         x_buf, c_buf, n_buf, nx_buf, gp, gpx, gq, gqx, wq, w1, gn,
         s1, sq, r1, rq, rz, parts, tell_v, tell_b, tell_z, send_sem, recv_sem, local_sem,
@@ -767,18 +549,9 @@
                 send_sem=send_sem.at[k], recv_sem=recv_sem.at[k],
                 device_id=device, device_id_type=MESH)
 
-        grads_in = (dq_in, dk_in, dv_in)
-
         def third(i):
             return pl.ds(i * local, local)
 
-        crossing = [
-            remote(swaps[r], n_ref.at[:, cols(relative(twin, r << 1))], nx_buf.at[r], (twin, line))
-            for r in range(chips)
-        ] + [remote(swaps[chips], gp_in, gpx, (twin, line))] + [
-            remote(swaps[chips + 1 + i], grads_in[i], gqx.at[:, third(i)], (twin, line))
-            for i in range(3)
-        ]
         bias_tells = [
             remote(tells[r - 1], sum_ref, tell_b.at[r], (relative(me, r), line)) for r in range(1, dp)
         ]
@@ -794,37 +567,24 @@
         ]
         tile = 512
         pieces = (
-            [(gp_in, gp)]
-            + [(grads_in[i], gq.at[:, third(i)]) for i in range(3)]
+            [(gp_in, gp), (gq_in, gq)]
             + [(w1_ref.at[pl.ds(n, tile), :], w1.at[pl.ds(n, tile), :]) for n in range(0, width, tile)]
             + [
                 (wq_ref.at[i, pl.ds(n, tile), :], wq.at[pl.ds(n, tile), third(i)])
                 for n in range(0, width, tile) for i in range(3)
             ]
-            + [(n_ref, n_buf), (x_ref, x_buf), (c_ref, c_buf)]
+            + [(n_ref, n_buf), (nx_in, nx_buf), (gpx_in, gpx), (gqx_in, gqx), (x_ref, x_buf), (c_ref, c_buf)]
         )
         loads = [pltpu.make_async_copy(a, b, local_sem.at[k]) for k, (a, b) in enumerate(pieces)]
         tiles = width // tile
-        for copy in loads[:4]:
+        late = 2 + 4 * tiles
+        for copy in loads:
             copy.start()
-        for n in range(tiles):
-            loads[4 + n].start()
-            for i in range(3):
-                loads[4 + tiles + 3 * n + i].start()
         greet(dp, me, tensor, line, wide=True)
-        for copy in loads[4 + 4 * tiles :]:
-            copy.start()
-        for copy in crossing:
-            copy.start()
         for copy in bias_tells:
             copy.start()
-        for copy in loads[:4]:
+        for copy in loads[:late]:
             copy.wait()
-        for n in range(tiles):
-            loads[4 + n].wait()
-            for i in range(3):
-                loads[4 + tiles + 3 * n + i].wait()
-
         upper = lax.div(line, tensor // 2)
 
         @pl.loop(0, tensor)
@@ -845,14 +605,14 @@
                     ins.start(0, k)
                     ins.start(1, k)
 
-        loads[4 + 4 * tiles].wait()
+        for copy in loads[late : late + 4]:
+            copy.wait()
 
         def weight_grad(target, plan, own, crossed, size, step):
             @pl.loop(0, chips)
             def _(i):
                 r = chips - 1 - i
-                slot = me + 2 * ((r % 2) * (1 - 2 * (lax.div(me, 2) % 2))) + 4 * (
-                    lax.div(r, 2) * (1 - 2 * (lax.div(me, 4) % 2)))
+                slot = chip_slot(me, r)
 
                 @pl.loop(0, size, step=step)
                 def _(n):
@@ -867,8 +627,6 @@
                     def _():
                         plan.start(k)
 
-        for copy in crossing:
-            copy.wait_recv()
         weight_grad(s1, fc1, gp, gpx, units, 1024)
         ins.advance(1, add_into)
         weight_grad(sq, qkv, gq, gqx, wide, 768)
@@ -880,7 +638,7 @@
         for r in range(1, dp):
             total = total + tell_b[r]
         bout_ref[...] = total
-        for copy in loads[5 + 4 * tiles :]:
+        for copy in loads[late + 4 :]:
             copy.wait()
         qkv.middle()
         ins.arrive()
@@ -928,7 +686,7 @@
         for k in range(1, tensor):
             total_z = total_z + tell_z[k]
         vout_ref[...] = total_z
-        for copy in crossing + bias_tells + vec_tells + line_tells:
+        for copy in bias_tells + vec_tells + line_tells:
             copy.wait_send()
         for plan in (fc1, qkv, ins):
             plan.finish()
@@ -944,7 +702,7 @@
             jax.ShapeDtypeStruct((8, part), f32),
             jax.ShapeDtypeStruct((8, local), f32),
         ),
-        in_specs=[ANY] * 2 + [VMEM] * 2 + [ANY] * 7,
+        in_specs=[ANY] * 2 + [VMEM] * 2 + [ANY] * 8,
         out_specs=(ANY, ANY, ANY, VMEM, VMEM),
         scratch_shapes=[
             pltpu.VMEM((rows, width), bf16),
@@ -962,7 +720,7 @@
             pltpu.VMEM((chips, part, wide), bf16),
             pltpu.VMEM((6, part, units // 2), bf16),
             pltpu.VMEM((6, part, wide // 2), bf16),
-            pltpu.VMEM((2, tensor - 1, rows, width), bf16),
+            pltpu.VMEM((2 * tensor - 3, rows, width), bf16),
             pltpu.VMEM((8, width), f32),
             pltpu.VMEM((dp, 8, part), f32),
             pltpu.VMEM((dp, 8, local), f32),
@@ -1005,16 +763,9 @@
     q_ref, k_ref, v_ref, bias_ref, cos_ref, slo_ref, shi_ref, segc_ref, segr_ref,
     qs_ref, ks_ref, vs_ref, o_ref, p_ref, mask_ref,
 ):
-    length = q_ref.shape[0]
-    spans, _ = spans_of(length)
-
     @pl.when(pl.program_id(1) == 0)
     def _():
-        for i, (low, high, at) in enumerate(spans):
-            keys = lax.broadcasted_iota(jnp.int32, (high - low, BLOCK), 0) + low
-            queries = lax.broadcasted_iota(jnp.int32, (high - low, BLOCK), 1) + i * BLOCK
-            same = segc_ref[low:high, :] == segr_ref[:, i * BLOCK : (i + 1) * BLOCK]
-            mask_ref[at : at + high - low, :] = jnp.where((keys <= queries) & same, 0.0, -1e30)
+        fill_mask(mask_ref, segc_ref, segr_ref, q_ref.shape[0])
 
     cosine, slo, shi = cos_ref[...], slo_ref[...], shi_ref[...]
     query = turn(q_ref[...] + bias_ref[0:1, :], cosine, slo, shi).astype(bf16) * bf16(HD**-0.5)
@@ -1023,18 +774,14 @@
     qs_ref[...] = query
     ks_ref[...] = key
     vs_ref[...] = value
-    heads = 128 // HD
-    for i, (low, high, at) in enumerate(spans):
-        q_i = query[i * BLOCK : (i + 1) * BLOCK]
-        total = jnp.zeros((BLOCK, 128), f32)
-        for e in range(heads):
-            scores = dot_nt(only(key[low:high], e), q_i) + mask_ref[at : at + high - low, :]
-            exponent = jnp.exp(scores - jnp.max(scores, 0, keepdims=True))
-            inverse = 1.0 / jnp.sum(exponent, 0, keepdims=True)
-            probs = (exponent * inverse).astype(bf16)
-            p_ref[e, at : at + high - low, :] = probs
-            total = total + dot_tn(probs, only(value[low:high], e))
-        o_ref[i * BLOCK : (i + 1) * BLOCK, :] = total.astype(bf16)
+
+    def keep(e, at, probs):
+        p_ref[e, at, :] = probs
+
+    def write(at, result):
+        o_ref[at, :] = result
+
+    attend_pair(query, key, value, mask_ref, keep, write)
 
 
 def attend(q, k, v, qkv_bias, tables, segments, rows):
@@ -1071,48 +818,13 @@
     q_ref, k_ref, v_ref, g_ref, o_ref, p_ref, cos_ref, slo_ref, shi_ref,
     dq_ref, dk_ref, dv_ref, bias_ref, kacc_ref, vacc_ref,
 ):
-    length = q_ref.shape[0]
-    spans, _ = spans_of(length)
-    heads = 128 // HD
-    grad = g_ref[...]
-    inner = grad.astype(f32) * o_ref[...].astype(f32)
-    lane = lax.broadcasted_iota(jnp.int32, (8, 128), 1)
-    row = lax.broadcasted_iota(jnp.int32, (8, 128), 0)
-    pick = jnp.where(lax.div(lane, HD) == row, 1.0, 0.0)
-    delta = lax.dot_general(
-        pick, inner, (((1,), (1,)), ((), ())),
-        precision=lax.Precision.HIGHEST, preferred_element_type=f32)
-    query, key, value = q_ref[...], k_ref[...], v_ref[...]
-    kacc_ref[...] = jnp.zeros_like(kacc_ref)
-    vacc_ref[...] = jnp.zeros_like(vacc_ref)
-    cosine, slo, shi = cos_ref[...], slo_ref[...], shi_ref[...]
-    first = jnp.zeros((1, 128), f32)
-    for i, (low, high, at) in enumerate(spans):
-        mine = slice(i * BLOCK, (i + 1) * BLOCK)
-        g_i, q_i = grad[mine], query[mine]
-        dq = jnp.zeros((BLOCK, 128), f32)
-        ps, dss = [], []
-        for e in range(heads):
-            probs = p_ref[e, at : at + high - low, :]
-            dprobs = dot_nt(only(value[low:high], e), g_i)
-            ds = (probs.astype(f32) * (dprobs - delta[e : e + 1, mine])).astype(bf16)
-            dq = dq + dot_tn(ds, only(key[low:high], e))
-            ps.append(probs)
-            dss.append(ds)
-        g_cat = jnp.concatenate([only(g_i, e) for e in range(heads)], 0)
-        q_cat = jnp.concatenate([only(q_i, e) for e in range(heads)], 0)
-        vacc_ref[low:high, :] += dot_nn(jnp.concatenate(ps, 1), g_cat)
-        kacc_ref[low:high, :] += dot_nn(jnp.concatenate(dss, 1), q_cat)
-        dq = dq * f32(HD**-0.5)
-        dq = turn(dq, cosine[mine], -slo[mine], -shi[mine]).astype(bf16)
-        dq_ref[mine, :] = dq
-        first = first + jnp.sum(dq.astype(f32), 0, keepdims=True)
-    dk = turn(kacc_ref[...], cosine, -slo, -shi).astype(bf16)
-    dv = vacc_ref[...].astype(bf16)
-    dk_ref[...] = dk
-    dv_ref[...] = dv
-    sums = [first, jnp.sum(dk.astype(f32), 0, keepdims=True), jnp.sum(dv.astype(f32), 0, keepdims=True)]
-    sums = jnp.concatenate(sums + [jnp.zeros((5, 128), f32)], 0)
+    def write(which, at, value):
+        (dq_ref, dk_ref, dv_ref)[which][at, :] = value
+
+    sums = attend_back_pair(
+        q_ref[...], k_ref[...], v_ref[...], g_ref[...], o_ref[...],
+        lambda e, at: p_ref[e, at, :], (cos_ref, slo_ref, shi_ref), kacc_ref, vacc_ref, write)
+    sums = jnp.concatenate(list(sums) + [jnp.zeros((5, 128), f32)], 0)
 
     @pl.when(pl.program_id(1) == 0)
     def _():
@@ -1148,6 +860,460 @@
     )(q, k, v, g, o, probs, *tables)
 
 
+def attend_pair(query, key, value, mask_ref, keep, write):
+    length = query.shape[0]
+    spans, _ = spans_of(length)
+    for i, (low, high, at) in enumerate(spans):
+        mine = slice(i * BLOCK, (i + 1) * BLOCK)
+        total = jnp.zeros((BLOCK, 128), f32)
+        for e in range(128 // HD):
+            scores = dot_nt(only(key[low:high], e), query[mine]) + mask_ref[at : at + high - low, :]
+            exponent = jnp.exp(scores - jnp.max(scores, 0, keepdims=True))
+            inverse = 1.0 / jnp.sum(exponent, 0, keepdims=True)
+            probs = (exponent * inverse).astype(bf16)
+            keep(e, slice(at, at + high - low), probs)
+            total = total + dot_tn(probs, only(value[low:high], e))
+        write(mine, total.astype(bf16))
+
+
+def fill_mask(mask_ref, segc_ref, segr_ref, length):
+    for i, (low, high, at) in enumerate(spans_of(length)[0]):
+        keys = lax.broadcasted_iota(jnp.int32, (high - low, BLOCK), 0) + low
+        queries = lax.broadcasted_iota(jnp.int32, (high - low, BLOCK), 1) + i * BLOCK
+        same = segc_ref[low:high, :] == segr_ref[:, i * BLOCK : (i + 1) * BLOCK]
+        mask_ref[at : at + high - low, :] = jnp.where((keys <= queries) & same, 0.0, -1e30)
+
+
+def attend_back_pair(query, key, value, grad, result, probs_of, tables, kacc_ref, vacc_ref, write):
+    length = query.shape[0]
+    spans, _ = spans_of(length)
+    heads = 128 // HD
+    inner = grad.astype(f32) * result.astype(f32)
+    lane = lax.broadcasted_iota(jnp.int32, (8, 128), 1)
+    row = lax.broadcasted_iota(jnp.int32, (8, 128), 0)
+    pick = jnp.where(lax.div(lane, HD) == row, 1.0, 0.0)
+    delta = lax.dot_general(
+        pick, inner, (((1,), (1,)), ((), ())),
+        precision=lax.Precision.HIGHEST, preferred_element_type=f32)
+    kacc_ref[...] = jnp.zeros_like(kacc_ref)
+    vacc_ref[...] = jnp.zeros_like(vacc_ref)
+    cos_ref, slo_ref, shi_ref = tables
+    first = jnp.zeros((1, 128), f32)
+    for i, (low, high, at) in enumerate(spans):
+        mine = slice(i * BLOCK, (i + 1) * BLOCK)
+        g_i, q_i = grad[mine], query[mine]
+        dq = jnp.zeros((BLOCK, 128), f32)
+        ps, dss = [], []
+        for e in range(heads):
+            probs = probs_of(e, slice(at, at + high - low))
+            dprobs = dot_nt(only(value[low:high], e), g_i)
+            ds = (probs.astype(f32) * (dprobs - delta[e : e + 1, mine])).astype(bf16)
+            dq = dq + dot_tn(ds, only(key[low:high], e))
+            ps.append(probs)
+            dss.append(ds)
+        g_cat = jnp.concatenate([only(g_i, e) for e in range(heads)], 0)
+        q_cat = jnp.concatenate([only(q_i, e) for e in range(heads)], 0)
+        vacc_ref[low:high, :] += dot_nn(jnp.concatenate(ps, 1), g_cat)
+        kacc_ref[low:high, :] += dot_nn(jnp.concatenate(dss, 1), q_cat)
+        dq = dq * f32(HD**-0.5)
+        dq = turn(dq, cos_ref[mine, :], -slo_ref[mine, :], -shi_ref[mine, :]).astype(bf16)
+        write(0, mine, dq)
+        first = first + jnp.sum(dq.astype(f32), 0, keepdims=True)
+    everything = slice(0, length)
+    dk = turn(kacc_ref[...], cos_ref[...], -slo_ref[...], -shi_ref[...]).astype(bf16)
+    dv = vacc_ref[...].astype(bf16)
+    write(1, everything, dk)
+    write(2, everything, dv)
+    return first, jnp.sum(dk.astype(f32), 0, keepdims=True), jnp.sum(dv.astype(f32), 0, keepdims=True)
+
+
+def forward_call(dp, tensor, arrays):
+    hidden, cotangent, w_qkv, w_dense, w_fc1, w_fc2, vectors = arrays[:7]
+    rows, width = hidden.shape
+    local = w_qkv.shape[2]
+    units = w_fc1.shape[1]
+    part = width // dp
+    chips = dp // 2
+    tokens = rows * tensor
+    pairs = local // 128
+    stored = spans_of(tokens)[1]
+    sems = Sems()
+    orders = orders_of(dp)
+    plan_vec = CubeGather(sems, orders[:1])
+    plan_qkv, plan_dense, plan_fc1, plan_fc2 = (CubeGather(sems, orders) for _ in range(4))
+    plan_n, plan_c = LineGather(sems, tensor, 2), LineGather(sems, tensor, 2)
+    line_out = LineReduce(sems, tensor)
+    swaps = [sems.take() for _ in range(2 * chips + 3)]
+
+    def kernel(
+        x_ref, c_ref, wq_ref, wd_ref, w1_ref, w2_ref, vec_ref,
+        qb_ref, fb_ref, cos_ref, slo_ref, shi_ref, segc_ref, segr_ref,
+        out_ref, gq_ref, g1_ref, g2_ref, n_out, nx_out, c_out, cx_out, a_out, ax_out, d_out,
+        t_out, tx_out, dq_out, dqx_out, gvec_ref, qsum_ref,
+        x_buf, vec_buf, nv, wa, wb, wd, act, slope, qkv3, attn, pb, mask, g_buf, kacc, vacc, rz,
+        send_sem, recv_sem, local_sem,
+    ):
+        me, line = lax.axis_index("dp"), lax.axis_index("tensor")
+        twin = flip(me, 0)
+        half = part // 2
+        local_count = [0]
+
+        def cols(a):
+            return pl.ds(pl.multiple_of(a * part, part), part)
+
+        def half_rows(a, h):
+            return pl.ds(pl.multiple_of(a * part + h * half, half), half)
+
+        def tok(b, u):
+            return pl.ds(pl.multiple_of(b * rows + u * (rows // 2), rows // 2), rows // 2)
+
+        def block(b):
+            return pl.ds(pl.multiple_of(b * rows, rows), rows)
+
+        def piece(n, h):
+            return pl.ds(h * (n // 2), n // 2)
+
+        def copy_of(a, b):
+            local_count[0] += 1
+            return pltpu.make_async_copy(a, b, local_sem.at[local_count[0] - 1])
+
+        def to_twin(k, source, target):
+            return pltpu.make_async_remote_copy(
+                src_ref=source, dst_ref=target,
+                send_sem=send_sem.at[swaps[k]], recv_sem=recv_sem.at[swaps[k]],
+                device_id=(twin, line), device_id_type=MESH)
+
+        pair = (send_sem, recv_sem)
+        vec = plan_vec.bind(me, line, lambda h: vec_ref, lambda a, h: vec_buf.at[:, cols(a)], *pair)
+        qkv = plan_qkv.bind(
+            me, line,
+            lambda h: wq_ref.at[:, pl.ds(h * half, half), :],
+            lambda a, h: gq_ref.at[:, half_rows(a, h), :], *pair)
+        fc1 = plan_fc1.bind(
+            me, line,
+            lambda h: w1_ref.at[pl.ds(h * half, half), :],
+            lambda a, h: g1_ref.at[half_rows(a, h), :], *pair)
+        dense = plan_dense.bind(
+            me, line,
+            lambda h: wd_ref.at[piece(local, h), :],
+            lambda a, h: wd.at[piece(local, h), cols(a)], *pair)
+        fc2 = plan_fc2.bind(
+            me, line,
+            lambda h: w2_ref.at[piece(units, h), :],
+            lambda a, h: g2_ref.at[piece(units, h), cols(a)], *pair)
+        norm = plan_n.bind(
+            line, me, lambda u: nv.at[tok(line, u)], lambda b, u: nv.at[tok(b, u)], *pair)
+        cot = plan_c.bind(
+            line, me, lambda u: c_ref.at[piece(rows, u)], lambda b, u: c_out.at[tok(b, u)], *pair)
+        outs = line_out.bind(line, me, lambda d: nv.at[pl.ds(d * rows, rows), :], rz, *pair)
+        stages = dp.bit_length() - 1
+
+        keeps = [
+            copy_of(x_ref, x_buf),
+            copy_of(vec_ref, vec_buf.at[:, cols(me)]),
+            copy_of(wq_ref, gq_ref.at[:, cols(me), :]),
+            copy_of(w1_ref, g1_ref.at[cols(me), :]),
+            copy_of(wd_ref, wd.at[:, cols(me)]),
+            copy_of(w2_ref, g2_ref.at[:, cols(me)]),
+            copy_of(c_ref, c_out.at[block(line), :]),
+        ]
+        keeps[0].start()
+        greet(dp, me, tensor, line)
+        vec.start()
+        qkv.start()
+        cot.start(0)
+        for copy in keeps[1:]:
+            copy.start()
+        for j in range(stages):
+            vec.advance(j)
+        keeps[0].wait()
+        keeps[1].wait()
+
+        @pl.loop(0, rows, step=32)
+        def _(r):
+            x = x_buf[pl.ds(r, 32), :].astype(f32)
+            centred = x - jnp.mean(x, -1, keepdims=True)
+            spread = jnp.mean(centred * centred, -1, keepdims=True)
+            unit = centred * lax.rsqrt(spread + layer_eps)
+            at = pl.ds(pl.multiple_of(line * rows + r, 32), 32)
+            nv[at, :] = (unit * vec_buf[0:1, :] + vec_buf[1:2, :]).astype(bf16)
+
+        norm.start(0)
+        norm.start(1)
+        gvec_ref[...] = vec_buf[...]
+        qkv.advance(0)
+        fc1.start()
+        fill_mask(mask, segc_ref, segr_ref, tokens)
+
+        def project(b):
+            at = block(b)
+            cosine, slo, shi = cos_ref[at, :], slo_ref[at, :], shi_ref[at, :]
+            for i in range(3):
+                value = dot_nn(nv[at, :], wa[:, i * local : (i + 1) * local]) + qb_ref[i : i + 1, :]
+                if i == 2:
+                    qkv3[2, at, :] = value.astype(bf16)
+                    continue
+                for h in range(pairs):
+                    lanes = slice(h * 128, (h + 1) * 128)
+                    turned = turn(value[:, lanes], cosine, slo, shi).astype(bf16)
+                    if i == 0:
+                        turned = turned * bf16(HD**-0.5)
+                    qkv3[i, at, lanes] = turned
+
+        def hidden_layer(b):
+            at = block(b)
+
+            @pl.loop(0, units, step=512)
+            def _(n):
+                to = pl.ds(pl.multiple_of(n, 512), 512)
+                pre = dot_nn(nv[at, :], wb[:, to]) + fb_ref[0:1, to]
+                square = pre * pre
+                bend = jnp.tanh(0.7978845608028654 * pre * (1.0 + 0.044715 * square))
+                act[at, to] = (0.5 * pre * (1.0 + bend)).astype(bf16)
+                rise = 0.7978845608028654 * (1.0 + 3 * 0.044715 * square)
+                slope[at, to] = (
+                    0.5 * (1.0 + bend) + 0.5 * pre * (1.0 - bend * bend) * rise
+                ).astype(bf16)
+
+        norm.advance(0, 0)
+        for j in range(1, stages - 1):
+            qkv.advance(j)
+        norm.advance(0, 1)
+        qkv.advance(stages - 1)
+        keeps[2].wait()
+        load_q = [
+            copy_of(gq_ref.at[i], wa.at[:, pl.ds(i * local, local)]) for i in range(3)
+        ]
+        for copy in load_q:
+            copy.start()
+        fc1.advance(0)
+        dense.start()
+        fc2.start()
+        for copy in load_q:
+            copy.wait()
+
+        @pl.loop(0, 4)
+        def _(i):
+            s = i - 1
+
+            @pl.when(i == 2)
+            def _():
+                norm.advance(1, 0)
+                norm.advance(1, 1)
+                cot.start(1)
+
+            @pl.when(i == 3)
+            def _():
+                for j in range(1, stages):
+                    fc1.advance(j)
+                dense.advance(0)
+                norm.advance(2, 0)
+                norm.advance(2, 1)
+
+            @pl.loop(0, 2)
+            def _(way):
+                b = line + (2 * way - 1) * (1 + s)
+
+                @pl.when((b >= 0) & (b < tensor) & ((i > 0) | (way == 0)))
+                def _():
+                    project(b)
+
+        keeps[3].wait()
+        load_1 = copy_of(g1_ref, wb)
+        load_1.start()
+        n_store = copy_of(nv, n_out)
+        n_store.start()
+        cross_n = [
+            to_twin(r, nv.at[:, cols(relative(twin, r << 1))], nx_out.at[r]) for r in range(chips)
+        ]
+        for copy in cross_n:
+            copy.start()
+        fc2.advance(0)
+        cot.advance(0, 0)
+        load_1.wait()
+
+        @pl.loop(0, tensor)
+        def _(b):
+            hidden_layer(b)
+
+            @pl.when(b == 1)
+            def _():
+                cot.advance(0, 1)
+                for j in range(1, stages - 1):
+                    dense.advance(j)
+
+        for j in range(1, stages - 1):
+            fc2.advance(j)
+        stores = [copy_of(act, a_out), copy_of(slope, d_out)]
+        cross_a = to_twin(chips, act, ax_out)
+        for copy in stores + [cross_a]:
+            copy.start()
+        dense.advance(stages - 1)
+        fc2.advance(stages - 1)
+        keeps[4].wait()
+        keeps[5].wait()
+        load_2 = copy_of(g2_ref, wa)
+        load_2.start()
+
+        @pl.loop(0, pairs)
+        def _(h):
+            lanes = pl.ds(pl.multiple_of(h * 128, 128), 128)
+
+            def keep(e, at, value):
+                pb[2 * h + e, at, :] = value
+
+            def write(at, value):
+                attn[at, lanes] = value
+
+            attend_pair(
+                qkv3[0, :, lanes], qkv3[1, :, lanes], qkv3[2, :, lanes], mask, keep, write)
+
+            @pl.when(h == 1)
+            def _():
+                cot.advance(1, 0)
+
+        cross_t = to_twin(chips + 1, attn, tx_out)
+        stores.append(copy_of(attn, t_out))
+        stores[-1].start()
+        cross_t.start()
+        cot.advance(1, 1)
+        load_2.wait()
+        norm.finish()
+        n_store.wait()
+        for copy in cross_n:
+            copy.wait_send()
+        upper = lax.div(line, tensor // 2)
+
+        @pl.loop(0, tensor)
+        def _(i):
+            d = (1 - upper) * (tensor - 1 - i) + upper * i
+            at = block(d)
+
+            @pl.loop(0, width, step=1024)
+            def _(n):
+                to = pl.ds(pl.multiple_of(n, 1024), 1024)
+                value = dot_nn(act[at, :], wa[:, to]) + dot_nn(attn[at, :], wd[:, to])
+                nv[at, to] = value.astype(bf16)
+
+            for k in range(tensor - 1):
+
+                @pl.when(i == k)
+                def _():
+                    outs.start(0, k)
+                    outs.start(1, k)
+
+        cot.advance(2, 0)
+        outs.advance(1, add_into)
+        cot.advance(2, 1)
+        keeps[6].wait()
+        grad = wa.at[pl.ds(0, tokens), :]
+        load_c = copy_of(c_out, grad)
+        load_c.start()
+        cross_c = [
+            to_twin(chips + 2 + r, c_out.at[:, cols(relative(twin, r << 1))], cx_out.at[r])
+            for r in range(chips)
+        ]
+        for copy in cross_c:
+            copy.start()
+        load_c.wait()
+        g_buf[...] = dot_nt(grad[...], wd[...]).astype(bf16)
+        outs.advance(2, add_into)
+        qsum_ref[...] = jnp.zeros_like(qsum_ref)
+
+        @pl.loop(0, pairs)
+        def _(h):
+            lanes = pl.ds(pl.multiple_of(h * 128, 128), 128)
+
+            def write(which, at, value):
+                wb[at, pl.ds(pl.multiple_of(which * local + h * 128, 128), 128)] = value
+
+            sums = attend_back_pair(
+                qkv3[0, :, lanes], qkv3[1, :, lanes], qkv3[2, :, lanes],
+                g_buf[:, lanes], attn[:, lanes], lambda e, at: pb[2 * h + e, at, :],
+                (cos_ref, slo_ref, shi_ref), kacc, vacc, write)
+            for k in range(3):
+                qsum_ref[k : k + 1, lanes] = sums[k]
+
+        back = wb.at[pl.ds(0, tokens), pl.ds(0, 3 * local)]
+        stores.append(copy_of(back, dq_out))
+        stores[-1].start()
+        cross_d = to_twin(2 * chips + 2, back, dqx_out)
+        cross_d.start()
+        outs.arrive()
+
+        @pl.loop(0, rows, step=32)
+        def _(r):
+            at = pl.ds(r, 32)
+            own = pl.ds(pl.multiple_of(line * rows + r, 32), 32)
+            total = x_buf[at, :].astype(f32) + outs.total(nv[own, :], at) + vec_buf[2:3, :]
+            x_buf[at, :] = total.astype(bf16)
+
+        stores.append(copy_of(x_buf, out_ref))
+        stores[-1].start()
+        crossed = cross_n + [cross_a, cross_t] + cross_c + [cross_d]
+        for copy in crossed:
+            copy.wait_recv()
+        for copy in crossed[chips:]:
+            copy.wait_send()
+        for plan in (vec, qkv, fc1, dense, fc2, cot, outs):
+            plan.finish()
+        for copy in stores:
+            copy.wait()
+
+    def shape(*dims):
+        return jax.ShapeDtypeStruct(dims, bf16)
+
+    return pl.pallas_call(
+        kernel,
+        out_shape=(
+            shape(rows, width),
+            shape(3, width, local),
+            shape(width, units),
+            shape(units, width),
+            shape(tokens, width),
+            shape(chips, tokens, part),
+            shape(tokens, width),
+            shape(chips, tokens, part),
+            shape(tokens, units),
+            shape(tokens, units),
+            shape(tokens, units),
+            shape(tokens, local),
+            shape(tokens, local),
+            shape(tokens, 3 * local),
+            shape(tokens, 3 * local),
+            jax.ShapeDtypeStruct((8, width), f32),
+            jax.ShapeDtypeStruct((8, local), f32),
+        ),
+        in_specs=[ANY] * 7 + [VMEM] * 7,
+        out_specs=(ANY,) * 15 + (VMEM,) * 2,
+        scratch_shapes=[
+            pltpu.VMEM((rows, width), bf16),
+            pltpu.VMEM((8, width), f32),
+            pltpu.VMEM((tokens, width), bf16),
+            pltpu.VMEM((width, width), bf16),
+            pltpu.VMEM((width, units), bf16),
+            pltpu.VMEM((local, width), bf16),
+            pltpu.VMEM((tokens, units), bf16),
+            pltpu.VMEM((tokens, units), bf16),
+            pltpu.VMEM((3, tokens, local), bf16),
+            pltpu.VMEM((tokens, local), bf16),
+            pltpu.VMEM((local // HD, stored, BLOCK), bf16),
+            pltpu.VMEM((stored, BLOCK), f32),
+            pltpu.VMEM((tokens, local), bf16),
+            pltpu.VMEM((tokens, 128), f32),
+            pltpu.VMEM((tokens, 128), f32),
+            pltpu.VMEM((2 * tensor - 3, rows, width), bf16),
+            pltpu.SemaphoreType.DMA((sems.count,)),
+            pltpu.SemaphoreType.DMA((sems.count,)),
+            pltpu.SemaphoreType.DMA((24,)),
+        ],
+        compiler_params=pltpu.CompilerParams(
+            collective_id=0, has_side_effects=True, vmem_limit_bytes=VMEM_LIMIT
+        ),
+        name="forward",
+    )(*arrays)
+
+
 def rotary_tables(segments):
     rows, length = segments.shape
     index = jnp.arange(length, dtype=jnp.int32)[None]
@@ -1184,29 +1350,24 @@
         hidden_in, cotangent, qkv_weight.transpose(1, 0, 2),
         dense_weight, fc1_weight, fc2_weight, vectors,
     )
-    gathered = gather_call(dp, tensor, *mine) if fast else gather_plain(*mine)
-    w_qkv, w_dense, w_fc1, w_fc2, normed, grad_out, vec = gathered
-    gain, out_bias = vec[0:1], vec[2:3]
     tables = rotary_tables(segments)
     bias = jnp.pad(qkv_bias.astype(f32), ((0, 5), (0, 0)))
-    query, key, value, attn_vec, probs = attend(
-        *(matmul(normed, w_qkv[i]) for i in range(3)), bias, tables, segments, seqs
-    )
-    pre_act = matmul(normed, w_fc1) + fc1_bias.astype(f32)
-    act_vals, gelu_pull = jax.vjp(lambda pre: jax.nn.gelu(pre, approximate=True), pre_act)
-    act_vals = act_vals.astype(bf16)
-    slope = gelu_pull(jnp.ones_like(pre_act))[0].astype(bf16)
-    branches = matmul(attn_vec, w_dense) + matmul(act_vals, w_fc2)
-    grad_attn = matmul(grad_out, w_dense.T).astype(bf16)
-    *grads, qkv_sums = attend_back(query, key, value, grad_attn, attn_vec, probs, tables, seqs)
     if fast:
-        out, grad_pre, fc1_sums, sent_fc2, sent_dense = first_call(
+        (
+            out, w_qkv, w_fc1, w_fc2, normed, crossed_normed, grad_out, crossed_out,
+            act, crossed_act, slope, attn, crossed_attn, grad_qkv, crossed_qkv, vec, qkv_sums,
+        ) = forward_call(
             dp, tensor,
-            (hidden_in, vec, branches.astype(bf16), grad_out, act_vals, slope, attn_vec, w_fc2))
+            (*mine, bias, fc1_bias.astype(f32)[None], *tables,
+             segments.reshape(-1, 1), segments.reshape(1, -1)))
+        grad_pre, crossed_pre, fc1_sums, sent_fc2, sent_dense = first_call(
+            dp, tensor,
+            (grad_out, crossed_out, act, crossed_act, slope, attn, crossed_attn, w_fc2))
         sums = jnp.concatenate([fc1_sums[0].reshape(4, local), qkv_sums[:3], jnp.zeros((1, local), f32)], 0)
         hidden_grad, sent_fc1, sent_qkv, vec_sums, all_sums = second_call(
             dp, tensor,
-            (hidden_in, cotangent, vec, sums, normed, grad_pre, *grads, w_qkv, w_fc1))
+            (hidden_in, cotangent, vec, sums, normed, grad_pre, grad_qkv,
+             crossed_normed, crossed_pre, crossed_qkv, w_qkv, w_fc1))
         quarter = vec_sums.shape[1] // tensor
         at = lax.axis_index("tensor") * quarter
         small = lax.dynamic_slice(vec_sums, (0, at), (3, quarter))
@@ -1225,6 +1386,18 @@
             small[2],
         )
 
+    w_qkv, w_dense, w_fc1, w_fc2, normed, grad_out, vec = gather_plain(*mine)
+    gain, out_bias = vec[0:1], vec[2:3]
+    query, key, value, attn_vec, probs = attend(
+        *(matmul(normed, w_qkv[i]) for i in range(3)), bias, tables, segments, seqs
+    )
+    pre_act = matmul(normed, w_fc1) + fc1_bias.astype(f32)
+    act_vals, gelu_pull = jax.vjp(lambda pre: jax.nn.gelu(pre, approximate=True), pre_act)
+    act_vals = act_vals.astype(bf16)
+    slope = gelu_pull(jnp.ones_like(pre_act))[0].astype(bf16)
+    branches = matmul(attn_vec, w_dense) + matmul(act_vals, w_fc2)
+    grad_attn = matmul(grad_out, w_dense.T).astype(bf16)
+    *grads, qkv_sums = attend_back(query, key, value, grad_attn, attn_vec, probs, tables, seqs)
     resid_in = hidden_in.astype(f32)
     cot_float = cotangent.astype(f32)
     centred = resid_in - jnp.mean(resid_in, -1, keepdims=True)

time: 477 us -> 391 us (0.82); the launches traced: 469 us -> 390 us
  matrix products: 56.2 us -> 0 us
  Pallas kernels: 385 us -> 358 us
    dot_general x7 -> x0, matrix products: 56.2 us -> none  [matmul(): return jnp.dot(a, b, preferred_element_type=f32)]
    pallas_call x4 -> x2, Pallas kernels: 290 us -> 264 us  [the longest x1 213 us: forward_call(): pl.pallas_call(kernel, out_shape=(shape(rows, width), shape(3, width, loc...]
where the time goes in v3:
time: 391 us; the launch traced here: 390 us
  Pallas kernels  358 us (92%)
  other arithmetic  16.2 us (4%)
  local copies, waits for them, and re-layouts  15.5 us (4%)
    pallas_call x1, Pallas kernels, forward_call(): pl.pallas_call(kernel, out_shape=(shape(rows, width), shape(3, width, loc...  213 us
    pallas_call x1, Pallas kernels, second_call(): pl.pallas_call(kernel, out_shape=(jax.ShapeDtypeStruct((rows, width), bf1...  93.3 us
    pallas_call x1, Pallas kernels, first_call(): pl.pallas_call(kernel, out_shape=(jax.ShapeDtypeStruct((tokens, units), b...  51.3 us
    unnamed x18, local copies, waits for them, and re-layouts  8.84 us

profile of v3, /device:TPU:0, one launch (start us, length us, event | category | flops | bytes accessed | tf_op | source)
XLA Modules:
  0.0 390.1 jit_solution(9140411941678131908)
XLA Ops:
  0.6 0.7 convert_add_fusion
  1.3 0.7 stack.25
  2.0 0.7 stack.24
  2.6 0.6 select_maximum_fusion.vec_ref
  3.2 1.3 pad_convert_fusion.qb_ref
  4.5 1.3 broadcast_in_dim.64
  5.8 1.4 fusion.5
  7.2 2.6 fusion.8
  9.9 3.2 fusion
  13.1 1.7 copy.28.segc_ref
  14.8 213.1 %forward.1 = (bf16[256,2048]{1,0:T(8,128)(2,1)}, bf16[3,2048,512]{2,1,0:T(8,128)(2,1)}, bf16[2048,2048]{1,0:T(8,128)(2,1)}, bf16[2048,2048]{1,0:T(8,128)(2,1)}, ...) custom-call(bf16[256,2048]{1,0:T(8,128)(2,1)} %x_ref.3, ...), custom_call_target="tpu_custom_call" | custom-call | tf_op jit(solution)/shard_map/forward/pallas_call | solution.py:1266
  227.9 0.7 slice.23
  228.6 51.3 %first_back.1 = (bf16[1024,2048]{1,0:T(8,128)(2,1)}, bf16[1024,2048]{1,0:T(8,128)(2,1)}, f32[8,2048]{1,0:T(8,128)}, bf16[256,2048]{1,0:T(8,128)(2,1)}, bf16[256,512]{1,0:T(8,128)(2,1)}) custom-call(bf16[1024,2048]{1,0:T(8,128)(2,1)} %get-tuple-element.41.c_ref, bf16[4,1024,256]{2,1,0:T(8,128)(2,1)} %get-tuple-element.42.cx_ref, ...), custom_call_target="tpu_custom_call" | custom-call | tf_op jit(solution)/shard_map/first_back/pallas_call | solution.py:481
  279.9 0.9 slice_reduce_fusion
  280.9 0.7 maximum_maximum_fusion.sum_ref
  281.6 93.3 %second_back.1 = (bf16[256,2048]{1,0:T(8,128)(2,1)}, bf16[256,2048]{1,0:T(8,128)(2,1)}, bf16[256,1536]{1,0:T(8,128)(2,1)}, f32[8,256]{1,0:T(8,128)}, f32[8,512]{1,0:T(8,128)}) custom-call(bf16[256,2048]{1,0:T(8,128)(2,1)} %x_ref.3, bf16[256,2048]{1,0:T(8,128)(2,1)} %c_ref.3, f32[8,2048]{1,0:T(8,128)} %get-tuple-element.40.vec_ref, ...), custom_call_target="tpu_custom_call" | custom-call | tf_op jit(solution)/shard_map/second_back/pallas_call | solution.py:696
  374.9 0.8 constant_dynamic-slice_fusion
  376.2 1.4 copy.29
  377.6 1.6 copy.30
  379.9 1.0 copy.31
  380.9 2.8 convert_element_type.58
  384.5 1.8 copy.32
  386.9 2.3 copy.38
  389.2 1.0 copy.39
  (22 shorter events, 2.7 us)
Async XLA Ops:
  374.8 4.4 %copy-start.3 = (f32[8,512]{1,0:T(8,128)S(1)}, f32[8,512]{1,0:T(8,128)}, u32[]{:S(2)}) copy-start(f32[8,512]{1,0:T(8,128)} %get-tuple-element.62) | copy-start | bytes 49156
  374.8 5.0 %copy-start.2 = (bf16[256,512]{1,0:T(8,128)(2,1)S(1)}, bf16[256,512]{1,0:T(8,128)(2,1)}, u32[]{:S(2)}) copy-start(bf16[256,512]{1,0:T(8,128)(2,1)} %get-tuple-element.63) | copy-start | bytes 786436
  376.2 10.2 %copy-start.4 = (f32[64]{0:T(128)}, f32[64]{0:T(128)S(1)}, u32[]{:S(2)}) copy-start(f32[64]{0:T(128)S(1)} %get-tuple-element.144) | copy-start | bytes 772
  377.6 6.7 %copy-start = (bf16[256,2048]{1,0:T(8,128)(2,1)S(1)}, bf16[256,2048]{1,0:T(8,128)(2,1)}, u32[]{:S(2)}) copy-start(bf16[256,2048]{1,0:T(8,128)(2,1)} %get-tuple-element.65) | copy-start | bytes 3145732
  384.5 4.6 %copy-start.1 = (bf16[256,2048]{1,0:T(8,128)(2,1)S(1)}, bf16[256,2048]{1,0:T(8,128)(2,1)}, u32[]{:S(2)}) copy-start(bf16[256,2048]{1,0:T(8,128)(2,1)} %get-tuple-element.138) | copy-start | bytes 3145732

commit v4 on v3

--- a/solution.py
+++ b/solution.py
@@ -180,22 +180,19 @@
                 self.copy(way, s, u).wait_send()
 
 
-def greet(dp, me, tensor, line, wide=False):
+def greet(dp, me, tensor, line, all_tensor):
     barrier = pltpu.get_barrier_semaphore()
 
     def hello(a, b):
         pl.semaphore_signal(barrier, inc=1, device_id=(a, b), device_id_type=MESH)
 
-    if wide:
-        for r in range(1, dp):
-            hello(relative(me, r), line)
+    for r in range(1, dp):
+        hello(relative(me, r), line)
+    if all_tensor:
         for k in range(1, tensor):
             hello(me, lax.rem(line + k, tensor))
         pl.semaphore_wait(barrier, dp + tensor - 2)
         return
-    bits = dp.bit_length() - 1
-    for bit in range(bits):
-        hello(flip(me, bit), line)
 
     @pl.when(line > 0)
     def _():
@@ -206,7 +203,7 @@
         hello(me, line + 1)
 
     left, right = jnp.minimum(line, 1), jnp.minimum(tensor - 1 - line, 1)
-    pl.semaphore_wait(barrier, bits + left + right)
+    pl.semaphore_wait(barrier, dp - 1 + left + right)
 
 
 def orders_of(dp):
@@ -241,14 +238,10 @@
     def __init__(self, sems):
         self.ids = [sems.take() for _ in range(self.COUNT)]
 
-    def bind(self, me, other, parts, landing, send_sem, recv_sem):
-        self.me, self.other, self.parts, self.landing = me, other, parts, landing
+    def bind(self, me, other, view, landing, send_sem, recv_sem):
+        self.me, self.other, self.view, self.landing = me, other, view, landing
         self.send_sem, self.recv_sem = send_sem, recv_sem
-        self.half = parts.shape[-1] // 2
         return self
-
-    def view(self, r, h):
-        return self.parts.at[r, :, pl.ds(h * self.half, self.half)]
 
     def copy(self, slot):
         r, h, bit = [(2, 0, 2), (3, 0, 2), (1, 0, 1), (1, 1, 1), (3, 1, 1), (2, 1, 2)][slot]
@@ -287,6 +280,11 @@
             self.copy(slot).wait_send()
 
 
+def halves_of(parts):
+    half = parts.shape[-1] // 2
+    return lambda r, h: parts.at[r, :, pl.ds(h * half, half)]
+
+
 class LineReduce:
     def __init__(self, sems, size):
         self.size = size
@@ -383,134 +381,6 @@
         + 2 * ((r % 2) * (1 - 2 * (lax.div(me, 2) % 2)))
         + 4 * (lax.div(r, 2) * (1 - 2 * (lax.div(me, 4) % 2)))
     )
-
-
-def first_call(dp, tensor, arrays):
-    grad_out, crossed_out, act, crossed_act, slope, attn, crossed_attn, w_fc2 = arrays
-    tokens, width = grad_out.shape
-    units = act.shape[1]
-    local = attn.shape[1]
-    part = width // dp
-    chips = dp // 2
-    sems = Sems()
-    reduce_fc2, reduce_dense = ChipReduce(sems), ChipReduce(sems)
-    swap_at = sems.take()
-
-    def kernel(
-        c_ref, cx_ref, a_ref, ax_ref, d_ref, t_ref, tx_ref, w2_ref,
-        gp_ref, gpx_ref, sum_ref, s2_out, sd_out,
-        c_buf, cx_buf, a_buf, ax_buf, t_buf, tx_buf, w2_buf, d_buf,
-        s2, sd, r2, rd, send_sem, recv_sem, local_sem,
-    ):
-        me, line = lax.axis_index("dp"), lax.axis_index("tensor")
-
-        def cols(a):
-            return pl.ds(pl.multiple_of(a * part, part), part)
-
-        pair = (send_sem, recv_sem)
-        fc2 = reduce_fc2.bind(me, line, s2, r2, *pair)
-        dense = reduce_dense.bind(me, line, sd, rd, *pair)
-        loads = [
-            pltpu.make_async_copy(a, b, local_sem.at[k])
-            for k, (a, b) in enumerate([
-                (c_ref, c_buf), (cx_ref, cx_buf), (a_ref, a_buf), (ax_ref, ax_buf),
-                (t_ref, t_buf), (tx_ref, tx_buf), (w2_ref, w2_buf), (d_ref, d_buf),
-            ])
-        ]
-        for copy in loads:
-            copy.start()
-        greet(dp, me, tensor, line)
-        for copy in loads[:4]:
-            copy.wait()
-
-        def weight_grad(target, plan, own, crossed, size, step):
-            @pl.loop(0, chips)
-            def _(i):
-                r = chips - 1 - i
-                slot = chip_slot(me, r)
-
-                @pl.loop(0, size, step=step)
-                def _(n):
-                    at = pl.ds(pl.multiple_of(n, step), step)
-                    value = dot_tn(c_buf[:, cols(slot)], own[:, at])
-                    value = value + dot_tn(cx_buf[r], crossed[:, at])
-                    target[r, :, at] = value.astype(bf16)
-
-                for k in range(1, chips):
-
-                    @pl.when(r == k)
-                    def _():
-                        plan.start(k)
-
-        weight_grad(s2, fc2, a_buf, ax_buf, units, 1024)
-        for copy in loads[4:6]:
-            copy.wait()
-        weight_grad(sd, dense, t_buf, tx_buf, local, local)
-        for copy in loads[6:]:
-            copy.wait()
-
-        @pl.loop(0, units, step=512)
-        def _(n):
-            at = pl.ds(pl.multiple_of(n, 512), 512)
-            value = dot_nt(c_buf[...], w2_buf[at, :]) * d_buf[:, at].astype(f32)
-            value = value.astype(bf16)
-            d_buf[:, at] = value
-            sum_ref[0:1, at] = jnp.sum(value.astype(f32), 0, keepdims=True)
-
-        store = pltpu.make_async_copy(d_buf, gp_ref, local_sem.at[len(loads)])
-        store.start()
-        cross = pltpu.make_async_remote_copy(
-            src_ref=d_buf, dst_ref=gpx_ref,
-            send_sem=send_sem.at[swap_at], recv_sem=recv_sem.at[swap_at],
-            device_id=(flip(me, 0), line), device_id_type=MESH)
-        cross.start()
-        fc2.middle()
-        dense.middle()
-        fc2.final()
-        dense.final()
-        store2 = pltpu.make_async_copy(s2.at[0], s2_out, local_sem.at[len(loads) + 1])
-        stored = pltpu.make_async_copy(sd.at[0], sd_out, local_sem.at[len(loads) + 2])
-        store2.start()
-        stored.start()
-        cross.wait()
-        for plan in (fc2, dense):
-            plan.finish()
-        for copy in (store, store2, stored):
-            copy.wait()
-
-    return pl.pallas_call(
-        kernel,
-        out_shape=(
-            jax.ShapeDtypeStruct((tokens, units), bf16),
-            jax.ShapeDtypeStruct((tokens, units), bf16),
-            jax.ShapeDtypeStruct((8, units), f32),
-            jax.ShapeDtypeStruct((part, units), bf16),
-            jax.ShapeDtypeStruct((part, local), bf16),
-        ),
-        in_specs=[ANY] * 8,
-        out_specs=(ANY, ANY, VMEM, ANY, ANY),
-        scratch_shapes=[
-            pltpu.VMEM((tokens, width), bf16),
-            pltpu.VMEM((chips, tokens, part), bf16),
-            pltpu.VMEM((tokens, units), bf16),
-            pltpu.VMEM((tokens, units), bf16),
-            pltpu.VMEM((tokens, local), bf16),
-            pltpu.VMEM((tokens, local), bf16),
-            pltpu.VMEM((units, width), bf16),
-            pltpu.VMEM((tokens, units), bf16),
-            pltpu.VMEM((chips, part, units), bf16),
-            pltpu.VMEM((chips, part, local), bf16),
-            pltpu.VMEM((6, part, units // 2), bf16),
-            pltpu.VMEM((6, part, local // 2), bf16),
-            pltpu.SemaphoreType.DMA((sems.count,)),
-            pltpu.SemaphoreType.DMA((sems.count,)),
-            pltpu.SemaphoreType.DMA((12,)),
-        ],
-        compiler_params=pltpu.CompilerParams(
-            collective_id=1, has_side_effects=True, vmem_limit_bytes=VMEM_LIMIT
-        ),
-        name="first_back",
-    )(*arrays)
 
 
 def second_call(dp, tensor, arrays):
@@ -539,8 +409,8 @@
             return pl.ds(pl.multiple_of(a * part, part), part)
 
         pair = (send_sem, recv_sem)
-        fc1 = reduce_fc1.bind(me, line, s1, r1, *pair)
-        qkv = reduce_qkv.bind(me, line, sq, rq, *pair)
+        fc1 = reduce_fc1.bind(me, line, halves_of(s1), r1, *pair)
+        qkv = reduce_qkv.bind(me, line, halves_of(sq), rq, *pair)
         ins = line_in.bind(line, me, lambda d: gn.at[pl.ds(d * rows, rows), :], rz, *pair)
 
         def remote(k, source, target, device):
@@ -580,7 +450,7 @@
         late = 2 + 4 * tiles
         for copy in loads:
             copy.start()
-        greet(dp, me, tensor, line, wide=True)
+        greet(dp, me, tensor, line, True)
         for copy in bias_tells:
             copy.start()
         for copy in loads[:late]:
@@ -880,8 +750,33 @@
     for i, (low, high, at) in enumerate(spans_of(length)[0]):
         keys = lax.broadcasted_iota(jnp.int32, (high - low, BLOCK), 0) + low
         queries = lax.broadcasted_iota(jnp.int32, (high - low, BLOCK), 1) + i * BLOCK
-        same = segc_ref[low:high, :] == segr_ref[:, i * BLOCK : (i + 1) * BLOCK]
+        own = segr_ref[:, i * BLOCK : (i + 1) * BLOCK].astype(f32)
+        same = segc_ref[low:high, 0:1].astype(f32) == own
         mask_ref[at : at + high - low, :] = jnp.where((keys <= queries) & same, 0.0, -1e30)
+
+
+def fill_tables(seg_ref, column_ref, cos_ref, slo_ref, shi_ref):
+    length = seg_ref.shape[1]
+    row = seg_ref[...].astype(f32)
+    column_ref[...] = jnp.broadcast_to(row, (128, length)).T
+    starts = [jnp.sum(jnp.where(row < number, 1.0, 0.0), 1, keepdims=True) for number in range(1, 4)]
+    lane = lax.broadcasted_iota(jnp.int32, (1, 128), 1) % HD
+    exponent = (2 * (lane % (ROT // 2))).astype(f32) / ROT
+    frequency = 1.0 / jnp.exp(exponent * f32(9.210340371976184))
+
+    @pl.loop(0, length, step=128)
+    def _(r):
+        at = pl.ds(pl.multiple_of(r, 128), 128)
+        column = column_ref[at, :]
+        start = jnp.zeros_like(column)
+        for number in range(1, 4):
+            start = jnp.where(column == number, starts[number - 1], start)
+        index = (lax.broadcasted_iota(jnp.int32, (128, 128), 0) + r).astype(f32)
+        angle = (index - start) * frequency
+        cosine, sine = jnp.cos(angle), jnp.sin(angle)
+        cos_ref[at, :] = jnp.where(lane < ROT, cosine, 1.0)
+        slo_ref[at, :] = jnp.where(lane < ROT // 2, -sine, 0.0)
+        shi_ref[at, :] = jnp.where((lane >= ROT // 2) & (lane < ROT), sine, 0.0)
 
 
 def attend_back_pair(query, key, value, grad, result, probs_of, tables, kacc_ref, vacc_ref, write):
@@ -939,18 +834,20 @@
     stored = spans_of(tokens)[1]
     sems = Sems()
     orders = orders_of(dp)
-    plan_vec = CubeGather(sems, orders[:1])
+    vec_ids = [sems.take() for _ in range(dp - 1)]
     plan_qkv, plan_dense, plan_fc1, plan_fc2 = (CubeGather(sems, orders) for _ in range(4))
     plan_n, plan_c = LineGather(sems, tensor, 2), LineGather(sems, tensor, 2)
     line_out = LineReduce(sems, tensor)
-    swaps = [sems.take() for _ in range(2 * chips + 3)]
+    reduce_fc2, reduce_dense = ChipReduce(sems), ChipReduce(sems)
+    swaps = [sems.take() for _ in range(2 * chips + 4)]
 
     def kernel(
         x_ref, c_ref, wq_ref, wd_ref, w1_ref, w2_ref, vec_ref,
-        qb_ref, fb_ref, cos_ref, slo_ref, shi_ref, segc_ref, segr_ref,
-        out_ref, gq_ref, g1_ref, g2_ref, n_out, nx_out, c_out, cx_out, a_out, ax_out, d_out,
-        t_out, tx_out, dq_out, dqx_out, gvec_ref, qsum_ref,
-        x_buf, vec_buf, nv, wa, wb, wd, act, slope, qkv3, attn, pb, mask, g_buf, kacc, vacc, rz,
+        qb_ref, fb_ref, seg_ref,
+        out_ref, gq_ref, g1_ref, g2_ref, n_out, nx_out, c_out, cx_out, ax_out, d_out,
+        tx_out, dq_out, dqx_out, gp_out, gpx_out, s2_out, sd_out, gvec_ref, qsum_ref, sum_ref,
+        x_buf, vec_buf, nv, wa, wb, wd, act, slope, qkv3, attn, pb, mask, g_buf, kacc, vacc,
+        cos_ref, slo_ref, shi_ref, rz, r2, rd,
         send_sem, recv_sem, local_sem,
     ):
         me, line = lax.axis_index("dp"), lax.axis_index("tensor")
@@ -984,7 +881,13 @@
                 device_id=(twin, line), device_id_type=MESH)
 
         pair = (send_sem, recv_sem)
-        vec = plan_vec.bind(me, line, lambda h: vec_ref, lambda a, h: vec_buf.at[:, cols(a)], *pair)
+        vec = [
+            pltpu.make_async_remote_copy(
+                src_ref=vec_ref, dst_ref=vec_buf.at[:, cols(me)],
+                send_sem=send_sem.at[k], recv_sem=recv_sem.at[k],
+                device_id=(relative(me, r), line), device_id_type=MESH)
+            for r, k in enumerate(vec_ids, 1)
+        ]
         qkv = plan_qkv.bind(
             me, line,
             lambda h: wq_ref.at[:, pl.ds(h * half, half), :],
@@ -1008,26 +911,35 @@
         outs = line_out.bind(line, me, lambda d: nv.at[pl.ds(d * rows, rows), :], rz, *pair)
         stages = dp.bit_length() - 1
 
-        keeps = [
+        takes = [
             copy_of(x_ref, x_buf),
             copy_of(vec_ref, vec_buf.at[:, cols(me)]),
-            copy_of(wq_ref, gq_ref.at[:, cols(me), :]),
-            copy_of(w1_ref, g1_ref.at[cols(me), :]),
             copy_of(wd_ref, wd.at[:, cols(me)]),
-            copy_of(w2_ref, g2_ref.at[:, cols(me)]),
-            copy_of(c_ref, c_out.at[block(line), :]),
+            copy_of(wq_ref, qkv3.at[:, pl.ds(0, part), :]),
+            copy_of(w1_ref, act.at[pl.ds(0, part), :]),
+            copy_of(c_ref, act.at[pl.ds(part, rows), :]),
+            copy_of(w2_ref, wb.at[:, pl.ds(0, part)]),
         ]
-        keeps[0].start()
-        greet(dp, me, tensor, line)
-        vec.start()
+        keeps = [
+            copy_of(qkv3.at[:, pl.ds(0, part), :], gq_ref.at[:, cols(me), :]),
+            copy_of(act.at[pl.ds(0, part), :], g1_ref.at[cols(me), :]),
+            copy_of(act.at[pl.ds(part, rows), :], c_out.at[block(line), :]),
+            copy_of(wb.at[:, pl.ds(0, part)], g2_ref.at[:, cols(me)]),
+        ]
+        for copy in takes[:2]:
+            copy.start()
+        greet(dp, me, tensor, line, False)
+        for copy in vec:
+            copy.start()
         qkv.start()
         cot.start(0)
-        for copy in keeps[1:]:
+        for copy in takes[2:]:
             copy.start()
-        for j in range(stages):
-            vec.advance(j)
-        keeps[0].wait()
-        keeps[1].wait()
+        fill_tables(seg_ref, kacc, cos_ref, slo_ref, shi_ref)
+        for copy in takes[:2]:
+            copy.wait()
+        for copy in vec:
+            copy.wait_recv()
 
         @pl.loop(0, rows, step=32)
         def _(r):
@@ -1043,13 +955,16 @@
         gvec_ref[...] = vec_buf[...]
         qkv.advance(0)
         fc1.start()
-        fill_mask(mask, segc_ref, segr_ref, tokens)
+        for take, copy in zip(takes[3:], keeps):
+            take.wait()
+            copy.start()
+        fill_mask(mask, kacc, seg_ref, tokens)
 
         def project(b):
             at = block(b)
             cosine, slo, shi = cos_ref[at, :], slo_ref[at, :], shi_ref[at, :]
             for i in range(3):
-                value = dot_nn(nv[at, :], wa[:, i * local : (i + 1) * local]) + qb_ref[i : i + 1, :]
+                value = dot_nn(nv[at, :], wa[:, i * local : (i + 1) * local]) + qb_ref[i : i + 1, :].astype(f32)
                 if i == 2:
                     qkv3[2, at, :] = value.astype(bf16)
                     continue
@@ -1066,7 +981,7 @@
             @pl.loop(0, units, step=512)
             def _(n):
                 to = pl.ds(pl.multiple_of(n, 512), 512)
-                pre = dot_nn(nv[at, :], wb[:, to]) + fb_ref[0:1, to]
+                pre = dot_nn(nv[at, :], wb[:, to]) + fb_ref[0:1, to].astype(f32)
                 square = pre * pre
                 bend = jnp.tanh(0.7978845608028654 * pre * (1.0 + 0.044715 * square))
                 act[at, to] = (0.5 * pre * (1.0 + bend)).astype(bf16)
@@ -1075,12 +990,21 @@
                     0.5 * (1.0 + bend) + 0.5 * pre * (1.0 - bend * bend) * rise
                 ).astype(bf16)
 
+        def blocks_of(s, task):
+            @pl.loop(0, 2)
+            def _(way):
+                b = line + (2 * way - 1) * (1 + s)
+
+                @pl.when((b >= 0) & (b < tensor) & ((s >= 0) | (way == 0)))
+                def _():
+                    task(b)
+
         norm.advance(0, 0)
         for j in range(1, stages - 1):
             qkv.advance(j)
         norm.advance(0, 1)
         qkv.advance(stages - 1)
-        keeps[2].wait()
+        keeps[0].wait()
         load_q = [
             copy_of(gq_ref.at[i], wa.at[:, pl.ds(i * local, local)]) for i in range(3)
         ]
@@ -1092,68 +1016,46 @@
         for copy in load_q:
             copy.wait()
 
-        @pl.loop(0, 4)
-        def _(i):
-            s = i - 1
-
-            @pl.when(i == 2)
+        @pl.loop(-1, tensor - 2)
+        def _(s):
+            @pl.when(s == tensor - 3)
             def _():
-                norm.advance(1, 0)
-                norm.advance(1, 1)
+                norm.advance(tensor - 3, 0)
+                norm.advance(tensor - 3, 1)
                 cot.start(1)
-
-            @pl.when(i == 3)
-            def _():
-                for j in range(1, stages):
-                    fc1.advance(j)
-                dense.advance(0)
-                norm.advance(2, 0)
-                norm.advance(2, 1)
-
-            @pl.loop(0, 2)
-            def _(way):
-                b = line + (2 * way - 1) * (1 + s)
-
-                @pl.when((b >= 0) & (b < tensor) & ((i > 0) | (way == 0)))
-                def _():
-                    project(b)
-
-        keeps[3].wait()
+                cot.advance(0, 0)
+
+            blocks_of(s, project)
+
+        for j in range(1, stages):
+            fc1.advance(j)
+        dense.advance(0)
+        for copy in keeps[1:]:
+            copy.wait()
         load_1 = copy_of(g1_ref, wb)
         load_1.start()
+        load_1.wait()
+
+        @pl.loop(-1, tensor - 1)
+        def _(s):
+            @pl.when(s == tensor - 2)
+            def _():
+                norm.advance(tensor - 2, 0)
+                norm.advance(tensor - 2, 1)
+                fc2.advance(0)
+                blocks_of(tensor - 2, project)
+
+            blocks_of(s, hidden_layer)
+
         n_store = copy_of(nv, n_out)
         n_store.start()
         cross_n = [
             to_twin(r, nv.at[:, cols(relative(twin, r << 1))], nx_out.at[r]) for r in range(chips)
         ]
-        for copy in cross_n:
+        store_d = copy_of(slope, d_out)
+        cross_a = to_twin(chips, act, ax_out)
+        for copy in cross_n + [store_d, cross_a]:
             copy.start()
-        fc2.advance(0)
-        cot.advance(0, 0)
-        load_1.wait()
-
-        @pl.loop(0, tensor)
-        def _(b):
-            hidden_layer(b)
-
-            @pl.when(b == 1)
-            def _():
-                cot.advance(0, 1)
-                for j in range(1, stages - 1):
-                    dense.advance(j)
-
-        for j in range(1, stages - 1):
-            fc2.advance(j)
-        stores = [copy_of(act, a_out), copy_of(slope, d_out)]
-        cross_a = to_twin(chips, act, ax_out)
-        for copy in stores + [cross_a]:
-            copy.start()
-        dense.advance(stages - 1)
-        fc2.advance(stages - 1)
-        keeps[4].wait()
-        keeps[5].wait()
-        load_2 = copy_of(g2_ref, wa)
-        load_2.start()
 
         @pl.loop(0, pairs)
         def _(h):
@@ -1168,20 +1070,30 @@
             attend_pair(
                 qkv3[0, :, lanes], qkv3[1, :, lanes], qkv3[2, :, lanes], mask, keep, write)
 
+            @pl.when(h == 0)
+            def _():
+                for j in range(1, stages - 1):
+                    dense.advance(j)
+
             @pl.when(h == 1)
             def _():
-                cot.advance(1, 0)
+                cot.advance(0, 1)
 
         cross_t = to_twin(chips + 1, attn, tx_out)
-        stores.append(copy_of(attn, t_out))
-        stores[-1].start()
         cross_t.start()
-        cot.advance(1, 1)
-        load_2.wait()
+        for j in range(1, stages - 1):
+            fc2.advance(j)
+        dense.advance(stages - 1)
+        fc2.advance(stages - 1)
+        takes[2].wait()
+        load_2 = copy_of(g2_ref, wa)
+        load_2.start()
+        cot.advance(1, 0)
         norm.finish()
         n_store.wait()
         for copy in cross_n:
             copy.wait_send()
+        load_2.wait()
         upper = lax.div(line, tensor // 2)
 
         @pl.loop(0, tensor)
@@ -1202,22 +1114,85 @@
                     outs.start(0, k)
                     outs.start(1, k)
 
+            @pl.when(i == tensor - 2)
+            def _():
+                cot.advance(1, 1)
+
+        store_d.wait()
+        cross_a.wait_recv()
+        cross_t.wait_recv()
+        load_ax = copy_of(ax_out, slope)
+        load_tx = copy_of(tx_out, wb.at[pl.ds(tokens, tokens), pl.ds(width // 2, local)])
+        load_ax.start()
+        load_tx.start()
         cot.advance(2, 0)
         outs.advance(1, add_into)
         cot.advance(2, 1)
-        keeps[6].wait()
         grad = wa.at[pl.ds(0, tokens), :]
         load_c = copy_of(c_out, grad)
-        load_c.start()
         cross_c = [
             to_twin(chips + 2 + r, c_out.at[:, cols(relative(twin, r << 1))], cx_out.at[r])
             for r in range(chips)
         ]
         for copy in cross_c:
             copy.start()
+        load_c.start()
         load_c.wait()
         g_buf[...] = dot_nt(grad[...], wd[...]).astype(bf16)
-        outs.advance(2, add_into)
+        load_cx = [
+            copy_of(cx_out.at[r], wb.at[pl.ds(tokens, tokens), pl.ds(r * part, part)])
+            for r in range(chips)
+        ]
+        for crossed, copy in zip(cross_c, load_cx):
+            crossed.wait_recv()
+            copy.start()
+        for copy in load_cx + [load_ax, load_tx]:
+            copy.wait()
+
+        def weight_grad(left, spot, plan, own, crossed, size, step):
+            @pl.loop(0, chips)
+            def _(i):
+                r = chips - 1 - i
+                slot = chip_slot(me, r)
+
+                @pl.loop(0, size, step=step)
+                def _(n):
+                    at = pl.multiple_of(n, step)
+                    value = dot_tn(left[:, cols(slot)], own(at))
+                    crossed_left = wb[pl.ds(tokens, tokens), pl.ds(pl.multiple_of(r * part, part), part)]
+                    value = value + dot_tn(crossed_left, crossed(at))
+                    spot(r, at, value.astype(bf16))
+
+                for k in range(1, chips):
+
+                    @pl.when(r == k)
+                    def _():
+                        plan.start(k)
+
+        def spot_2(r, at, value):
+            wa[pl.ds(pl.multiple_of(tokens + r * part, part), part), pl.ds(at, 1024)] = value
+
+        def spot_d(r, at, value):
+            wb[pl.ds(pl.multiple_of(r * part, part), part), pl.ds(3 * local, local)] = value
+
+        sum_2 = reduce_fc2.bind(
+            me, line,
+            lambda r, h: wa.at[pl.ds(tokens + r * part, part), pl.ds(h * (units // 2), units // 2)],
+            r2, *pair)
+        sum_d = reduce_dense.bind(
+            me, line,
+            lambda r, h: wb.at[pl.ds(r * part, part), pl.ds(3 * local + h * (local // 2), local // 2)],
+            rd, *pair)
+        weight_grad(
+            grad, spot_2, sum_2, lambda at: act[:, pl.ds(at, 1024)],
+            lambda at: slope[:, pl.ds(at, 1024)], units, 1024)
+        weight_grad(
+            grad, spot_d, sum_d, lambda at: attn[...],
+            lambda at: wb[pl.ds(tokens, tokens), pl.ds(width // 2, local)], local, local)
+        sum_2.middle()
+        cross_a.wait_send()
+        load_d = copy_of(d_out, act)
+        load_d.start()
         qsum_ref[...] = jnp.zeros_like(qsum_ref)
 
         @pl.loop(0, pairs)
@@ -1234,11 +1209,43 @@
             for k in range(3):
                 qsum_ref[k : k + 1, lanes] = sums[k]
 
+            @pl.when(h == 0)
+            def _():
+                outs.advance(2, add_into)
+
+            @pl.when(h == 2)
+            def _():
+                sum_d.middle()
+
+        slabs = width // BLOCK
+        load_w = [
+            copy_of(g2_ref.at[:, pl.ds(e * BLOCK, BLOCK)], pb.at[e, pl.ds(0, units), :])
+            for e in range(slabs)
+        ]
+        for copy in load_w:
+            copy.start()
         back = wb.at[pl.ds(0, tokens), pl.ds(0, 3 * local)]
-        stores.append(copy_of(back, dq_out))
-        stores[-1].start()
+        store_q = copy_of(back, dq_out)
+        store_q.start()
         cross_d = to_twin(2 * chips + 2, back, dqx_out)
         cross_d.start()
+        for copy in load_w:
+            copy.wait()
+        load_d.wait()
+
+        @pl.loop(0, units, step=512)
+        def _(n):
+            at = pl.ds(pl.multiple_of(n, 512), 512)
+            weight = jnp.concatenate([pb[e, at, :] for e in range(slabs)], 1)
+            value = dot_nt(grad[...], weight) * act[:, at].astype(f32)
+            value = value.astype(bf16)
+            act[:, at] = value
+            sum_ref[0:1, at] = jnp.sum(value.astype(f32), 0, keepdims=True)
+
+        store_p = copy_of(act, gp_out)
+        store_p.start()
+        cross_p = to_twin(2 * chips + 3, act, gpx_out)
+        cross_p.start()
         outs.arrive()
 
         @pl.loop(0, rows, step=32)
@@ -1248,16 +1255,21 @@
             total = x_buf[at, :].astype(f32) + outs.total(nv[own, :], at) + vec_buf[2:3, :]
             x_buf[at, :] = total.astype(bf16)
 
-        stores.append(copy_of(x_buf, out_ref))
-        stores[-1].start()
-        crossed = cross_n + [cross_a, cross_t] + cross_c + [cross_d]
-        for copy in crossed:
+        store_o = copy_of(x_buf, out_ref)
+        store_o.start()
+        sum_2.final()
+        sum_d.final()
+        store_2 = copy_of(wa.at[pl.ds(tokens, part), :], s2_out)
+        store_dense = copy_of(wb.at[pl.ds(0, part), pl.ds(3 * local, local)], sd_out)
+        store_2.start()
+        store_dense.start()
+        for copy in cross_n + [cross_d, cross_p]:
             copy.wait_recv()
-        for copy in crossed[chips:]:
+        for copy in vec + [cross_t] + cross_c + [cross_d, cross_p]:
             copy.wait_send()
-        for plan in (vec, qkv, fc1, dense, fc2, cot, outs):
+        for plan in (qkv, fc1, dense, fc2, cot, outs, sum_2, sum_d):
             plan.finish()
-        for copy in stores:
+        for copy in (store_q, store_p, store_o, store_2, store_dense):
             copy.wait()
 
     def shape(*dims):
@@ -1276,16 +1288,19 @@
             shape(chips, tokens, part),
             shape(tokens, units),
             shape(tokens, units),
-            shape(tokens, units),
-            shape(tokens, local),
             shape(tokens, local),
             shape(tokens, 3 * local),
             shape(tokens, 3 * local),
+            shape(tokens, units),
+            shape(tokens, units),
+            shape(part, units),
+            shape(part, local),
             jax.ShapeDtypeStruct((8, width), f32),
             jax.ShapeDtypeStruct((8, local), f32),
+            jax.ShapeDtypeStruct((8, units), f32),
         ),
-        in_specs=[ANY] * 7 + [VMEM] * 7,
-        out_specs=(ANY,) * 15 + (VMEM,) * 2,
+        in_specs=[ANY] * 7 + [VMEM] * 3,
+        out_specs=(ANY,) * 17 + (VMEM,) * 3,
         scratch_shapes=[
             pltpu.VMEM((rows, width), bf16),
             pltpu.VMEM((8, width), f32),
@@ -1300,18 +1315,69 @@
             pltpu.VMEM((local // HD, stored, BLOCK), bf16),
             pltpu.VMEM((stored, BLOCK), f32),
             pltpu.VMEM((tokens, local), bf16),
-            pltpu.VMEM((tokens, 128), f32),
-            pltpu.VMEM((tokens, 128), f32),
+        ]
+        + [pltpu.VMEM((tokens, 128), f32)] * 5
+        + [
             pltpu.VMEM((2 * tensor - 3, rows, width), bf16),
+            pltpu.VMEM((6, part, units // 2), bf16),
+            pltpu.VMEM((6, part, local // 2), bf16),
             pltpu.SemaphoreType.DMA((sems.count,)),
             pltpu.SemaphoreType.DMA((sems.count,)),
-            pltpu.SemaphoreType.DMA((24,)),
+            pltpu.SemaphoreType.DMA((48,)),
         ],
         compiler_params=pltpu.CompilerParams(
             collective_id=0, has_side_effects=True, vmem_limit_bytes=VMEM_LIMIT
         ),
         name="forward",
     )(*arrays)
+
+
+def finish_kernel(s2_ref, sd_ref, s1_ref, sq_ref, o_ref, h_ref, w2_ref, wd_ref, w1_ref, wq_ref, out_ref, hid_ref):
+    w2_ref[...] = s2_ref[...].T.astype(f32)
+    wd_ref[...] = sd_ref[...].T.astype(f32)
+    w1_ref[...] = s1_ref[...].astype(f32)
+    local = wq_ref.shape[2]
+    for i in range(3):
+        wq_ref[i] = sq_ref[:, i * local : (i + 1) * local].astype(f32)
+    out_ref[...] = o_ref[...]
+    hid_ref[...] = h_ref[...]
+
+
+def finish(sent_fc2, sent_dense, sent_fc1, sent_qkv, out, hidden_grad):
+    part, units = sent_fc2.shape
+    local = sent_dense.shape[1]
+    rows, width = out.shape
+    steps = 4
+
+    def down(n, m):
+        return pl.BlockSpec((n // steps, m), lambda i: (i, 0))
+
+    def across(n, m):
+        return pl.BlockSpec((n, m // steps), lambda i: (0, i))
+
+    return pl.pallas_call(
+        finish_kernel,
+        grid=(steps,),
+        out_shape=(
+            jax.ShapeDtypeStruct((units, part), f32),
+            jax.ShapeDtypeStruct((local, part), f32),
+            jax.ShapeDtypeStruct((part, units), f32),
+            jax.ShapeDtypeStruct((3, part, local), f32),
+            jax.ShapeDtypeStruct((rows, width), bf16),
+            jax.ShapeDtypeStruct((rows, width), bf16),
+        ),
+        in_specs=[
+            across(part, units), across(part, local), down(part, units), down(part, 3 * local),
+            down(rows, width), down(rows, width),
+        ],
+        out_specs=(
+            down(units, part), down(local, part), down(part, units),
+            pl.BlockSpec((3, part // steps, local), lambda i: (0, i, 0)),
+            down(rows, width), down(rows, width),
+        ),
+        compiler_params=pltpu.CompilerParams(vmem_limit_bytes=VMEM_LIMIT),
+        name="finish",
+    )(sent_fc2, sent_dense, sent_fc1, sent_qkv, out, hidden_grad)
 
 
 def rotary_tables(segments):
@@ -1344,25 +1410,20 @@
 ):
     seqs = segments.shape[0]
     local = qkv_weight.shape[2]
-    vectors = jnp.stack([ln_gain.astype(f32), ln_bias.astype(f32), dense_bias.astype(f32) + fc2_bias.astype(f32)])
-    vectors = jnp.pad(vectors, ((0, 5), (0, 0)))
+    number = lax.broadcasted_iota(jnp.int32, (8, ln_gain.shape[0]), 0)
+    vectors = jnp.where(number == 1, ln_bias.astype(f32)[None], ln_gain.astype(f32)[None])
+    vectors = jnp.where(
+        number == 2, dense_bias.astype(f32)[None] + fc2_bias.astype(f32)[None], vectors)
     mine = (
         hidden_in, cotangent, qkv_weight.transpose(1, 0, 2),
         dense_weight, fc1_weight, fc2_weight, vectors,
     )
-    tables = rotary_tables(segments)
-    bias = jnp.pad(qkv_bias.astype(f32), ((0, 5), (0, 0)))
     if fast:
         (
-            out, w_qkv, w_fc1, w_fc2, normed, crossed_normed, grad_out, crossed_out,
-            act, crossed_act, slope, attn, crossed_attn, grad_qkv, crossed_qkv, vec, qkv_sums,
-        ) = forward_call(
-            dp, tensor,
-            (*mine, bias, fc1_bias.astype(f32)[None], *tables,
-             segments.reshape(-1, 1), segments.reshape(1, -1)))
-        grad_pre, crossed_pre, fc1_sums, sent_fc2, sent_dense = first_call(
-            dp, tensor,
-            (grad_out, crossed_out, act, crossed_act, slope, attn, crossed_attn, w_fc2))
+            out, w_qkv, w_fc1, _, normed, crossed_normed, _, _, _, _, _,
+            grad_qkv, crossed_qkv, grad_pre, crossed_pre, sent_fc2, sent_dense,
+            vec, qkv_sums, fc1_sums,
+        ) = forward_call(dp, tensor, (*mine, qkv_bias, fc1_bias[None], segments))
         sums = jnp.concatenate([fc1_sums[0].reshape(4, local), qkv_sums[:3], jnp.zeros((1, local), f32)], 0)
         hidden_grad, sent_fc1, sent_qkv, vec_sums, all_sums = second_call(
             dp, tensor,
@@ -1371,21 +1432,25 @@
         quarter = vec_sums.shape[1] // tensor
         at = lax.axis_index("tensor") * quarter
         small = lax.dynamic_slice(vec_sums, (0, at), (3, quarter))
+        grad_w2, grad_wd, grad_w1, grad_wq, out, hidden_grad = finish(
+            sent_fc2, sent_dense, sent_fc1, sent_qkv, out, hidden_grad)
         return (
             out,
             hidden_grad,
             small[0],
             small[1],
-            sent_qkv.astype(f32).reshape(-1, 3, local),
+            grad_wq.transpose(1, 0, 2),
             all_sums[4:7],
-            sent_dense.T.astype(f32),
+            grad_wd,
             small[2],
-            sent_fc1.astype(f32),
+            grad_w1,
             all_sums[:4].reshape(-1),
-            sent_fc2.T.astype(f32),
+            grad_w2,
             small[2],
         )
 
+    tables = rotary_tables(segments)
+    bias = jnp.pad(qkv_bias.astype(f32), ((0, 5), (0, 0)))
     w_qkv, w_dense, w_fc1, w_fc2, normed, grad_out, vec = gather_plain(*mine)
     gain, out_bias = vec[0:1], vec[2:3]
     query, key, value, attn_vec, probs = attend(

time: 391 us -> 321 us (0.82)
  Pallas kernels: 358 us -> 311 us
  other arithmetic: 16.2 us -> 3.35 us
  local copies, waits for them, and re-layouts: 15.5 us -> 5.95 us
    pallas_call x1, Pallas kernels: 51.3 us -> 6.29 us  [finish(): pl.pallas_call(finish_kernel, grid=(steps,), out_shape=(jax.ShapeDtypeStr...]
    unnamed x18 -> x7, local copies, waits for them, and re-layouts: 8.84 us -> 1.12 us
    pallas_call x1, Pallas kernels: 213 us -> 207 us  [forward_call(): pl.pallas_call(kernel, out_shape=(shape(rows, width), shape(3, width, loc...]
    convert_element_type x4 -> x2, other arithmetic: 5.71 us -> 1.31 us  [the longest x1 0.66 us: on_device(): ln_bias.astype(f32)[None]]
    pallas_call x1, Pallas kernels: 93.3 us -> 97.3 us  [second_call(): pl.pallas_call(kernel, out_shape=(jax.ShapeDtypeStruct((rows, width), bf1...]
where the time goes in v4:
time: 321 us
  Pallas kernels  311 us (97%)
  local copies, waits for them, and re-layouts  5.95 us (2%)
  other arithmetic  3.35 us (1%)
    pallas_call x1, Pallas kernels, forward_call(): pl.pallas_call(kernel, out_shape=(shape(rows, width), shape(3, width, loc...  207 us
    pallas_call x1, Pallas kernels, second_call(): pl.pallas_call(kernel, out_shape=(jax.ShapeDtypeStruct((rows, width), bf1...  97.3 us

profile of v4, /device:TPU:0, one launch (start us, length us, event | category | flops | bytes accessed | tf_op | source)
XLA Modules:
  0.0 320.6 jit_solution(1291083862527076250)
XLA Ops:
  0.7 0.7 convert_add_fusion
  1.3 0.7 convert_element_type.14
  2.0 0.7 convert_element_type.15
  2.6 0.7 select_select_fusion.vec_ref
  3.3 1.3 broadcast_in_dim.37.fb_ref
  4.6 207.0 %forward.1 = (bf16[256,2048]{1,0:T(8,128)(2,1)}, bf16[3,2048,512]{2,1,0:T(8,128)(2,1)}, bf16[2048,2048]{1,0:T(8,128)(2,1)}, bf16[2048,2048]{1,0:T(8,128)(2,1)}, ...) custom-call(bf16[256,2048]{1,0:T(8,128)(2,1)} %x_ref.3, ...), custom_call_target="tpu_custom_call" | custom-call | tf_op jit(solution)/shard_map/forward/pallas_call | solution.py:1278
  211.6 0.9 slice_reduce_fusion
  212.5 0.7 slice.23
  213.2 0.1 pad.2.clone
  213.3 0.7 maximum_maximum_fusion.sum_ref
  214.0 97.3 %second_back.1 = (bf16[256,2048]{1,0:T(8,128)(2,1)}, bf16[256,2048]{1,0:T(8,128)(2,1)}, bf16[256,1536]{1,0:T(8,128)(2,1)}, f32[8,256]{1,0:T(8,128)}, f32[8,512]{1,0:T(8,128)}) custom-call(bf16[256,2048]{1,0:T(8,128)(2,1)} %x_ref.3, bf16[256,2048]{1,0:T(8,128)(2,1)} %c_ref.3, f32[8,2048]{1,0:T(8,128)} %get-tuple-element.39.vec_ref, ...), custom_call_target="tpu_custom_call" | custom-call | tf_op jit(solution)/shard_map/second_back/pallas_call | solution.py:566
  311.3 0.0 copy-start
  311.3 6.3 %finish.1 = (f32[2048,256]{1,0:T(8,128)}, f32[512,256]{1,0:T(8,128)}, f32[256,2048]{1,0:T(8,128)}, f32[3,256,512]{2,1,0:T(8,128)}, bf16[256,2048]{1,0:T(8,128)(2,1)}, /*index=5*/bf16[256,2048]{1,0:T(8,128)(2,1)}) custom-call(bf16[256,2048]{1,0:T(8,128)(2,1)} %get-tuple-element.37.s2_ref, bf16[256,512]{1,0:T(8,128)(2,1)} %get-tuple-element.38.sd_ref, ...), custom_call_target="tpu_custom_call" | custom-call | tf_op jit(solution)/shard_map/finish/pallas_call | solution.py:1358
  317.6 0.0 copy-done
  317.6 0.6 copy.25
  318.2 0.8 constant_dynamic-slice_fusion
  319.0 0.5 slice_bitcast_fusion.1
  319.5 0.0 copy-start.1
  319.5 0.6 slice.26
  320.1 0.5 copy.27
  320.6 0.0 copy-done.1
  (3 shorter events, 0.0 us)
Async XLA Ops:
  311.3 6.3 %copy-start = (f32[8,512]{1,0:T(8,128)S(1)}, f32[8,512]{1,0:T(8,128)}, u32[]{:S(2)}) copy-start(f32[8,512]{1,0:T(8,128)} %get-tuple-element.58) | copy-start | bytes 49156
  319.5 1.1 copy-start.1

commit v5 on v4

--- a/solution.py
+++ b/solution.py
@@ -180,30 +180,15 @@
                 self.copy(way, s, u).wait_send()
 
 
-def greet(dp, me, tensor, line, all_tensor):
+def greet(dp, me, tensor, line, meanwhile):
     barrier = pltpu.get_barrier_semaphore()
-
-    def hello(a, b):
-        pl.semaphore_signal(barrier, inc=1, device_id=(a, b), device_id_type=MESH)
-
     for r in range(1, dp):
-        hello(relative(me, r), line)
-    if all_tensor:
-        for k in range(1, tensor):
-            hello(me, lax.rem(line + k, tensor))
-        pl.semaphore_wait(barrier, dp + tensor - 2)
-        return
-
-    @pl.when(line > 0)
-    def _():
-        hello(me, line - 1)
-
-    @pl.when(line < tensor - 1)
-    def _():
-        hello(me, line + 1)
-
-    left, right = jnp.minimum(line, 1), jnp.minimum(tensor - 1 - line, 1)
-    pl.semaphore_wait(barrier, dp - 1 + left + right)
+        pl.semaphore_signal(barrier, inc=1, device_id=(relative(me, r), line), device_id_type=MESH)
+    for k in range(1, tensor):
+        to = (me, lax.rem(line + k, tensor))
+        pl.semaphore_signal(barrier, inc=1, device_id=to, device_id_type=MESH)
+    meanwhile()
+    pl.semaphore_wait(barrier, dp + tensor - 2)
 
 
 def orders_of(dp):
@@ -238,8 +223,9 @@
     def __init__(self, sems):
         self.ids = [sems.take() for _ in range(self.COUNT)]
 
-    def bind(self, me, other, view, landing, send_sem, recv_sem):
+    def bind(self, me, other, view, landing, stage, stage_sem, send_sem, recv_sem):
         self.me, self.other, self.view, self.landing = me, other, view, landing
+        self.stage, self.stage_sem = stage, stage_sem
         self.send_sem, self.recv_sem = send_sem, recv_sem
         return self
 
@@ -259,30 +245,36 @@
         for slot in {3: (1, 4), 2: (0,), 1: (3,), 0: ()}[r]:
             self.copy(slot).start()
 
+    def fetch(self, slots):
+        half = self.landing.shape[-1]
+        held = [self.stage.at[k, :, pl.ds(0, half)] for k in range(len(slots))]
+        copies = []
+        for k, slot in enumerate(slots):
+            self.copy(slot).wait_recv()
+            copies.append(
+                pltpu.make_async_copy(self.landing.at[slot], held[k], self.stage_sem.at[k]))
+            copies[k].start()
+        for copy in copies:
+            copy.wait()
+        return held
+
     def middle(self):
-        for slot, r, h, last in ((1, 1, 0, 2), (4, 2, 1, 5)):
-            self.copy(slot).wait_recv()
+        held = self.fetch((1, 4))
+        for k, (r, h, last) in enumerate(((1, 0, 2), (2, 1, 5))):
             view = self.view(r, h)
-            view[...] = (view[...].astype(f32) + self.landing[slot].astype(f32)).astype(bf16)
+            view[...] = (view[...].astype(f32) + held[k][...].astype(f32)).astype(bf16)
             self.copy(last).start()
 
     def final(self):
-        for h in (0, 1):
-            for slot in ((0, 2), (3, 5))[h]:
-                self.copy(slot).wait_recv()
-            a, b = ((0, 2), (3, 5))[h]
+        for h, slots in ((0, (0, 2)), (1, (3, 5))):
+            a, b = self.fetch(slots)
             view = self.view(0, h)
-            total = view[...].astype(f32) + self.landing[a].astype(f32) + self.landing[b].astype(f32)
+            total = view[...].astype(f32) + a[...].astype(f32) + b[...].astype(f32)
             view[...] = total.astype(bf16)
 
     def finish(self):
         for slot in range(self.COUNT):
             self.copy(slot).wait_send()
-
-
-def halves_of(parts):
-    half = parts.shape[-1] // 2
-    return lambda r, h: parts.at[r, :, pl.ds(h * half, half)]
 
 
 class LineReduce:
@@ -290,8 +282,9 @@
         self.size = size
         self.ids = {(way, i): sems.take() for way in (0, 1) for i in range(size - 1)}
 
-    def bind(self, me, other, own, landing, send_sem, recv_sem):
+    def bind(self, me, other, own, landing, stage, last, stage_sem, send_sem, recv_sem):
         self.me, self.other, self.own, self.landing = me, other, own, landing
+        self.stage, self.last, self.stage_sem = stage, last, stage_sem
         self.send_sem, self.recv_sem = send_sem, recv_sem
         return self
 
@@ -301,12 +294,14 @@
     def place(self, way, i):
         return i if way == 0 else 2 * self.size - 4 - i
 
+    def buffer(self, way, i):
+        return self.stage.at[i if way == 0 else self.size - 2 - i]
+
     def copy(self, way, i, edge):
         k = self.ids[way, i]
-        here = self.landing.at[self.place(way, i)]
         return pltpu.make_async_remote_copy(
-            src_ref=self.own(self.target(way, i)) if edge else here,
-            dst_ref=here,
+            src_ref=self.own(self.target(way, i)) if edge else self.buffer(way, i),
+            dst_ref=self.landing.at[self.place(way, i)],
             send_sem=self.send_sem.at[k],
             recv_sem=self.recv_sem.at[k],
             device_id=(self.other, self.me + 1 if way == 0 else self.me - 1),
@@ -325,7 +320,7 @@
         def _():
             self.copy(way, i, True).start()
 
-    def advance(self, step, add):
+    def advance(self, step):
         for way in (0, 1):
             steps_from_edge = self.me if way == 0 else self.size - 1 - self.me
             for i in range(step):
@@ -333,18 +328,15 @@
                 @pl.when(self.passes(way, i) & (steps_from_edge == step - i))
                 def _():
                     self.copy(way, i, False).wait_recv()
-                    add(self.landing.at[self.place(way, i)], self.own(self.target(way, i)))
+                    held = self.buffer(way, i)
+                    fetch = pltpu.make_async_copy(
+                        self.landing.at[self.place(way, i)], held, self.stage_sem.at[0])
+                    fetch.start()
+                    fetch.wait()
+                    add_into(held, self.own(self.target(way, i)))
                     self.copy(way, i, False).start()
 
     def arrive(self):
-        for way in (0, 1):
-            for i in range(self.size - 1):
-
-                @pl.when(self.me == self.target(way, i))
-                def _():
-                    self.copy(way, i, False).wait_recv()
-
-    def finish(self):
         for way, i in self.ids:
 
             @pl.when(self.edge(way))
@@ -355,15 +347,28 @@
             def _():
                 self.copy(way, i, False).wait_send()
 
+        def fetch(way, i):
+            return pltpu.make_async_copy(
+                self.landing.at[self.place(way, i)], self.last(way), self.stage_sem.at[way])
+
+        for way, i in self.ids:
+
+            @pl.when(self.me == self.target(way, i))
+            def _():
+                self.copy(way, i, False).wait_recv()
+                fetch(way, i).start()
+
+        for way, i in self.ids:
+
+            @pl.when(self.me == self.target(way, i))
+            def _():
+                fetch(way, i).wait()
+
     def total(self, own, rows):
-        last = self.size - 1
         value = own.astype(f32)
-        lefts = jnp.clip(last - self.me, 0, last - 1)
-        rights = jnp.clip(self.me, 0, last - 1)
-        from_left = self.landing[lefts, rows, :].astype(f32)
-        from_right = self.landing[2 * self.size - 4 - rights, rows, :].astype(f32)
-        value = value + jnp.where(self.me > 0, from_left, 0.0)
-        return value + jnp.where(self.me < last, from_right, 0.0)
+        for way, there in ((0, self.me > 0), (1, self.me < self.size - 1)):
+            value = value + jnp.where(there, self.last(way)[rows, :].astype(f32), 0.0)
+        return value
 
 
 def add_into(landing, own):
@@ -381,229 +386,6 @@
         + 2 * ((r % 2) * (1 - 2 * (lax.div(me, 2) % 2)))
         + 4 * (lax.div(r, 2) * (1 - 2 * (lax.div(me, 4) % 2)))
     )
-
-
-def second_call(dp, tensor, arrays):
-    hidden, cotangent, vec, sums, normed, grad_pre, grad_qkv = arrays[:7]
-    rows, width = hidden.shape
-    tokens, units = grad_pre.shape
-    wide = grad_qkv.shape[1]
-    local = wide // 3
-    part = width // dp
-    chips = dp // 2
-    sems = Sems()
-    reduce_fc1, reduce_qkv = ChipReduce(sems), ChipReduce(sems)
-    line_in = LineReduce(sems, tensor)
-    tells = [sems.take() for _ in range(2 * (dp - 1) + tensor - 1)]
-
-    def kernel(
-        x_ref, c_ref, vec_ref, sum_ref, n_ref, gp_in, gq_in, nx_in, gpx_in, gqx_in, wq_ref, w1_ref,
-        hid_ref, s1_out, sq_out, vout_ref, bout_ref,
-        x_buf, c_buf, n_buf, nx_buf, gp, gpx, gq, gqx, wq, w1, gn,
-        s1, sq, r1, rq, rz, parts, tell_v, tell_b, tell_z, send_sem, recv_sem, local_sem,
-    ):
-        me, line = lax.axis_index("dp"), lax.axis_index("tensor")
-        twin = flip(me, 0)
-
-        def cols(a):
-            return pl.ds(pl.multiple_of(a * part, part), part)
-
-        pair = (send_sem, recv_sem)
-        fc1 = reduce_fc1.bind(me, line, halves_of(s1), r1, *pair)
-        qkv = reduce_qkv.bind(me, line, halves_of(sq), rq, *pair)
-        ins = line_in.bind(line, me, lambda d: gn.at[pl.ds(d * rows, rows), :], rz, *pair)
-
-        def remote(k, source, target, device):
-            return pltpu.make_async_remote_copy(
-                src_ref=source, dst_ref=target,
-                send_sem=send_sem.at[k], recv_sem=recv_sem.at[k],
-                device_id=device, device_id_type=MESH)
-
-        def third(i):
-            return pl.ds(i * local, local)
-
-        bias_tells = [
-            remote(tells[r - 1], sum_ref, tell_b.at[r], (relative(me, r), line)) for r in range(1, dp)
-        ]
-        vec_tells = [
-            remote(tells[dp - 2 + r], parts.at[:, cols(relative(me, r))], tell_v.at[r],
-                   (relative(me, r), line))
-            for r in range(1, dp)
-        ]
-        line_tells = [
-            remote(tells[2 * dp - 3 + k], tell_z.at[0], tell_z.at[k],
-                   (me, lax.rem(line + k, tensor)))
-            for k in range(1, tensor)
-        ]
-        tile = 512
-        pieces = (
-            [(gp_in, gp), (gq_in, gq)]
-            + [(w1_ref.at[pl.ds(n, tile), :], w1.at[pl.ds(n, tile), :]) for n in range(0, width, tile)]
-            + [
-                (wq_ref.at[i, pl.ds(n, tile), :], wq.at[pl.ds(n, tile), third(i)])
-                for n in range(0, width, tile) for i in range(3)
-            ]
-            + [(n_ref, n_buf), (nx_in, nx_buf), (gpx_in, gpx), (gqx_in, gqx), (x_ref, x_buf), (c_ref, c_buf)]
-        )
-        loads = [pltpu.make_async_copy(a, b, local_sem.at[k]) for k, (a, b) in enumerate(pieces)]
-        tiles = width // tile
-        late = 2 + 4 * tiles
-        for copy in loads:
-            copy.start()
-        greet(dp, me, tensor, line, True)
-        for copy in bias_tells:
-            copy.start()
-        for copy in loads[:late]:
-            copy.wait()
-        upper = lax.div(line, tensor // 2)
-
-        @pl.loop(0, tensor)
-        def _(i):
-            d = (1 - upper) * (tensor - 1 - i) + upper * i
-            at = pl.ds(pl.multiple_of(d * rows, rows), rows)
-
-            @pl.loop(0, width, step=1024)
-            def _(n):
-                to = pl.ds(pl.multiple_of(n, 1024), 1024)
-                value = dot_nt(gp[at, :], w1[to, :]) + dot_nt(gq[at, :], wq[to, :])
-                gn[at, to] = value.astype(bf16)
-
-            for k in range(tensor - 1):
-
-                @pl.when(i == k)
-                def _():
-                    ins.start(0, k)
-                    ins.start(1, k)
-
-        for copy in loads[late : late + 4]:
-            copy.wait()
-
-        def weight_grad(target, plan, own, crossed, size, step):
-            @pl.loop(0, chips)
-            def _(i):
-                r = chips - 1 - i
-                slot = chip_slot(me, r)
-
-                @pl.loop(0, size, step=step)
-                def _(n):
-                    at = pl.ds(pl.multiple_of(n, step), step)
-                    value = dot_tn(n_buf[:, cols(slot)], own[:, at])
-                    value = value + dot_tn(nx_buf[r], crossed[:, at])
-                    target[r, :, at] = value.astype(bf16)
-
-                for k in range(1, chips):
-
-                    @pl.when(r == k)
-                    def _():
-                        plan.start(k)
-
-        weight_grad(s1, fc1, gp, gpx, units, 1024)
-        ins.advance(1, add_into)
-        weight_grad(sq, qkv, gq, gqx, wide, 768)
-        ins.advance(2, add_into)
-        fc1.middle()
-        for copy in bias_tells:
-            copy.wait_recv()
-        total = sum_ref[...]
-        for r in range(1, dp):
-            total = total + tell_b[r]
-        bout_ref[...] = total
-        for copy in loads[late + 4 :]:
-            copy.wait()
-        qkv.middle()
-        ins.arrive()
-        parts[...] = jnp.zeros_like(parts)
-
-        @pl.loop(0, rows, step=32)
-        def _(r):
-            at = pl.ds(r, 32)
-            x = x_buf[at, :].astype(f32)
-            centred = x - jnp.mean(x, -1, keepdims=True)
-            inv_std = lax.rsqrt(jnp.mean(centred * centred, -1, keepdims=True) + layer_eps)
-            unit = centred * inv_std
-            own = pl.ds(pl.multiple_of(line * rows + r, 32), 32)
-            grad = ins.total(gn[own, :], at)
-            cot = c_buf[at, :].astype(f32)
-            scaled = grad * vec_ref[0:1, :]
-            first = jnp.mean(scaled, -1, keepdims=True)
-            second = jnp.mean(scaled * unit, -1, keepdims=True)
-            c_buf[at, :] = (cot + inv_std * (scaled - first - unit * second)).astype(bf16)
-            parts[0:1, :] += jnp.sum(grad * unit, 0, keepdims=True)
-            parts[1:2, :] += jnp.sum(grad, 0, keepdims=True)
-            parts[2:3, :] += jnp.sum(cot, 0, keepdims=True)
-
-        last = pltpu.make_async_copy(c_buf, hid_ref, local_sem.at[len(loads)])
-        last.start()
-        for copy in vec_tells:
-            copy.start()
-        fc1.final()
-        store1 = pltpu.make_async_copy(s1.at[0], s1_out, local_sem.at[len(loads) + 1])
-        store1.start()
-        for copy in vec_tells:
-            copy.wait_recv()
-        total_v = parts[:, cols(me)]
-        for r in range(1, dp):
-            total_v = total_v + tell_v[r]
-        tell_z[0] = total_v
-        for copy in line_tells:
-            copy.start()
-        qkv.final()
-        storeq = pltpu.make_async_copy(sq.at[0], sq_out, local_sem.at[len(loads) + 2])
-        storeq.start()
-        for copy in line_tells:
-            copy.wait_recv()
-        total_z = tell_z[0]
-        for k in range(1, tensor):
-            total_z = total_z + tell_z[k]
-        vout_ref[...] = total_z
-        for copy in bias_tells + vec_tells + line_tells:
-            copy.wait_send()
-        for plan in (fc1, qkv, ins):
-            plan.finish()
-        for copy in (last, store1, storeq):
-            copy.wait()
-
-    return pl.pallas_call(
-        kernel,
-        out_shape=(
-            jax.ShapeDtypeStruct((rows, width), bf16),
-            jax.ShapeDtypeStruct((part, units), bf16),
-            jax.ShapeDtypeStruct((part, wide), bf16),
-            jax.ShapeDtypeStruct((8, part), f32),
-            jax.ShapeDtypeStruct((8, local), f32),
-        ),
-        in_specs=[ANY] * 2 + [VMEM] * 2 + [ANY] * 8,
-        out_specs=(ANY, ANY, ANY, VMEM, VMEM),
-        scratch_shapes=[
-            pltpu.VMEM((rows, width), bf16),
-            pltpu.VMEM((rows, width), bf16),
-            pltpu.VMEM((tokens, width), bf16),
-            pltpu.VMEM((chips, tokens, part), bf16),
-            pltpu.VMEM((tokens, units), bf16),
-            pltpu.VMEM((tokens, units), bf16),
-            pltpu.VMEM((tokens, wide), bf16),
-            pltpu.VMEM((tokens, wide), bf16),
-            pltpu.VMEM((width, wide), bf16),
-            pltpu.VMEM((width, units), bf16),
-            pltpu.VMEM((tokens, width), bf16),
-            pltpu.VMEM((chips, part, units), bf16),
-            pltpu.VMEM((chips, part, wide), bf16),
-            pltpu.VMEM((6, part, units // 2), bf16),
-            pltpu.VMEM((6, part, wide // 2), bf16),
-            pltpu.VMEM((2 * tensor - 3, rows, width), bf16),
-            pltpu.VMEM((8, width), f32),
-            pltpu.VMEM((dp, 8, part), f32),
-            pltpu.VMEM((dp, 8, local), f32),
-            pltpu.VMEM((tensor, 8, part), f32),
-            pltpu.SemaphoreType.DMA((sems.count,)),
-            pltpu.SemaphoreType.DMA((sems.count,)),
-            pltpu.SemaphoreType.DMA((30,)),
-        ],
-        compiler_params=pltpu.CompilerParams(
-            collective_id=2, has_side_effects=True, vmem_limit_bytes=VMEM_LIMIT
-        ),
-        name="second_back",
-    )(*arrays)
 
 
 def spans_of(length):
@@ -737,7 +519,7 @@
         mine = slice(i * BLOCK, (i + 1) * BLOCK)
         total = jnp.zeros((BLOCK, 128), f32)
         for e in range(128 // HD):
-            scores = dot_nt(only(key[low:high], e), query[mine]) + mask_ref[at : at + high - low, :]
+            scores = dot_nt(only(key[low:high], e), query[mine]) + mask_ref[at : at + high - low, :].astype(f32)
             exponent = jnp.exp(scores - jnp.max(scores, 0, keepdims=True))
             inverse = 1.0 / jnp.sum(exponent, 0, keepdims=True)
             probs = (exponent * inverse).astype(bf16)
@@ -752,7 +534,8 @@
         queries = lax.broadcasted_iota(jnp.int32, (high - low, BLOCK), 1) + i * BLOCK
         own = segr_ref[:, i * BLOCK : (i + 1) * BLOCK].astype(f32)
         same = segc_ref[low:high, 0:1].astype(f32) == own
-        mask_ref[at : at + high - low, :] = jnp.where((keys <= queries) & same, 0.0, -1e30)
+        allowed = jnp.where((keys <= queries) & same, 0.0, -1e30)
+        mask_ref[at : at + high - low, :] = allowed.astype(mask_ref.dtype)
 
 
 def fill_tables(seg_ref, column_ref, cos_ref, slo_ref, shi_ref):
@@ -822,10 +605,11 @@
     return first, jnp.sum(dk.astype(f32), 0, keepdims=True), jnp.sum(dv.astype(f32), 0, keepdims=True)
 
 
-def forward_call(dp, tensor, arrays):
+def block_call(dp, tensor, arrays):
     hidden, cotangent, w_qkv, w_dense, w_fc1, w_fc2, vectors = arrays[:7]
     rows, width = hidden.shape
     local = w_qkv.shape[2]
+    wide = 3 * local
     units = w_fc1.shape[1]
     part = width // dp
     chips = dp // 2
@@ -837,23 +621,26 @@
     vec_ids = [sems.take() for _ in range(dp - 1)]
     plan_qkv, plan_dense, plan_fc1, plan_fc2 = (CubeGather(sems, orders) for _ in range(4))
     plan_n, plan_c = LineGather(sems, tensor, 2), LineGather(sems, tensor, 2)
-    line_out = LineReduce(sems, tensor)
-    reduce_fc2, reduce_dense = ChipReduce(sems), ChipReduce(sems)
+    line_out, line_in = LineReduce(sems, tensor), LineReduce(sems, tensor)
+    reduce_fc2, reduce_dense, reduce_fc1, reduce_qkv = (ChipReduce(sems) for _ in range(4))
     swaps = [sems.take() for _ in range(2 * chips + 4)]
+    tells = [sems.take() for _ in range(2 * (dp - 1) + tensor - 1)]
 
     def kernel(
-        x_ref, c_ref, wq_ref, wd_ref, w1_ref, w2_ref, vec_ref,
-        qb_ref, fb_ref, seg_ref,
-        out_ref, gq_ref, g1_ref, g2_ref, n_out, nx_out, c_out, cx_out, ax_out, d_out,
-        tx_out, dq_out, dqx_out, gp_out, gpx_out, s2_out, sd_out, gvec_ref, qsum_ref, sum_ref,
-        x_buf, vec_buf, nv, wa, wb, wd, act, slope, qkv3, attn, pb, mask, g_buf, kacc, vacc,
-        cos_ref, slo_ref, shi_ref, rz, r2, rd,
-        send_sem, recv_sem, local_sem,
+        x_ref, c_ref, wq_ref, wd_ref, w1_ref, w2_ref, vec_ref, qb_ref, fb_ref, seg_ref,
+        out_ref, hid_ref, s2_out, sd_out, s1_out, sq_out,
+        gq_ref, g1_ref, g2_ref, n_out, nx_out, ax_out, gqx_out, gpx_out,
+        land_out, land_in, land_2, land_d, land_1, land_q, vout_ref, bout_ref,
+        x_buf, vec_buf, nv, wa, wb, wd, act, slope, qkv3, abuf, pb, mask, cbuf, xbuf,
+        kacc, vacc, cos_ref, slo_ref, shi_ref, line_stage, chip_stage,
+        fsum, bsum, parts, tell_v, tell_b, tell_z,
+        send_sem, recv_sem, local_sem, stage_sem,
     ):
         me, line = lax.axis_index("dp"), lax.axis_index("tensor")
         twin = flip(me, 0)
         half = part // 2
         local_count = [0]
+        attn = abuf.at[:, pl.ds(0, local)]
 
         def cols(a):
             return pl.ds(pl.multiple_of(a * part, part), part)
@@ -874,18 +661,18 @@
             local_count[0] += 1
             return pltpu.make_async_copy(a, b, local_sem.at[local_count[0] - 1])
 
-        def to_twin(k, source, target):
+        def remote(k, source, target, device):
             return pltpu.make_async_remote_copy(
                 src_ref=source, dst_ref=target,
-                send_sem=send_sem.at[swaps[k]], recv_sem=recv_sem.at[swaps[k]],
-                device_id=(twin, line), device_id_type=MESH)
+                send_sem=send_sem.at[k], recv_sem=recv_sem.at[k],
+                device_id=device, device_id_type=MESH)
+
+        def to_twin(k, source, target):
+            return remote(swaps[k], source, target, (twin, line))
 
         pair = (send_sem, recv_sem)
         vec = [
-            pltpu.make_async_remote_copy(
-                src_ref=vec_ref, dst_ref=vec_buf.at[:, cols(me)],
-                send_sem=send_sem.at[k], recv_sem=recv_sem.at[k],
-                device_id=(relative(me, r), line), device_id_type=MESH)
+            remote(k, vec_ref, vec_buf.at[:, cols(me)], (relative(me, r), line))
             for r, k in enumerate(vec_ids, 1)
         ]
         qkv = plan_qkv.bind(
@@ -907,35 +694,60 @@
         norm = plan_n.bind(
             line, me, lambda u: nv.at[tok(line, u)], lambda b, u: nv.at[tok(b, u)], *pair)
         cot = plan_c.bind(
-            line, me, lambda u: c_ref.at[piece(rows, u)], lambda b, u: c_out.at[tok(b, u)], *pair)
-        outs = line_out.bind(line, me, lambda d: nv.at[pl.ds(d * rows, rows), :], rz, *pair)
+            line, me, lambda u: c_ref.at[piece(rows, u)], lambda b, u: cbuf.at[tok(b, u)], *pair)
+        staged = (stage_sem, *pair)
+
+        def lasts(way):
+            return wd.at[pl.ds(way * rows, rows), :]
+
+        outs = line_out.bind(
+            line, me, lambda d: nv.at[pl.ds(d * rows, rows), :], land_out, line_stage, lasts, *staged)
+        ins = line_in.bind(
+            line, me, lambda d: act.at[pl.ds(d * rows, rows), :], land_in, line_stage, lasts, *staged)
+        low, high = pl.ds(0, tokens), pl.ds(tokens, tokens)
+        sum_2 = reduce_fc2.bind(
+            me, line,
+            lambda r, h: wa.at[pl.ds(tokens + r * part, part), piece(units, h)],
+            land_2, chip_stage, *staged)
+        sum_d = reduce_dense.bind(
+            me, line,
+            lambda r, h: mask.at[pl.ds((2 * r + h) * part, part), :],
+            land_d, chip_stage, *staged)
+        sum_1 = reduce_fc1.bind(
+            me, line,
+            lambda r, h: wb.at[pl.ds(r * part, part), piece(units, h)],
+            land_1, chip_stage, *staged)
+        sum_q = reduce_qkv.bind(
+            me, line,
+            lambda r, h: abuf.at[pl.ds(r * part, part), piece(wide, h)],
+            land_q, chip_stage, *staged)
         stages = dp.bit_length() - 1
 
         takes = [
             copy_of(x_ref, x_buf),
             copy_of(vec_ref, vec_buf.at[:, cols(me)]),
             copy_of(wd_ref, wd.at[:, cols(me)]),
+            copy_of(c_ref, cbuf.at[block(line), :]),
             copy_of(wq_ref, qkv3.at[:, pl.ds(0, part), :]),
             copy_of(w1_ref, act.at[pl.ds(0, part), :]),
-            copy_of(c_ref, act.at[pl.ds(part, rows), :]),
             copy_of(w2_ref, wb.at[:, pl.ds(0, part)]),
         ]
         keeps = [
             copy_of(qkv3.at[:, pl.ds(0, part), :], gq_ref.at[:, cols(me), :]),
             copy_of(act.at[pl.ds(0, part), :], g1_ref.at[cols(me), :]),
-            copy_of(act.at[pl.ds(part, rows), :], c_out.at[block(line), :]),
             copy_of(wb.at[:, pl.ds(0, part)], g2_ref.at[:, cols(me)]),
         ]
         for copy in takes[:2]:
             copy.start()
-        greet(dp, me, tensor, line, False)
+        greet(
+            dp, me, tensor, line,
+            lambda: fill_tables(seg_ref, kacc, cos_ref, slo_ref, shi_ref))
         for copy in vec:
             copy.start()
         qkv.start()
         cot.start(0)
         for copy in takes[2:]:
             copy.start()
-        fill_tables(seg_ref, kacc, cos_ref, slo_ref, shi_ref)
         for copy in takes[:2]:
             copy.wait()
         for copy in vec:
@@ -952,10 +764,9 @@
 
         norm.start(0)
         norm.start(1)
-        gvec_ref[...] = vec_buf[...]
         qkv.advance(0)
         fc1.start()
-        for take, copy in zip(takes[3:], keeps):
+        for take, copy in zip(takes[4:], keeps):
             take.wait()
             copy.start()
         fill_mask(mask, kacc, seg_ref, tokens)
@@ -964,7 +775,8 @@
             at = block(b)
             cosine, slo, shi = cos_ref[at, :], slo_ref[at, :], shi_ref[at, :]
             for i in range(3):
-                value = dot_nn(nv[at, :], wa[:, i * local : (i + 1) * local]) + qb_ref[i : i + 1, :].astype(f32)
+                value = dot_nn(nv[at, :], wa[:, i * local : (i + 1) * local])
+                value = value + qb_ref[i : i + 1, :].astype(f32)
                 if i == 2:
                     qkv3[2, at, :] = value.astype(bf16)
                     continue
@@ -975,11 +787,15 @@
                         turned = turned * bf16(HD**-0.5)
                     qkv3[i, at, lanes] = turned
 
-        def hidden_layer(b):
+        def hidden_layer(b, first):
             at = block(b)
 
             @pl.loop(0, units, step=512)
             def _(n):
+                @pl.when(first & (n == units // 2))
+                def _():
+                    load_1[1].wait()
+
                 to = pl.ds(pl.multiple_of(n, 512), 512)
                 pre = dot_nn(nv[at, :], wb[:, to]) + fb_ref[0:1, to].astype(f32)
                 square = pre * pre
@@ -989,6 +805,18 @@
                 slope[at, to] = (
                     0.5 * (1.0 + bend) + 0.5 * pre * (1.0 - bend * bend) * rise
                 ).astype(bf16)
+
+        def slope_layer(b):
+            at = block(b)
+            abuf[at, pl.ds(local, local)] = dot_nt(cbuf[at, :], wd[...]).astype(bf16)
+
+            @pl.loop(0, units, step=1024)
+            def _(n):
+                to = pl.ds(pl.multiple_of(n, 1024), 1024)
+                value = dot_nt(cbuf[at, :], wa[to, :]) * slope[at, to].astype(f32)
+                value = value.astype(bf16)
+                slope[at, to] = value
+                fsum[0:1, to] += jnp.sum(value.astype(f32), 0, keepdims=True)
 
         def blocks_of(s, task):
             @pl.loop(0, 2)
@@ -1029,12 +857,12 @@
 
         for j in range(1, stages):
             fc1.advance(j)
-        dense.advance(0)
         for copy in keeps[1:]:
             copy.wait()
-        load_1 = copy_of(g1_ref, wb)
-        load_1.start()
-        load_1.wait()
+        load_1 = [copy_of(g1_ref.at[:, piece(units, h)], wb.at[:, piece(units, h)]) for h in (0, 1)]
+        load_1[0].start()
+        load_1[0].wait()
+        load_1[1].start()
 
         @pl.loop(-1, tensor - 1)
         def _(s):
@@ -1045,64 +873,81 @@
                 fc2.advance(0)
                 blocks_of(tensor - 2, project)
 
-            blocks_of(s, hidden_layer)
+            @pl.when(s == 0)
+            def _():
+                dense.advance(0)
+
+            blocks_of(s, lambda b: hidden_layer(b, s == -1))
 
         n_store = copy_of(nv, n_out)
         n_store.start()
         cross_n = [
             to_twin(r, nv.at[:, cols(relative(twin, r << 1))], nx_out.at[r]) for r in range(chips)
         ]
-        store_d = copy_of(slope, d_out)
         cross_a = to_twin(chips, act, ax_out)
-        for copy in cross_n + [store_d, cross_a]:
+        for copy in cross_n + [cross_a]:
             copy.start()
+
+        def prob_lanes(h, e):
+            return pl.ds(pl.multiple_of((2 * h + e) * BLOCK, BLOCK), BLOCK)
 
         @pl.loop(0, pairs)
         def _(h):
             lanes = pl.ds(pl.multiple_of(h * 128, 128), 128)
 
             def keep(e, at, value):
-                pb[2 * h + e, at, :] = value
+                pb[at, prob_lanes(h, e)] = value
 
             def write(at, value):
-                attn[at, lanes] = value
+                abuf[at, lanes] = value
 
             attend_pair(
                 qkv3[0, :, lanes], qkv3[1, :, lanes], qkv3[2, :, lanes], mask, keep, write)
 
-            @pl.when(h == 0)
-            def _():
+            @pl.when(h == 1)
+            def _():
+                cot.advance(0, 1)
                 for j in range(1, stages - 1):
                     dense.advance(j)
 
-            @pl.when(h == 1)
-            def _():
-                cot.advance(0, 1)
-
-        cross_t = to_twin(chips + 1, attn, tx_out)
+            @pl.when(h == 2)
+            def _():
+                for j in range(1, stages - 1):
+                    fc2.advance(j)
+
+        cross_t = to_twin(chips + 1, attn, xbuf.at[:, pl.ds(chips * part, local)])
         cross_t.start()
-        for j in range(1, stages - 1):
-            fc2.advance(j)
+        cross_a.wait_recv()
+        load_ax = copy_of(ax_out, wb.at[low, :])
+        load_ax.start()
         dense.advance(stages - 1)
         fc2.advance(stages - 1)
         takes[2].wait()
-        load_2 = copy_of(g2_ref, wa)
-        load_2.start()
+        takes[3].wait()
+        load_2 = [copy_of(g2_ref.at[:, piece(width, h)], wa.at[:, piece(width, h)]) for h in (0, 1)]
+        load_2[0].start()
         cot.advance(1, 0)
         norm.finish()
         n_store.wait()
         for copy in cross_n:
             copy.wait_send()
-        load_2.wait()
+        load_2[0].wait()
+        load_2[1].start()
         upper = lax.div(line, tensor // 2)
+
+        def outward(i):
+            return (1 - upper) * (tensor - 1 - i) + upper * i
 
         @pl.loop(0, tensor)
         def _(i):
-            d = (1 - upper) * (tensor - 1 - i) + upper * i
-            at = block(d)
+            at = block(outward(i))
 
             @pl.loop(0, width, step=1024)
             def _(n):
+                @pl.when((i == 0) & (n > 0))
+                def _():
+                    load_2[1].wait()
+
                 to = pl.ds(pl.multiple_of(n, 1024), 1024)
                 value = dot_nn(act[at, :], wa[:, to]) + dot_nn(attn[at, :], wd[:, to])
                 nv[at, to] = value.astype(bf16)
@@ -1118,49 +963,43 @@
             def _():
                 cot.advance(1, 1)
 
-        store_d.wait()
-        cross_a.wait_recv()
-        cross_t.wait_recv()
-        load_ax = copy_of(ax_out, slope)
-        load_tx = copy_of(tx_out, wb.at[pl.ds(tokens, tokens), pl.ds(width // 2, local)])
-        load_ax.start()
-        load_tx.start()
-        cot.advance(2, 0)
-        outs.advance(1, add_into)
-        cot.advance(2, 1)
-        grad = wa.at[pl.ds(0, tokens), :]
-        load_c = copy_of(c_out, grad)
+        fsum[...] = jnp.zeros_like(fsum)
         cross_c = [
-            to_twin(chips + 2 + r, c_out.at[:, cols(relative(twin, r << 1))], cx_out.at[r])
+            to_twin(chips + 2 + r, cbuf.at[:, cols(relative(twin, r << 1))],
+                    xbuf.at[:, pl.ds(r * part, part)])
             for r in range(chips)
         ]
-        for copy in cross_c:
-            copy.start()
-        load_c.start()
-        load_c.wait()
-        g_buf[...] = dot_nt(grad[...], wd[...]).astype(bf16)
-        load_cx = [
-            copy_of(cx_out.at[r], wb.at[pl.ds(tokens, tokens), pl.ds(r * part, part)])
-            for r in range(chips)
-        ]
-        for crossed, copy in zip(cross_c, load_cx):
-            crossed.wait_recv()
-            copy.start()
-        for copy in load_cx + [load_ax, load_tx]:
-            copy.wait()
-
-        def weight_grad(left, spot, plan, own, crossed, size, step):
+
+        @pl.loop(-1, tensor - 1)
+        def _(s):
+            @pl.when(s == tensor - 2)
+            def _():
+                cot.advance(tensor - 2, 0)
+                outs.advance(1)
+                cot.advance(tensor - 2, 1)
+                for copy in cross_c:
+                    copy.start()
+
+            blocks_of(s, slope_layer)
+
+        cross_p = to_twin(2 * chips + 3, slope, gpx_out)
+        cross_p.start()
+        for copy in cross_c + [cross_t]:
+            copy.wait_recv()
+        load_ax.wait()
+        dense.finish()
+
+        def weight_grad(left, plan, own, crossed, spot, size, step, hook=None):
             @pl.loop(0, chips)
             def _(i):
                 r = chips - 1 - i
                 slot = chip_slot(me, r)
+                across = pl.ds(pl.multiple_of(r * part, part), part)
 
                 @pl.loop(0, size, step=step)
                 def _(n):
                     at = pl.multiple_of(n, step)
-                    value = dot_tn(left[:, cols(slot)], own(at))
-                    crossed_left = wb[pl.ds(tokens, tokens), pl.ds(pl.multiple_of(r * part, part), part)]
-                    value = value + dot_tn(crossed_left, crossed(at))
+                    value = dot_tn(left(cols(slot)), own(at)) + dot_tn(xbuf[:, across], crossed(at))
                     spot(r, at, value.astype(bf16))
 
                 for k in range(1, chips):
@@ -1169,166 +1008,310 @@
                     def _():
                         plan.start(k)
 
-        def spot_2(r, at, value):
+                if hook is not None:
+                    hook(i)
+
+        def spot_a(r, at, value):
             wa[pl.ds(pl.multiple_of(tokens + r * part, part), part), pl.ds(at, 1024)] = value
 
         def spot_d(r, at, value):
-            wb[pl.ds(pl.multiple_of(r * part, part), part), pl.ds(3 * local, local)] = value
-
-        sum_2 = reduce_fc2.bind(
-            me, line,
-            lambda r, h: wa.at[pl.ds(tokens + r * part, part), pl.ds(h * (units // 2), units // 2)],
-            r2, *pair)
-        sum_d = reduce_dense.bind(
-            me, line,
-            lambda r, h: wb.at[pl.ds(r * part, part), pl.ds(3 * local + h * (local // 2), local // 2)],
-            rd, *pair)
+            for h in (0, 1):
+                to = pl.ds(pl.multiple_of((2 * r + h) * part, part), part)
+                mask[to, :] = value[:, h * (local // 2) : (h + 1) * (local // 2)]
+
+        def spot_1(r, at, value):
+            wb[pl.ds(pl.multiple_of(r * part, part), part), pl.ds(at, 1024)] = value
+
+        def spot_q(r, at, value):
+            abuf[pl.ds(pl.multiple_of(r * part, part), part), pl.ds(at, local)] = value
+
         weight_grad(
-            grad, spot_2, sum_2, lambda at: act[:, pl.ds(at, 1024)],
-            lambda at: slope[:, pl.ds(at, 1024)], units, 1024)
+            lambda a: cbuf[:, a], sum_2, lambda at: act[:, pl.ds(at, 1024)],
+            lambda at: wb[low, pl.ds(at, 1024)], spot_a, units, 1024)
         weight_grad(
-            grad, spot_d, sum_d, lambda at: attn[...],
-            lambda at: wb[pl.ds(tokens, tokens), pl.ds(width // 2, local)], local, local)
-        sum_2.middle()
-        cross_a.wait_send()
-        load_d = copy_of(d_out, act)
-        load_d.start()
-        qsum_ref[...] = jnp.zeros_like(qsum_ref)
+            lambda a: cbuf[:, a], sum_d, lambda at: attn[...],
+            lambda at: xbuf[:, pl.ds(chips * part, local)], spot_d, local, local)
+        load_n = copy_of(n_out, wa.at[low, :])
+        load_n.start()
+        load_g1 = copy_of(g1_ref.at[low, :], wb.at[low, :])
+        load_g1.start()
+        for copy in cross_n:
+            copy.wait_recv()
+        load_nx = [copy_of(nx_out.at[r], xbuf.at[:, pl.ds(r * part, part)]) for r in range(chips)]
+        for copy in load_nx:
+            copy.start()
+        cot.finish()
+        for copy in cross_c + [cross_a]:
+            copy.wait_send()
+        bsum[...] = jnp.zeros_like(bsum)
+        for k in range(units // local):
+            bsum[k : k + 1, :] = fsum[0:1, k * local : (k + 1) * local]
+        load_w = [copy_of(gq_ref.at[i], pb.at[pl.ds(0, width), pl.ds(i * local, local)]) for i in range(3)]
 
         @pl.loop(0, pairs)
         def _(h):
             lanes = pl.ds(pl.multiple_of(h * 128, 128), 128)
 
             def write(which, at, value):
-                wb[at, pl.ds(pl.multiple_of(which * local + h * 128, 128), 128)] = value
+                cbuf[at, pl.ds(pl.multiple_of(which * local + h * 128, 128), 128)] = value
 
             sums = attend_back_pair(
                 qkv3[0, :, lanes], qkv3[1, :, lanes], qkv3[2, :, lanes],
-                g_buf[:, lanes], attn[:, lanes], lambda e, at: pb[2 * h + e, at, :],
+                abuf[:, pl.ds(pl.multiple_of(local + h * 128, 128), 128)], abuf[:, lanes],
+                lambda e, at: pb[at, prob_lanes(h, e)],
                 (cos_ref, slo_ref, shi_ref), kacc, vacc, write)
             for k in range(3):
-                qsum_ref[k : k + 1, lanes] = sums[k]
+                bsum[units // local + k : units // local + k + 1, lanes] = sums[k]
+
+            for k in range(3):
+
+                @pl.when(h == k)
+                def _():
+                    load_w[k].start()
 
             @pl.when(h == 0)
             def _():
-                outs.advance(2, add_into)
-
-            @pl.when(h == 2)
-            def _():
+                sum_2.middle()
+
+            @pl.when(h == 1)
+            def _():
+                outs.advance(2)
+
+        back = cbuf.at[:, pl.ds(0, wide)]
+        cross_d = to_twin(2 * chips + 2, back, gqx_out)
+        cross_d.start()
+        bias_tells = [
+            remote(tells[r - 1], bsum, tell_b.at[r], (relative(me, r), line)) for r in range(1, dp)
+        ]
+        for copy in bias_tells:
+            copy.start()
+        for copy in load_w + [load_g1]:
+            copy.wait()
+        load_gx = [copy_of(gqx_out.at[:, pl.ds(i * local, local)], qkv3.at[i]) for i in range(3)]
+        store_o = copy_of(x_buf, out_ref)
+        load_px = copy_of(gpx_out, nv)
+        spare = pb.at[pl.ds(width, rows), :]
+        load_c = copy_of(c_ref, spare)
+
+        @pl.loop(0, tensor)
+        def _(i):
+            at = block(outward(i))
+
+            @pl.loop(0, width, step=1024)
+            def _(n):
+                to = pl.ds(pl.multiple_of(n, 1024), 1024)
+                value = dot_nt(slope[at, :], wb[to, :])
+                value = value + dot_nt(cbuf[at, pl.ds(0, wide)], pb[to, pl.ds(0, wide)])
+                act[at, to] = value.astype(bf16)
+
+            for k in range(tensor - 1):
+
+                @pl.when(i == k)
+                def _():
+                    ins.start(0, k)
+                    ins.start(1, k)
+
+            @pl.when(i == 0)
+            def _():
+                load_c.start()
                 sum_d.middle()
 
-        slabs = width // BLOCK
-        load_w = [
-            copy_of(g2_ref.at[:, pl.ds(e * BLOCK, BLOCK)], pb.at[e, pl.ds(0, units), :])
-            for e in range(slabs)
+            @pl.when(i == 1)
+            def _():
+                cross_d.wait_recv()
+                for copy in load_gx:
+                    copy.start()
+                load_n.wait()
+                for copy in load_nx + load_gx:
+                    copy.wait()
+                cross_t.wait_send()
+                weight_grad(
+                    lambda a: wa[low, a], sum_q, lambda at: cbuf[:, pl.ds(at, local)],
+                    lambda at: qkv3[lax.div(at, local)], spot_q, wide, local)
+
+            @pl.when(i == tensor - 2)
+            def _():
+                cross_p.wait_recv()
+                outs.arrive()
+
+                @pl.loop(0, rows, step=32)
+                def _(r):
+                    at = pl.ds(r, 32)
+                    own = pl.ds(pl.multiple_of(line * rows + r, 32), 32)
+                    total = x_buf[at, :].astype(f32) + outs.total(nv[own, :], at) + vec_buf[2:3, :]
+                    x_buf[at, :] = total.astype(bf16)
+
+                store_o.start()
+                load_px.start()
+
+        ins.advance(1)
+        load_px.wait()
+
+        def late_steps(i):
+            @pl.when(i == 0)
+            def _():
+                sum_q.middle()
+
+        weight_grad(
+            lambda a: wa[low, a], sum_1, lambda at: slope[:, pl.ds(at, 1024)],
+            lambda at: nv[:, pl.ds(at, 1024)], spot_1, units, 1024, late_steps)
+        sum_2.final()
+        sum_d.final()
+        store_2 = copy_of(wa.at[pl.ds(tokens, part), :], s2_out)
+        store_dense = [
+            copy_of(mask.at[pl.ds(h * part, part), :], sd_out.at[:, piece(local, h)]) for h in (0, 1)
         ]
-        for copy in load_w:
+        for copy in [store_2] + store_dense:
             copy.start()
-        back = wb.at[pl.ds(0, tokens), pl.ds(0, 3 * local)]
-        store_q = copy_of(back, dq_out)
+        store_o.wait()
+        load_x = copy_of(x_ref, x_buf)
+        load_x.start()
+        for copy in bias_tells:
+            copy.wait_recv()
+        total_b = bsum[...]
+        for r in range(1, dp):
+            total_b = total_b + tell_b[r]
+        bout_ref[...] = total_b
+        ins.advance(2)
+        sum_1.middle()
+        sum_q.final()
+        store_q = copy_of(abuf.at[pl.ds(0, part), :], sq_out)
         store_q.start()
-        cross_d = to_twin(2 * chips + 2, back, dqx_out)
-        cross_d.start()
-        for copy in load_w:
-            copy.wait()
-        load_d.wait()
-
-        @pl.loop(0, units, step=512)
-        def _(n):
-            at = pl.ds(pl.multiple_of(n, 512), 512)
-            weight = jnp.concatenate([pb[e, at, :] for e in range(slabs)], 1)
-            value = dot_nt(grad[...], weight) * act[:, at].astype(f32)
-            value = value.astype(bf16)
-            act[:, at] = value
-            sum_ref[0:1, at] = jnp.sum(value.astype(f32), 0, keepdims=True)
-
-        store_p = copy_of(act, gp_out)
-        store_p.start()
-        cross_p = to_twin(2 * chips + 3, act, gpx_out)
-        cross_p.start()
-        outs.arrive()
+        load_c.wait()
+        load_x.wait()
+        parts[...] = jnp.zeros_like(parts)
+        ins.arrive()
 
         @pl.loop(0, rows, step=32)
         def _(r):
             at = pl.ds(r, 32)
+            x = x_buf[at, :].astype(f32)
+            centred = x - jnp.mean(x, -1, keepdims=True)
+            inv_std = lax.rsqrt(jnp.mean(centred * centred, -1, keepdims=True) + layer_eps)
+            unit = centred * inv_std
             own = pl.ds(pl.multiple_of(line * rows + r, 32), 32)
-            total = x_buf[at, :].astype(f32) + outs.total(nv[own, :], at) + vec_buf[2:3, :]
-            x_buf[at, :] = total.astype(bf16)
-
-        store_o = copy_of(x_buf, out_ref)
-        store_o.start()
-        sum_2.final()
-        sum_d.final()
-        store_2 = copy_of(wa.at[pl.ds(tokens, part), :], s2_out)
-        store_dense = copy_of(wb.at[pl.ds(0, part), pl.ds(3 * local, local)], sd_out)
-        store_2.start()
-        store_dense.start()
-        for copy in cross_n + [cross_d, cross_p]:
+            grad = ins.total(act[own, :], at)
+            cot_rows = pl.ds(pl.multiple_of(width + r, 32), 32)
+            cotan = pb[cot_rows, :].astype(f32)
+            scaled = grad * vec_buf[0:1, :]
+            first = jnp.mean(scaled, -1, keepdims=True)
+            second = jnp.mean(scaled * unit, -1, keepdims=True)
+            x_buf[at, :] = (cotan + inv_std * (scaled - first - unit * second)).astype(bf16)
+            parts[0:1, :] += jnp.sum(grad * unit, 0, keepdims=True)
+            parts[1:2, :] += jnp.sum(grad, 0, keepdims=True)
+            parts[2:3, :] += jnp.sum(cotan, 0, keepdims=True)
+
+        vec_tells = [
+            remote(tells[dp - 2 + r], parts.at[:, cols(relative(me, r))], tell_v.at[r],
+                   (relative(me, r), line))
+            for r in range(1, dp)
+        ]
+        for copy in vec_tells:
+            copy.start()
+        store_h = copy_of(x_buf, hid_ref)
+        store_h.start()
+        for copy in vec_tells:
             copy.wait_recv()
-        for copy in vec + [cross_t] + cross_c + [cross_d, cross_p]:
+        total_v = parts[:, cols(me)]
+        for r in range(1, dp):
+            total_v = total_v + tell_v[r]
+        tell_z[0] = total_v
+        line_tells = [
+            remote(tells[2 * dp - 3 + k], tell_z.at[0], tell_z.at[k], (me, lax.rem(line + k, tensor)))
+            for k in range(1, tensor)
+        ]
+        for copy in line_tells:
+            copy.start()
+        sum_1.final()
+        store_1 = copy_of(wb.at[pl.ds(0, part), :], s1_out)
+        store_1.start()
+        for copy in line_tells:
+            copy.wait_recv()
+        total_z = tell_z[0]
+        for k in range(1, tensor):
+            total_z = total_z + tell_z[k]
+        vout_ref[...] = total_z
+        for copy in vec + [cross_p] + bias_tells + vec_tells + line_tells:
             copy.wait_send()
-        for plan in (qkv, fc1, dense, fc2, cot, outs, sum_2, sum_d):
+        for plan in (qkv, fc1, fc2, sum_2, sum_d, sum_1, sum_q):
             plan.finish()
-        for copy in (store_q, store_p, store_o, store_2, store_dense):
+        for copy in [cross_d]:
+            copy.wait_send()
+        for copy in store_dense + [store_2, store_q, store_h, store_1]:
             copy.wait()
 
     def shape(*dims):
         return jax.ShapeDtypeStruct(dims, bf16)
 
+    def vmem(*dims):
+        return pltpu.VMEM(dims, bf16)
+
+    landings = [
+        shape(2 * tensor - 3, rows, width),
+        shape(2 * tensor - 3, rows, width),
+        shape(6, part, units // 2),
+        shape(6, part, local // 2),
+        shape(6, part, units // 2),
+        shape(6, part, wide // 2),
+    ]
     return pl.pallas_call(
         kernel,
         out_shape=(
             shape(rows, width),
+            shape(rows, width),
+            shape(part, units),
+            shape(part, local),
+            shape(part, units),
+            shape(part, wide),
             shape(3, width, local),
             shape(width, units),
             shape(units, width),
             shape(tokens, width),
             shape(chips, tokens, part),
-            shape(tokens, width),
-            shape(chips, tokens, part),
             shape(tokens, units),
+            shape(tokens, wide),
             shape(tokens, units),
-            shape(tokens, local),
-            shape(tokens, 3 * local),
-            shape(tokens, 3 * local),
-            shape(tokens, units),
-            shape(tokens, units),
-            shape(part, units),
-            shape(part, local),
-            jax.ShapeDtypeStruct((8, width), f32),
+            *landings,
+            jax.ShapeDtypeStruct((8, part), f32),
             jax.ShapeDtypeStruct((8, local), f32),
-            jax.ShapeDtypeStruct((8, units), f32),
         ),
         in_specs=[ANY] * 7 + [VMEM] * 3,
-        out_specs=(ANY,) * 17 + (VMEM,) * 3,
+        out_specs=(ANY,) * 20 + (VMEM,) * 2,
         scratch_shapes=[
-            pltpu.VMEM((rows, width), bf16),
+            vmem(rows, width),
             pltpu.VMEM((8, width), f32),
-            pltpu.VMEM((tokens, width), bf16),
-            pltpu.VMEM((width, width), bf16),
-            pltpu.VMEM((width, units), bf16),
-            pltpu.VMEM((local, width), bf16),
-            pltpu.VMEM((tokens, units), bf16),
-            pltpu.VMEM((tokens, units), bf16),
-            pltpu.VMEM((3, tokens, local), bf16),
-            pltpu.VMEM((tokens, local), bf16),
-            pltpu.VMEM((local // HD, stored, BLOCK), bf16),
-            pltpu.VMEM((stored, BLOCK), f32),
-            pltpu.VMEM((tokens, local), bf16),
+            vmem(tokens, width),
+            vmem(width, width),
+            vmem(width, units),
+            vmem(local, width),
+            vmem(tokens, units),
+            vmem(tokens, units),
+            vmem(3, tokens, local),
+            vmem(tokens, wide),
+            vmem(stored, local // HD * BLOCK),
+            vmem(stored, BLOCK),
+            vmem(tokens, width),
+            vmem(tokens, chips * part + local),
         ]
         + [pltpu.VMEM((tokens, 128), f32)] * 5
         + [
-            pltpu.VMEM((2 * tensor - 3, rows, width), bf16),
-            pltpu.VMEM((6, part, units // 2), bf16),
-            pltpu.VMEM((6, part, local // 2), bf16),
+            vmem(tensor - 1, rows, width),
+            vmem(2, part, units // 2),
+            pltpu.VMEM((8, units), f32),
+            pltpu.VMEM((8, local), f32),
+            pltpu.VMEM((8, width), f32),
+            pltpu.VMEM((dp, 8, part), f32),
+            pltpu.VMEM((dp, 8, local), f32),
+            pltpu.VMEM((tensor, 8, part), f32),
             pltpu.SemaphoreType.DMA((sems.count,)),
             pltpu.SemaphoreType.DMA((sems.count,)),
             pltpu.SemaphoreType.DMA((48,)),
+            pltpu.SemaphoreType.DMA((2,)),
         ],
         compiler_params=pltpu.CompilerParams(
-            collective_id=0, has_side_effects=True, vmem_limit_bytes=VMEM_LIMIT
+            collective_id=0, has_side_effects=True, vmem_limit_bytes=67_043_328
         ),
-        name="forward",
+        name="block",
     )(*arrays)
 
 
@@ -1419,16 +1402,8 @@
         dense_weight, fc1_weight, fc2_weight, vectors,
     )
     if fast:
-        (
-            out, w_qkv, w_fc1, _, normed, crossed_normed, _, _, _, _, _,
-            grad_qkv, crossed_qkv, grad_pre, crossed_pre, sent_fc2, sent_dense,
-            vec, qkv_sums, fc1_sums,
-        ) = forward_call(dp, tensor, (*mine, qkv_bias, fc1_bias[None], segments))
-        sums = jnp.concatenate([fc1_sums[0].reshape(4, local), qkv_sums[:3], jnp.zeros((1, local), f32)], 0)
-        hidden_grad, sent_fc1, sent_qkv, vec_sums, all_sums = second_call(
-            dp, tensor,
-            (hidden_in, cotangent, vec, sums, normed, grad_pre, grad_qkv,
-             crossed_normed, crossed_pre, crossed_qkv, w_qkv, w_fc1))
+        (out, hidden_grad, sent_fc2, sent_dense, sent_fc1, sent_qkv, *_, vec_sums, all_sums) = block_call(
+            dp, tensor, (*mine, qkv_bias, fc1_bias[None], segments))
         quarter = vec_sums.shape[1] // tensor
         at = lax.axis_index("tensor") * quarter
         small = lax.dynamic_slice(vec_sums, (0, at), (3, quarter))

time: 321 us -> 296 us (0.922)
  Pallas kernels: 311 us -> 287 us
    pallas_call x2 -> x1, Pallas kernels: 304 us -> 281 us  [block_call(): pl.pallas_call(kernel, out_shape=(shape(rows, width), shape(rows, width),...]
where the time goes in v5:
time: 296 us; the launch traced here: 295 us
  Pallas kernels  287 us (97%)
  local copies, waits for them, and re-layouts  4.28 us (1%)
    pallas_call x1, Pallas kernels, block_call(): pl.pallas_call(kernel, out_shape=(shape(rows, width), shape(rows, width),...  281 us
    pallas_call x1, Pallas kernels, finish(): pl.pallas_call(finish_kernel, grid=(steps,), out_shape=(jax.ShapeDtypeStr...  6.29 us

profile of v5, /device:TPU:0, one launch (start us, length us, event | category | flops | bytes accessed | tf_op | source)
XLA Modules:
  0.0 294.9 jit_solution(16428545432656856616)
XLA Ops:
  0.7 0.7 convert_add_fusion
  1.3 0.7 convert_element_type.14
  2.0 0.7 convert_element_type.15
  2.6 0.7 select_select_fusion.vec_ref
  3.3 1.3 broadcast_in_dim.34.fb_ref
  4.6 281.0 %block.1 = (bf16[256,2048]{1,0:T(8,128)(2,1)}, bf16[256,2048]{1,0:T(8,128)(2,1)}, bf16[256,2048]{1,0:T(8,128)(2,1)}, bf16[256,512]{1,0:T(8,128)(2,1)}, bf16[256,...) custom-call(bf16[256,2048]{1,0:T(8,128)(2,1)} %x_ref.1, ...), custom_call_target="tpu_custom_call" | custom-call | tf_op jit(solution)/shard_map/block/pallas_call | solution.py:1257
  285.6 0.0 copy-start
  285.6 6.3 %finish.1 = (f32[2048,256]{1,0:T(8,128)}, f32[512,256]{1,0:T(8,128)}, f32[256,2048]{1,0:T(8,128)}, f32[3,256,512]{2,1,0:T(8,128)}, bf16[256,2048]{1,0:T(8,128)(2,1)}, /*index=5*/bf16[256,2048]{1,0:T(8,128)(2,1)}) custom-call(bf16[256,2048]{1,0:T(8,128)(2,1)} %get-tuple-element.26.s2_ref, bf16[256,512]{1,0:T(8,128)(2,1)} %get-tuple-element.27.sd_ref, ...), custom_call_target="tpu_custom_call" | custom-call | tf_op jit(solution)/shard_map/finish/pallas_call | solution.py:1341
  291.9 0.7 constant_dynamic-slice_fusion
  292.6 0.5 slice_bitcast_fusion.1
  293.2 0.0 copy-start.1
  293.2 0.0 copy-done
  293.2 0.6 copy.25
  293.8 0.6 slice.18
  294.4 0.5 copy.27
  294.9 0.0 copy-done.1
  (2 shorter events, 0.0 us)
Async XLA Ops:
  285.6 7.6 %copy-start = (f32[8,512]{1,0:T(8,128)S(1)}, f32[8,512]{1,0:T(8,128)}, u32[]{:S(2)}) copy-start(f32[8,512]{1,0:T(8,128)} %get-tuple-element.36) | copy-start | bytes 49156
  293.2 1.7 copy-start.1

commit v6 on v5

--- a/solution.py
+++ b/solution.py
@@ -336,17 +336,18 @@
                     add_into(held, self.own(self.target(way, i)))
                     self.copy(way, i, False).start()
 
+    def settle(self):
+        for way, i in self.ids:
+
+            @pl.when(self.edge(way))
+            def _():
+                self.copy(way, i, True).wait_send()
+
+            @pl.when(self.passes(way, i))
+            def _():
+                self.copy(way, i, False).wait_send()
+
     def arrive(self):
-        for way, i in self.ids:
-
-            @pl.when(self.edge(way))
-            def _():
-                self.copy(way, i, True).wait_send()
-
-            @pl.when(self.passes(way, i))
-            def _():
-                self.copy(way, i, False).wait_send()
-
         def fetch(way, i):
             return pltpu.make_async_copy(
                 self.landing.at[self.place(way, i)], self.last(way), self.stage_sem.at[way])
@@ -606,7 +607,7 @@
 
 
 def block_call(dp, tensor, arrays):
-    hidden, cotangent, w_qkv, w_dense, w_fc1, w_fc2, vectors = arrays[:7]
+    hidden, cotangent, w_qkv, w_dense, w_fc1, w_fc2 = arrays[:6]
     rows, width = hidden.shape
     local = w_qkv.shape[2]
     wide = 3 * local
@@ -627,13 +628,14 @@
     tells = [sems.take() for _ in range(2 * (dp - 1) + tensor - 1)]
 
     def kernel(
-        x_ref, c_ref, wq_ref, wd_ref, w1_ref, w2_ref, vec_ref, qb_ref, fb_ref, seg_ref,
+        x_ref, c_ref, wq_ref, wd_ref, w1_ref, w2_ref, gain_ref, beta_ref, bd_ref, b2_ref,
+        qb_ref, fb_ref, seg_ref,
         out_ref, hid_ref, s2_out, sd_out, s1_out, sq_out,
-        gq_ref, g1_ref, g2_ref, n_out, nx_out, ax_out, gqx_out, gpx_out,
+        gq_ref, g1_ref, g2_ref, x_out, n_out, nx_out, ax_out, gqx_out, gpx_out,
         land_out, land_in, land_2, land_d, land_1, land_q, vout_ref, bout_ref,
         x_buf, vec_buf, nv, wa, wb, wd, act, slope, qkv3, abuf, pb, mask, cbuf, xbuf,
         kacc, vacc, cos_ref, slo_ref, shi_ref, line_stage, chip_stage,
-        fsum, bsum, parts, tell_v, tell_b, tell_z,
+        fsum, bsum, parts, tell_v, tell_b, tell_z, vec_ref,
         send_sem, recv_sem, local_sem, stage_sem,
     ):
         me, line = lax.axis_index("dp"), lax.axis_index("tensor")
@@ -692,7 +694,7 @@
             lambda h: w2_ref.at[piece(units, h), :],
             lambda a, h: g2_ref.at[piece(units, h), cols(a)], *pair)
         norm = plan_n.bind(
-            line, me, lambda u: nv.at[tok(line, u)], lambda b, u: nv.at[tok(b, u)], *pair)
+            line, me, lambda u: x_ref.at[piece(rows, u)], lambda b, u: pb.at[tok(b, u)], *pair)
         cot = plan_c.bind(
             line, me, lambda u: c_ref.at[piece(rows, u)], lambda b, u: cbuf.at[tok(b, u)], *pair)
         staged = (stage_sem, *pair)
@@ -725,54 +727,56 @@
 
         takes = [
             copy_of(x_ref, x_buf),
-            copy_of(vec_ref, vec_buf.at[:, cols(me)]),
             copy_of(wd_ref, wd.at[:, cols(me)]),
             copy_of(c_ref, cbuf.at[block(line), :]),
             copy_of(wq_ref, qkv3.at[:, pl.ds(0, part), :]),
             copy_of(w1_ref, act.at[pl.ds(0, part), :]),
             copy_of(w2_ref, wb.at[:, pl.ds(0, part)]),
+            copy_of(x_ref, pb.at[block(line), :]),
         ]
         keeps = [
             copy_of(qkv3.at[:, pl.ds(0, part), :], gq_ref.at[:, cols(me), :]),
             copy_of(act.at[pl.ds(0, part), :], g1_ref.at[cols(me), :]),
             copy_of(wb.at[:, pl.ds(0, part)], g2_ref.at[:, cols(me)]),
         ]
-        for copy in takes[:2]:
-            copy.start()
+        takes[0].start()
+        for k, ref in enumerate((gain_ref, beta_ref, bd_ref)):
+            vec_ref[k : k + 1, :] = ref[...].astype(f32).reshape(1, part)
+        vec_ref[2:3, :] += b2_ref[...].astype(f32).reshape(1, part)
+        vec_buf[:, cols(me)] = vec_ref[...]
+        parts[0:1, :] = fb_ref[...].astype(f32).reshape(1, units)
         greet(
             dp, me, tensor, line,
             lambda: fill_tables(seg_ref, kacc, cos_ref, slo_ref, shi_ref))
         for copy in vec:
             copy.start()
+        norm.start(0)
+        norm.start(1)
         qkv.start()
-        cot.start(0)
-        for copy in takes[2:]:
+        for copy in takes[1:]:
             copy.start()
-        for copy in takes[:2]:
-            copy.wait()
+        takes[0].wait()
         for copy in vec:
             copy.wait_recv()
-
-        @pl.loop(0, rows, step=32)
-        def _(r):
-            x = x_buf[pl.ds(r, 32), :].astype(f32)
-            centred = x - jnp.mean(x, -1, keepdims=True)
-            spread = jnp.mean(centred * centred, -1, keepdims=True)
-            unit = centred * lax.rsqrt(spread + layer_eps)
-            at = pl.ds(pl.multiple_of(line * rows + r, 32), 32)
-            nv[at, :] = (unit * vec_buf[0:1, :] + vec_buf[1:2, :]).astype(bf16)
-
-        norm.start(0)
-        norm.start(1)
         qkv.advance(0)
         fc1.start()
-        for take, copy in zip(takes[4:], keeps):
+        for take, copy in zip(takes[3:6], keeps):
             take.wait()
             copy.start()
         fill_mask(mask, kacc, seg_ref, tokens)
 
         def project(b):
             at = block(b)
+
+            @pl.loop(0, rows, step=32)
+            def _(r):
+                some = pl.ds(pl.multiple_of(b * rows + r, 32), 32)
+                x = pb[some, :].astype(f32)
+                centred = x - jnp.mean(x, -1, keepdims=True)
+                spread = jnp.mean(centred * centred, -1, keepdims=True)
+                unit = centred * lax.rsqrt(spread + layer_eps)
+                nv[some, :] = (unit * vec_buf[0:1, :] + vec_buf[1:2, :]).astype(bf16)
+
             cosine, slo, shi = cos_ref[at, :], slo_ref[at, :], shi_ref[at, :]
             for i in range(3):
                 value = dot_nn(nv[at, :], wa[:, i * local : (i + 1) * local])
@@ -797,7 +801,7 @@
                     load_1[1].wait()
 
                 to = pl.ds(pl.multiple_of(n, 512), 512)
-                pre = dot_nn(nv[at, :], wb[:, to]) + fb_ref[0:1, to].astype(f32)
+                pre = dot_nn(nv[at, :], wb[:, to]) + parts[0:1, to]
                 square = pre * pre
                 bend = jnp.tanh(0.7978845608028654 * pre * (1.0 + 0.044715 * square))
                 act[at, to] = (0.5 * pre * (1.0 + bend)).astype(bf16)
@@ -828,10 +832,9 @@
                     task(b)
 
         norm.advance(0, 0)
-        for j in range(1, stages - 1):
+        norm.advance(0, 1)
+        for j in range(1, stages):
             qkv.advance(j)
-        norm.advance(0, 1)
-        qkv.advance(stages - 1)
         keeps[0].wait()
         load_q = [
             copy_of(gq_ref.at[i], wa.at[:, pl.ds(i * local, local)]) for i in range(3)
@@ -841,18 +844,16 @@
         fc1.advance(0)
         dense.start()
         fc2.start()
-        for copy in load_q:
+        for copy in load_q + [takes[6]]:
             copy.wait()
+        for s in range(1, tensor - 2):
+            norm.advance(s, 0)
+            norm.advance(s, 1)
+        cot.start(0)
+        cot.start(1)
 
         @pl.loop(-1, tensor - 2)
         def _(s):
-            @pl.when(s == tensor - 3)
-            def _():
-                norm.advance(tensor - 3, 0)
-                norm.advance(tensor - 3, 1)
-                cot.start(1)
-                cot.advance(0, 0)
-
             blocks_of(s, project)
 
         for j in range(1, stages):
@@ -864,12 +865,15 @@
         load_1[0].wait()
         load_1[1].start()
 
+        x_store = copy_of(pb.at[low, :], x_out)
+
         @pl.loop(-1, tensor - 1)
         def _(s):
             @pl.when(s == tensor - 2)
             def _():
                 norm.advance(tensor - 2, 0)
                 norm.advance(tensor - 2, 1)
+                x_store.start()
                 fc2.advance(0)
                 blocks_of(tensor - 2, project)
 
@@ -887,6 +891,8 @@
         cross_a = to_twin(chips, act, ax_out)
         for copy in cross_n + [cross_a]:
             copy.start()
+        norm.finish()
+        x_store.wait()
 
         def prob_lanes(h, e):
             return pl.ds(pl.multiple_of((2 * h + e) * BLOCK, BLOCK), BLOCK)
@@ -904,9 +910,13 @@
             attend_pair(
                 qkv3[0, :, lanes], qkv3[1, :, lanes], qkv3[2, :, lanes], mask, keep, write)
 
+            @pl.when(h == 0)
+            def _():
+                cot.advance(0, 0)
+                cot.advance(0, 1)
+
             @pl.when(h == 1)
             def _():
-                cot.advance(0, 1)
                 for j in range(1, stages - 1):
                     dense.advance(j)
 
@@ -917,17 +927,13 @@
 
         cross_t = to_twin(chips + 1, attn, xbuf.at[:, pl.ds(chips * part, local)])
         cross_t.start()
-        cross_a.wait_recv()
-        load_ax = copy_of(ax_out, wb.at[low, :])
-        load_ax.start()
         dense.advance(stages - 1)
         fc2.advance(stages - 1)
+        takes[1].wait()
         takes[2].wait()
-        takes[3].wait()
         load_2 = [copy_of(g2_ref.at[:, piece(width, h)], wa.at[:, piece(width, h)]) for h in (0, 1)]
         load_2[0].start()
         cot.advance(1, 0)
-        norm.finish()
         n_store.wait()
         for copy in cross_n:
             copy.wait_send()
@@ -963,6 +969,9 @@
             def _():
                 cot.advance(1, 1)
 
+        cross_a.wait_recv()
+        load_ax = copy_of(ax_out, wb.at[low, :])
+        load_ax.start()
         fsum[...] = jnp.zeros_like(fsum)
         cross_c = [
             to_twin(chips + 2 + r, cbuf.at[:, cols(relative(twin, r << 1))],
@@ -989,7 +998,7 @@
         load_ax.wait()
         dense.finish()
 
-        def weight_grad(left, plan, own, crossed, spot, size, step, hook=None):
+        def weight_grad(left, plan, own, crossed, spot, size, step, hook=None, second=None):
             @pl.loop(0, chips)
             def _(i):
                 r = chips - 1 - i
@@ -998,6 +1007,12 @@
 
                 @pl.loop(0, size, step=step)
                 def _(n):
+                    if second is not None:
+
+                        @pl.when((i == 0) & (n == step))
+                        def _():
+                            second.wait()
+
                     at = pl.multiple_of(n, step)
                     value = dot_tn(left(cols(slot)), own(at)) + dot_tn(xbuf[:, across], crossed(at))
                     spot(r, at, value.astype(bf16))
@@ -1089,9 +1104,14 @@
             copy.wait()
         load_gx = [copy_of(gqx_out.at[:, pl.ds(i * local, local)], qkv3.at[i]) for i in range(3)]
         store_o = copy_of(x_buf, out_ref)
-        load_px = copy_of(gpx_out, nv)
+        load_px = [copy_of(gpx_out.at[:, piece(units, h)], cbuf.at[:, piece(units, h)]) for h in (0, 1)]
         spare = pb.at[pl.ds(width, rows), :]
         load_c = copy_of(c_ref, spare)
+
+        def dense_step(i):
+            @pl.when(i == chips - 2)
+            def _():
+                sum_d.middle()
 
         @pl.loop(0, tensor)
         def _(i):
@@ -1114,7 +1134,6 @@
             @pl.when(i == 0)
             def _():
                 load_c.start()
-                sum_d.middle()
 
             @pl.when(i == 1)
             def _():
@@ -1127,25 +1146,17 @@
                 cross_t.wait_send()
                 weight_grad(
                     lambda a: wa[low, a], sum_q, lambda at: cbuf[:, pl.ds(at, local)],
-                    lambda at: qkv3[lax.div(at, local)], spot_q, wide, local)
-
-            @pl.when(i == tensor - 2)
-            def _():
-                cross_p.wait_recv()
-                outs.arrive()
-
-                @pl.loop(0, rows, step=32)
-                def _(r):
-                    at = pl.ds(r, 32)
-                    own = pl.ds(pl.multiple_of(line * rows + r, 32), 32)
-                    total = x_buf[at, :].astype(f32) + outs.total(nv[own, :], at) + vec_buf[2:3, :]
-                    x_buf[at, :] = total.astype(bf16)
-
-                store_o.start()
-                load_px.start()
-
+                    lambda at: qkv3[lax.div(at, local)], spot_q, wide, local, dense_step)
+
+        cross_d.wait_send()
+        cross_p.wait_recv()
+        load_px[0].start()
+        outs.settle()
         ins.advance(1)
-        load_px.wait()
+        load_xa = copy_of(x_out, wb.at[high, :])
+        load_px[0].wait()
+        load_px[1].start()
+        load_xa.start()
 
         def late_steps(i):
             @pl.when(i == 0)
@@ -1154,7 +1165,56 @@
 
         weight_grad(
             lambda a: wa[low, a], sum_1, lambda at: slope[:, pl.ds(at, 1024)],
-            lambda at: nv[:, pl.ds(at, 1024)], spot_1, units, 1024, late_steps)
+            lambda at: cbuf[:, pl.ds(at, 1024)], spot_1, units, 1024, late_steps, load_px[1])
+        def finish_out():
+            outs.arrive()
+
+            @pl.loop(0, rows, step=32)
+            def _(r):
+                at = pl.ds(r, 32)
+                own = pl.ds(pl.multiple_of(line * rows + r, 32), 32)
+                total = x_buf[at, :].astype(f32) + outs.total(nv[own, :], at) + vec_buf[2:3, :]
+                x_buf[at, :] = total.astype(bf16)
+
+            store_o.start()
+
+        parts[...] = jnp.zeros_like(parts)
+        load_xa.wait()
+        load_c.wait()
+
+        def norm_sums(b):
+            @pl.loop(0, rows, step=32)
+            def _(r):
+                some = pl.ds(pl.multiple_of(b * rows + r, 32), 32)
+                x = wb[pl.ds(pl.multiple_of(tokens + b * rows + r, 32), 32), :].astype(f32)
+                grad = act[some, :].astype(f32)
+                centred = x - jnp.mean(x, -1, keepdims=True)
+                inv_std = lax.rsqrt(jnp.mean(centred * centred, -1, keepdims=True) + layer_eps)
+                parts[0:1, :] += jnp.sum(grad * (centred * inv_std), 0, keepdims=True)
+                parts[1:2, :] += jnp.sum(grad, 0, keepdims=True)
+
+        @pl.loop(0, tensor)
+        def _(b):
+            @pl.when(b == tensor - 1)
+            def _():
+                finish_out()
+                ins.advance(2)
+
+            norm_sums(b)
+
+        @pl.loop(0, rows, step=32)
+        def _(r):
+            cotan = pb[pl.ds(pl.multiple_of(width + r, 32), 32), :].astype(f32)
+            parts[2:3, :] += jnp.sum(cotan, 0, keepdims=True)
+
+        vec_tells = [
+            remote(tells[dp - 2 + r], parts.at[:, cols(relative(me, r))], tell_v.at[r],
+                   (relative(me, r), line))
+            for r in range(1, dp)
+        ]
+        for copy in vec_tells:
+            copy.start()
+        sum_1.middle()
         sum_2.final()
         sum_d.final()
         store_2 = copy_of(wa.at[pl.ds(tokens, part), :], s2_out)
@@ -1172,44 +1232,6 @@
         for r in range(1, dp):
             total_b = total_b + tell_b[r]
         bout_ref[...] = total_b
-        ins.advance(2)
-        sum_1.middle()
-        sum_q.final()
-        store_q = copy_of(abuf.at[pl.ds(0, part), :], sq_out)
-        store_q.start()
-        load_c.wait()
-        load_x.wait()
-        parts[...] = jnp.zeros_like(parts)
-        ins.arrive()
-
-        @pl.loop(0, rows, step=32)
-        def _(r):
-            at = pl.ds(r, 32)
-            x = x_buf[at, :].astype(f32)
-            centred = x - jnp.mean(x, -1, keepdims=True)
-            inv_std = lax.rsqrt(jnp.mean(centred * centred, -1, keepdims=True) + layer_eps)
-            unit = centred * inv_std
-            own = pl.ds(pl.multiple_of(line * rows + r, 32), 32)
-            grad = ins.total(act[own, :], at)
-            cot_rows = pl.ds(pl.multiple_of(width + r, 32), 32)
-            cotan = pb[cot_rows, :].astype(f32)
-            scaled = grad * vec_buf[0:1, :]
-            first = jnp.mean(scaled, -1, keepdims=True)
-            second = jnp.mean(scaled * unit, -1, keepdims=True)
-            x_buf[at, :] = (cotan + inv_std * (scaled - first - unit * second)).astype(bf16)
-            parts[0:1, :] += jnp.sum(grad * unit, 0, keepdims=True)
-            parts[1:2, :] += jnp.sum(grad, 0, keepdims=True)
-            parts[2:3, :] += jnp.sum(cotan, 0, keepdims=True)
-
-        vec_tells = [
-            remote(tells[dp - 2 + r], parts.at[:, cols(relative(me, r))], tell_v.at[r],
-                   (relative(me, r), line))
-            for r in range(1, dp)
-        ]
-        for copy in vec_tells:
-            copy.start()
-        store_h = copy_of(x_buf, hid_ref)
-        store_h.start()
         for copy in vec_tells:
             copy.wait_recv()
         total_v = parts[:, cols(me)]
@@ -1222,6 +1244,10 @@
         ]
         for copy in line_tells:
             copy.start()
+        sum_q.final()
+        store_q = copy_of(abuf.at[pl.ds(0, part), :], sq_out)
+        store_q.start()
+        load_x.wait()
         sum_1.final()
         store_1 = copy_of(wb.at[pl.ds(0, part), :], s1_out)
         store_1.start()
@@ -1231,12 +1257,29 @@
         for k in range(1, tensor):
             total_z = total_z + tell_z[k]
         vout_ref[...] = total_z
+        ins.settle()
+        ins.arrive()
+
+        @pl.loop(0, rows, step=32)
+        def _(r):
+            at = pl.ds(r, 32)
+            x = x_buf[at, :].astype(f32)
+            centred = x - jnp.mean(x, -1, keepdims=True)
+            inv_std = lax.rsqrt(jnp.mean(centred * centred, -1, keepdims=True) + layer_eps)
+            unit = centred * inv_std
+            own = pl.ds(pl.multiple_of(line * rows + r, 32), 32)
+            scaled = ins.total(act[own, :], at) * vec_buf[0:1, :]
+            cotan = pb[pl.ds(pl.multiple_of(width + r, 32), 32), :].astype(f32)
+            first = jnp.mean(scaled, -1, keepdims=True)
+            second = jnp.mean(scaled * unit, -1, keepdims=True)
+            x_buf[at, :] = (cotan + inv_std * (scaled - first - unit * second)).astype(bf16)
+
+        store_h = copy_of(x_buf, hid_ref)
+        store_h.start()
         for copy in vec + [cross_p] + bias_tells + vec_tells + line_tells:
             copy.wait_send()
         for plan in (qkv, fc1, fc2, sum_2, sum_d, sum_1, sum_q):
             plan.finish()
-        for copy in [cross_d]:
-            copy.wait_send()
         for copy in store_dense + [store_2, store_q, store_h, store_1]:
             copy.wait()
 
@@ -1267,6 +1310,7 @@
             shape(width, units),
             shape(units, width),
             shape(tokens, width),
+            shape(tokens, width),
             shape(chips, tokens, part),
             shape(tokens, units),
             shape(tokens, wide),
@@ -1275,8 +1319,8 @@
             jax.ShapeDtypeStruct((8, part), f32),
             jax.ShapeDtypeStruct((8, local), f32),
         ),
-        in_specs=[ANY] * 7 + [VMEM] * 3,
-        out_specs=(ANY,) * 20 + (VMEM,) * 2,
+        in_specs=[ANY] * 6 + [VMEM] * 7,
+        out_specs=(ANY,) * 21 + (VMEM,) * 2,
         scratch_shapes=[
             vmem(rows, width),
             pltpu.VMEM((8, width), f32),
@@ -1303,6 +1347,7 @@
             pltpu.VMEM((dp, 8, part), f32),
             pltpu.VMEM((dp, 8, local), f32),
             pltpu.VMEM((tensor, 8, part), f32),
+            pltpu.VMEM((8, part), f32),
             pltpu.SemaphoreType.DMA((sems.count,)),
             pltpu.SemaphoreType.DMA((sems.count,)),
             pltpu.SemaphoreType.DMA((48,)),
@@ -1315,7 +1360,10 @@
     )(*arrays)
 
 
-def finish_kernel(s2_ref, sd_ref, s1_ref, sq_ref, o_ref, h_ref, w2_ref, wd_ref, w1_ref, wq_ref, out_ref, hid_ref):
+def finish_kernel(
+    s2_ref, sd_ref, s1_ref, sq_ref, o_ref, h_ref, v_ref, b_ref,
+    w2_ref, wd_ref, w1_ref, wq_ref, out_ref, hid_ref, gain_ref, beta_ref, both_ref, same_ref, bq_ref, b1_ref,
+):
     w2_ref[...] = s2_ref[...].T.astype(f32)
     wd_ref[...] = sd_ref[...].T.astype(f32)
     w1_ref[...] = s1_ref[...].astype(f32)
@@ -1325,12 +1373,30 @@
     out_ref[...] = o_ref[...]
     hid_ref[...] = h_ref[...]
 
-
-def finish(sent_fc2, sent_dense, sent_fc1, sent_qkv, out, hidden_grad):
+    @pl.when(pl.program_id(0) == 0)
+    def _():
+        line = lax.axis_index("tensor")
+        count = gain_ref.shape[0]
+        mine = v_ref[:, :count]
+        for k in range(1, v_ref.shape[1] // count):
+            mine = jnp.where(line == k, v_ref[:, k * count : (k + 1) * count], mine)
+        gain_ref[...] = mine[0]
+        beta_ref[...] = mine[1]
+        both_ref[...] = mine[2]
+        same_ref[...] = mine[2]
+        lines = b1_ref.shape[0] // b_ref.shape[1]
+        bq_ref[...] = b_ref[lines : lines + 3, :]
+        for k in range(lines):
+            b1_ref[pl.ds(k * b_ref.shape[1], b_ref.shape[1])] = b_ref[k]
+
+
+def finish(tensor, sent_fc2, sent_dense, sent_fc1, sent_qkv, out, hidden_grad, vec_sums, all_sums):
     part, units = sent_fc2.shape
     local = sent_dense.shape[1]
     rows, width = out.shape
     steps = 4
+    quarter = vec_sums.shape[1] // tensor
+    fixed = VMEM
 
     def down(n, m):
         return pl.BlockSpec((n // steps, m), lambda i: (i, 0))
@@ -1348,19 +1414,22 @@
             jax.ShapeDtypeStruct((3, part, local), f32),
             jax.ShapeDtypeStruct((rows, width), bf16),
             jax.ShapeDtypeStruct((rows, width), bf16),
+            *[jax.ShapeDtypeStruct((quarter,), f32)] * 4,
+            jax.ShapeDtypeStruct((3, local), f32),
+            jax.ShapeDtypeStruct((units,), f32),
         ),
         in_specs=[
             across(part, units), across(part, local), down(part, units), down(part, 3 * local),
-            down(rows, width), down(rows, width),
+            down(rows, width), down(rows, width), fixed, fixed,
         ],
         out_specs=(
             down(units, part), down(local, part), down(part, units),
             pl.BlockSpec((3, part // steps, local), lambda i: (0, i, 0)),
-            down(rows, width), down(rows, width),
+            down(rows, width), down(rows, width), *[fixed] * 6,
         ),
         compiler_params=pltpu.CompilerParams(vmem_limit_bytes=VMEM_LIMIT),
         name="finish",
-    )(sent_fc2, sent_dense, sent_fc1, sent_qkv, out, hidden_grad)
+    )(sent_fc2, sent_dense, sent_fc1, sent_qkv, out, hidden_grad, vec_sums, all_sums)
 
 
 def rotary_tables(segments):
@@ -1393,40 +1462,39 @@
 ):
     seqs = segments.shape[0]
     local = qkv_weight.shape[2]
+    mine = (
+        hidden_in, cotangent, qkv_weight.transpose(1, 0, 2), dense_weight, fc1_weight, fc2_weight,
+    )
+    if fast:
+        (out, hidden_grad, sent_fc2, sent_dense, sent_fc1, sent_qkv, *_, vec_sums, all_sums) = block_call(
+            dp, tensor, (*mine, ln_gain, ln_bias, dense_bias, fc2_bias, qkv_bias, fc1_bias, segments))
+        (
+            grad_w2, grad_wd, grad_w1, grad_wq, out, hidden_grad,
+            gain_grad, beta_grad, bias_grad, same_grad, qkv_grad, fc1_grad,
+        ) = finish(
+            tensor, sent_fc2, sent_dense, sent_fc1, sent_qkv, out, hidden_grad, vec_sums, all_sums)
+        return (
+            out,
+            hidden_grad,
+            gain_grad,
+            beta_grad,
+            grad_wq.transpose(1, 0, 2),
+            qkv_grad,
+            grad_wd,
+            bias_grad,
+            grad_w1,
+            fc1_grad,
+            grad_w2,
+            same_grad,
+        )
+
     number = lax.broadcasted_iota(jnp.int32, (8, ln_gain.shape[0]), 0)
     vectors = jnp.where(number == 1, ln_bias.astype(f32)[None], ln_gain.astype(f32)[None])
     vectors = jnp.where(
         number == 2, dense_bias.astype(f32)[None] + fc2_bias.astype(f32)[None], vectors)
-    mine = (
-        hidden_in, cotangent, qkv_weight.transpose(1, 0, 2),
-        dense_weight, fc1_weight, fc2_weight, vectors,
-    )
-    if fast:
-        (out, hidden_grad, sent_fc2, sent_dense, sent_fc1, sent_qkv, *_, vec_sums, all_sums) = block_call(
-            dp, tensor, (*mine, qkv_bias, fc1_bias[None], segments))
-        quarter = vec_sums.shape[1] // tensor
-        at = lax.axis_index("tensor") * quarter
-        small = lax.dynamic_slice(vec_sums, (0, at), (3, quarter))
-        grad_w2, grad_wd, grad_w1, grad_wq, out, hidden_grad = finish(
-            sent_fc2, sent_dense, sent_fc1, sent_qkv, out, hidden_grad)
-        return (
-            out,
-            hidden_grad,
-            small[0],
-            small[1],
-            grad_wq.transpose(1, 0, 2),
-            all_sums[4:7],
-            grad_wd,
-            small[2],
-            grad_w1,
-            all_sums[:4].reshape(-1),
-            grad_w2,
-            small[2],
-        )
-
     tables = rotary_tables(segments)
     bias = jnp.pad(qkv_bias.astype(f32), ((0, 5), (0, 0)))
-    w_qkv, w_dense, w_fc1, w_fc2, normed, grad_out, vec = gather_plain(*mine)
+    w_qkv, w_dense, w_fc1, w_fc2, normed, grad_out, vec = gather_plain(*mine, vectors)
     gain, out_bias = vec[0:1], vec[2:3]
     query, key, value, attn_vec, probs = attend(
         *(matmul(normed, w_qkv[i]) for i in range(3)), bias, tables, segments, seqs

time: 296 us -> 282 us (0.953)
  Pallas kernels: 287 us -> 280 us
  local copies, waits for them, and re-layouts: 4.28 us -> 0 us
    pallas_call x1, Pallas kernels: 281 us -> 273 us  [block_call(): pl.pallas_call(kernel, out_shape=(shape(rows, width), shape(rows, width),...]
where the time goes in v6:
time: 282 us; the launch traced here: 281 us
  Pallas kernels  280 us (99%)
    pallas_call x1, Pallas kernels, block_call(): pl.pallas_call(kernel, out_shape=(shape(rows, width), shape(rows, width),...  273 us
    pallas_call x1, Pallas kernels, finish(): pl.pallas_call(finish_kernel, grid=(steps,), out_shape=(jax.ShapeDtypeStr...  6.6 us

profile of v6, /device:TPU:0, one launch (start us, length us, event | category | flops | bytes accessed | tf_op | source)
XLA Modules:
  0.0 280.6 jit_solution(16387349108567172533)
XLA Ops:
  0.6 273.2 %block.1 = (bf16[256,2048]{1,0:T(8,128)(2,1)}, bf16[256,2048]{1,0:T(8,128)(2,1)}, bf16[256,2048]{1,0:T(8,128)(2,1)}, bf16[256,512]{1,0:T(8,128)(2,1)}, bf16[256,...) custom-call(bf16[256,2048]{1,0:T(8,128)(2,1)} %x_ref.1, ...), custom_call_target="tpu_custom_call" | custom-call | tf_op jit(solution)/shard_map/block/pallas_call | solution.py:1300
  273.8 6.6 %finish.1 = (f32[2048,256]{1,0:T(8,128)}, f32[512,256]{1,0:T(8,128)}, f32[256,2048]{1,0:T(8,128)}, f32[3,256,512]{2,1,0:T(8,128)}, bf16[256,2048]{1,0:T(8,128)(2...) custom-call(bf16[256,2048]{1,0:T(8,128)(2,1)} %get-tuple-element.32., ...), custom_call_target="tpu_custom_call" | custom-call | tf_op jit(solution)/shard_map/finish/pallas_call | solution.py:1407

commit v7 on v6

--- a/solution.py
+++ b/solution.py
@@ -1251,12 +1251,6 @@
         sum_1.final()
         store_1 = copy_of(wb.at[pl.ds(0, part), :], s1_out)
         store_1.start()
-        for copy in line_tells:
-            copy.wait_recv()
-        total_z = tell_z[0]
-        for k in range(1, tensor):
-            total_z = total_z + tell_z[k]
-        vout_ref[...] = total_z
         ins.settle()
         ins.arrive()
 
@@ -1276,6 +1270,12 @@
 
         store_h = copy_of(x_buf, hid_ref)
         store_h.start()
+        for copy in line_tells:
+            copy.wait_recv()
+        total_z = tell_z[0]
+        for k in range(1, tensor):
+            total_z = total_z + tell_z[k]
+        vout_ref[...] = total_z
         for copy in vec + [cross_p] + bias_tells + vec_tells + line_tells:
             copy.wait_send()
         for plan in (qkv, fc1, fc2, sum_2, sum_d, sum_1, sum_q):

time: 282 us -> 281 us (level)
  no operation moved by 1% of the time
where the time goes in v7:
time: 281 us; the launch traced here: 279 us
  Pallas kernels  279 us (99%)
    pallas_call x1, Pallas kernels, block_call(): pl.pallas_call(kernel, out_shape=(shape(rows, width), shape(rows, width),...  272 us
    pallas_call x1, Pallas kernels, finish(): pl.pallas_call(finish_kernel, grid=(steps,), out_shape=(jax.ShapeDtypeStr...  6.6 us

profile of v7, /device:TPU:0, one launch (start us, length us, event | category | flops | bytes accessed | tf_op | source)
XLA Modules:
  0.0 279.4 jit_solution(3824636288689187808)
XLA Ops:
  0.6 271.9 %block.1 = (bf16[256,2048]{1,0:T(8,128)(2,1)}, bf16[256,2048]{1,0:T(8,128)(2,1)}, bf16[256,2048]{1,0:T(8,128)(2,1)}, bf16[256,512]{1,0:T(8,128)(2,1)}, bf16[256,...) custom-call(bf16[256,2048]{1,0:T(8,128)(2,1)} %x_ref.1, ...), custom_call_target="tpu_custom_call" | custom-call | tf_op jit(solution)/shard_map/block/pallas_call | solution.py:1300
  272.6 6.6 %finish.1 = (f32[2048,256]{1,0:T(8,128)}, f32[512,256]{1,0:T(8,128)}, f32[256,2048]{1,0:T(8,128)}, f32[3,256,512]{2,1,0:T(8,128)}, bf16[256,2048]{1,0:T(8,128)(2...) custom-call(bf16[256,2048]{1,0:T(8,128)(2,1)} %get-tuple-element.32., ...), custom_call_target="tpu_custom_call" | custom-call | tf_op jit(solution)/shard_map/finish/pallas_call | solution.py:1407

commit v8 on v7

--- a/solution.py
+++ b/solution.py
@@ -101,8 +101,8 @@
             for h in range(len(self.plans)):
                 self.copy(h, j, 0).start()
 
-    def advance(self, j):
-        for i in range(len(self.plans[0][j][1])):
+    def advance(self, j, some=slice(None)):
+        for i in range(len(self.plans[0][j][1]))[some]:
             for h, stages in enumerate(self.plans):
                 self.copy(h, j, i).wait_recv()
                 slot = stages[j][2][i]
@@ -922,11 +922,13 @@
 
             @pl.when(h == 2)
             def _():
-                for j in range(1, stages - 1):
-                    fc2.advance(j)
+                fc2.advance(1, slice(0, 1))
 
         cross_t = to_twin(chips + 1, attn, xbuf.at[:, pl.ds(chips * part, local)])
         cross_t.start()
+        fc2.advance(1, slice(1, None))
+        for j in range(2, stages - 1):
+            fc2.advance(j)
         dense.advance(stages - 1)
         fc2.advance(stages - 1)
         takes[1].wait()

time: 281 us -> 282 us (level)
  no operation moved by 1% of the time
where the time goes in v8:
time: 282 us; the launch traced here: 281 us
  Pallas kernels  280 us (99%)
    pallas_call x1, Pallas kernels, block_call(): pl.pallas_call(kernel, out_shape=(shape(rows, width), shape(rows, width),...  273 us
    pallas_call x1, Pallas kernels, finish(): pl.pallas_call(finish_kernel, grid=(steps,), out_shape=(jax.ShapeDtypeStr...  6.6 us

profile of v8, /device:TPU:0, one launch (start us, length us, event | category | flops | bytes accessed | tf_op | source)
XLA Modules:
  0.0 280.7 jit_solution(16965757622187327552)
XLA Ops:
  0.6 273.2 %block.1 = (bf16[256,2048]{1,0:T(8,128)(2,1)}, bf16[256,2048]{1,0:T(8,128)(2,1)}, bf16[256,2048]{1,0:T(8,128)(2,1)}, bf16[256,512]{1,0:T(8,128)(2,1)}, bf16[256,...) custom-call(bf16[256,2048]{1,0:T(8,128)(2,1)} %x_ref.1, ...), custom_call_target="tpu_custom_call" | custom-call | tf_op jit(solution)/shard_map/block/pallas_call | solution.py:1302
  273.9 6.6 %finish.1 = (f32[2048,256]{1,0:T(8,128)}, f32[512,256]{1,0:T(8,128)}, f32[256,2048]{1,0:T(8,128)}, f32[3,256,512]{2,1,0:T(8,128)}, bf16[256,2048]{1,0:T(8,128)(2...) custom-call(bf16[256,2048]{1,0:T(8,128)(2,1)} %get-tuple-element.32., ...), custom_call_target="tpu_custom_call" | custom-call | tf_op jit(solution)/shard_map/finish/pallas_call | solution.py:1409
